TPU v7x, 32 devices: a whole 2x2x4 slice. The times are simulated.
32 devices in a mesh: row: 4 (over y, x), col: 8 (over z, core).
Axes of the slice: x: 2, y: 2, z: 4, core: 2. Of those that a mesh axis runs over, the one named last changes fastest.
Arguments:
- layer_input: bfloat16 [8192, 2048], P(('row', 'col')), may hold values from -6 to 6
- out_grad: bfloat16 [8192, 2048], P(('row', 'col')), may hold values from -6 to 6
- kv_grad: bfloat16 [8192, 256], P(('row', 'col')), may hold values from -6 to 6
- lengths: int32 [4, 4], P('row'), may hold values from 1 to 1024, 2048 in all within a row
- token_deal: int32 [4, 2048], P('row'), may hold values from 0 to 2047, each once within a row
- attn_gain: float32 [2048], P('row'), may hold values from 0.25 to 1.75
- query_weight: float32 [2048, 2048], P('row', 'col'), may hold values from -0.125 to 0.125
- key_weight: float32 [2048, 128], P('row'), may hold values from -0.125 to 0.125
- value_weight: float32 [2048, 128], P('row'), may hold values from -0.125 to 0.125
- out_weight: float32 [2048, 2048], P('col', 'row'), may hold values from -1 to 1
- mlp_gain: float32 [2048], P('row'), may hold values from 0.25 to 1.75
- gate_weight: float32 [2048, 5632], P('row', 'col'), may hold values from -0.125 to 0.125
- up_weight: float32 [2048, 5632], P('row', 'col'), may hold values from -0.125 to 0.125
- down_weight: float32 [5632, 2048], P('col', 'row'), may hold values from -0.3125 to 0.3125
Outputs:
- layer_output: bfloat16 [8192, 2048], P(('row', 'col'))
- input_grad: float32 [8192, 2048], P(('row', 'col'))
- shared_kv: bfloat16 [8192, 256], P(('row', 'col'))
- attn_gain_grad: float32 [2048], P('row')
- query_weight_grad: float32 [2048, 2048], P('row', 'col')
- key_weight_grad: float32 [2048, 128], P('row')
- value_weight_grad: float32 [2048, 128], P('row')
- out_weight_grad: float32 [2048, 2048], P('col', 'row')
- mlp_gain_grad: float32 [2048], P('row')
- gate_weight_grad: float32 [2048, 5632], P('row', 'col')
- up_weight_grad: float32 [2048, 5632], P('row', 'col')
- down_weight_grad: float32 [5632, 2048], P('col', 'row')
Inputs may be any that keep to these rules, and one draw needn't show every extreme that they name: Each row holds 4 lengths that sum to 2048; the longest of each row is exactly 1024. `token_deal`: each row is a permutation of 0 to 2047.
All inputs are finite; a program needn't handle non-finite values.
Results may differ from a plain program's by a relative error of at most 0.017.
The roundings to bfloat16 on the way count: a program that leaves them out, or rounds other values in their place, can miss the bound.
Values may be sent and summed in bfloat16 or wider, within the bound.
No kernel may reach another device: no remote copies, remote signals or barrier semaphores. Data moves between devices by JAX's collectives and lax.ppermute only.
A program may use at most 320 MiB of HBM per device.

v0:
```python
import jax
import jax.numpy as jnp
from jax import lax
from jax.sharding import PartitionSpec as P

norm_eps = 1e-05
rope_base = 10000.0
masked_score = -1e30


def rotate_pairs(values, positions, direction):
    half_dim = values.shape[-1] // 2
    frequency = rope_base ** (-jnp.arange(half_dim, dtype=jnp.float32) / half_dim)
    angles = positions.astype(jnp.float32)[:, None, None] * frequency
    cosine = jnp.cos(angles)
    sine_part = jnp.sin(angles) * direction
    first_half = values[..., :half_dim]
    second = values[..., half_dim:]
    return jnp.concatenate(
        [first_half * cosine - second * sine_part, second * cosine + first_half * sine_part],
        axis=-1,
    )


def norm_parts(values, gain):
    factor = lax.rsqrt(jnp.mean(values * values, axis=-1, keepdims=True) + norm_eps)
    return (factor, values * factor * gain)


def norm_backward(values, factor, gain, grad_rows):
    weighted = grad_rows * gain
    inner_mean = jnp.mean(weighted * values, axis=-1, keepdims=True)
    input_part = factor * weighted - values * factor * factor * factor * inner_mean
    gain_part = jnp.sum(grad_rows * values * factor, axis=0)
    return (input_part, gain_part)


def sequence_info(seq_lengths, group_rows):
    positions = jnp.arange(group_rows, dtype=jnp.int32)
    seq_ends = jnp.cumsum(seq_lengths)
    seq_ids = jnp.sum((positions[:, None] >= seq_ends[None, :]).astype(jnp.int32), axis=1)
    starts = jnp.sum(
        jnp.where(seq_ends[None, :] <= positions[:, None], seq_lengths[None, :], 0), axis=1
    )
    return (positions, seq_ids, positions - starts)


def block_scores(query_block, key_rows, seq_ids, first_row, block_rows, score_scale):
    key_index = jnp.arange(key_rows.shape[0], dtype=jnp.int32)
    row_index = first_row + jnp.arange(block_rows, dtype=jnp.int32)
    row_seq = lax.dynamic_slice_in_dim(seq_ids, first_row, block_rows, 0)
    scores = (
        jnp.einsum("qhd,kd->hqk", query_block, key_rows, preferred_element_type=jnp.float32)
        * score_scale
    )
    allowed = (row_seq[:, None] == seq_ids[None, :]) & (key_index[None, :] <= row_index[:, None])
    return jnp.where(allowed[None], scores, masked_score)


def attend_forward(queries, key_rows, value_rows, seq_ids):
    group_rows, head_count, head_dim = queries.shape
    block_rows = min(512, group_rows)
    score_scale = float(head_dim) ** (-0.5)
    count_blocks = group_rows // block_rows
    query_blocks = queries.reshape(count_blocks, block_rows, head_count, head_dim)
    first_rows = jnp.arange(count_blocks, dtype=jnp.int32) * block_rows

    def one_block(pieces):
        query_block, first_row = pieces
        scores = block_scores(query_block, key_rows, seq_ids, first_row, block_rows, score_scale)
        highest = jnp.max(scores, axis=-1, keepdims=True)
        exponent = jnp.exp(scores - highest)
        row_total = jnp.sum(exponent, axis=-1, keepdims=True)
        prob_low = (exponent / row_total).astype(jnp.bfloat16)
        mixed_rows = jnp.einsum(
            "hqk,kd->qhd", prob_low, value_rows, preferred_element_type=jnp.float32
        )
        return (mixed_rows.astype(jnp.bfloat16), (highest + jnp.log(row_total))[..., 0])

    mixed_rows, log_norm = lax.map(one_block, (query_blocks, first_rows))
    return (mixed_rows.reshape(group_rows, head_count, head_dim), log_norm)


def attend_backward(queries, key_rows, value_rows, seq_ids, mixed_grad, log_norm):
    group_rows, head_count, head_dim = queries.shape
    block_rows = min(512, group_rows)
    score_scale = float(head_dim) ** (-0.5)
    count_blocks = group_rows // block_rows
    query_blocks = queries.reshape(count_blocks, block_rows, head_count, head_dim)
    grad_blocks = mixed_grad.reshape(count_blocks, block_rows, head_count, head_dim)
    first_rows = jnp.arange(count_blocks, dtype=jnp.int32) * block_rows

    def one_block(carry, pieces):
        key_grad, value_grad = carry
        query_block, grad_block, norm_block, first_row = pieces
        scores = block_scores(query_block, key_rows, seq_ids, first_row, block_rows, score_scale)
        softmax_rows = jnp.exp(scores - norm_block[..., None])
        prob_low = softmax_rows.astype(jnp.bfloat16)
        prob_grad = jnp.einsum(
            "qhd,kd->hqk", grad_block, value_rows, preferred_element_type=jnp.float32
        )
        row_dot = jnp.sum(softmax_rows * prob_grad, axis=-1, keepdims=True)
        score_grad = (softmax_rows * (prob_grad - row_dot)).astype(jnp.bfloat16)
        query_grad = (
            jnp.einsum("hqk,kd->qhd", score_grad, key_rows, preferred_element_type=jnp.float32)
            * score_scale
        )
        key_grad = (
            key_grad
            + jnp.einsum("hqk,qhd->kd", score_grad, query_block, preferred_element_type=jnp.float32)
            * score_scale
        )
        value_grad = value_grad + jnp.einsum(
            "hqk,qhd->kd", prob_low, grad_block, preferred_element_type=jnp.float32
        )
        return ((key_grad, value_grad), query_grad)

    zero_rows = jnp.zeros((group_rows, head_dim), jnp.float32)
    (key_grad, value_grad), query_grad = lax.scan(
        one_block, (zero_rows, zero_rows), (query_blocks, grad_blocks, log_norm, first_rows)
    )
    return (query_grad.reshape(group_rows, head_count, head_dim), key_grad, value_grad)


def local(
    layer_input,
    out_grad,
    kv_grad,
    lengths,
    token_deal,
    attn_gain,
    query_weight,
    key_weight,
    value_weight,
    out_weight,
    mlp_gain,
    gate_weight,
    up_weight,
    down_weight,
):
    own_rows = layer_input.shape[0]
    col_index = lax.axis_index("col")
    group_rows = own_rows * lax.axis_size("col")
    head_dim = key_weight.shape[1]
    (
        gain_one,
        query_copy,
        key_copy,
        value_copy,
        out_copy,
        gain_two,
        gate_copy,
        up_copy,
        down_copy,
    ) = (
        lax.all_gather(attn_gain.astype(jnp.bfloat16), "row", axis=0, tiled=True),
        lax.all_gather(query_weight.astype(jnp.bfloat16), "row", axis=0, tiled=True),
        lax.all_gather(key_weight.astype(jnp.bfloat16), "row", axis=0, tiled=True),
        lax.all_gather(value_weight.astype(jnp.bfloat16), "row", axis=0, tiled=True),
        lax.all_gather(out_weight.astype(jnp.bfloat16), "row", axis=1, tiled=True),
        lax.all_gather(mlp_gain.astype(jnp.bfloat16), "row", axis=0, tiled=True),
        lax.all_gather(gate_weight.astype(jnp.bfloat16), "row", axis=0, tiled=True),
        lax.all_gather(up_weight.astype(jnp.bfloat16), "row", axis=0, tiled=True),
        lax.all_gather(down_weight.astype(jnp.bfloat16), "row", axis=1, tiled=True),
    )
    gain_one = gain_one.astype(jnp.float32)
    gain_two = gain_two.astype(jnp.float32)
    head_count = query_copy.shape[1] // head_dim
    positions, seq_ids, within = sequence_info(lengths[0], group_rows)
    slot_order = token_deal[0]
    inverse = jnp.zeros((group_rows,), jnp.int32).at[slot_order].set(positions)
    slot_pos = within[slot_order]
    own_pos = lax.dynamic_slice_in_dim(slot_pos, col_index * own_rows, own_rows, 0)
    input_rows = layer_input.astype(jnp.float32)
    factor_one, normed_one = norm_parts(input_rows, gain_one)
    normed_own = normed_one.astype(jnp.bfloat16)
    normed_rows, grad_rows = (
        lax.all_gather(normed_own, "col", axis=0, tiled=True),
        lax.all_gather(out_grad, "col", axis=0, tiled=True),
    )
    queries = jnp.dot(normed_rows, query_copy, preferred_element_type=jnp.float32).reshape(
        group_rows, head_count, head_dim
    )
    queries = rotate_pairs(queries, slot_pos, 1.0).astype(jnp.bfloat16)
    key_proj = jnp.dot(normed_rows, key_copy, preferred_element_type=jnp.float32)
    key_rows = rotate_pairs(key_proj[:, None, :], slot_pos, 1.0)[:, 0, :].astype(jnp.bfloat16)
    value_rows = jnp.dot(normed_rows, value_copy, preferred_element_type=jnp.float32).astype(
        jnp.bfloat16
    )
    shared_rows = jnp.concatenate([key_rows, value_rows], axis=1)
    shared_own = lax.dynamic_slice_in_dim(shared_rows, col_index * own_rows, own_rows, 0)
    query_orig = queries[inverse]
    key_orig = key_rows[inverse]
    value_orig = value_rows[inverse]
    mixed_orig, log_norm = attend_forward(query_orig, key_orig, value_orig, seq_ids)
    mixed_slot = mixed_orig[slot_order].reshape(group_rows, head_count * head_dim)
    out_full = lax.all_gather(out_copy, "col", axis=0, tiled=True)
    mixed_own = lax.all_to_all(mixed_slot, "col", split_axis=0, concat_axis=1, tiled=True)
    attended = jnp.dot(mixed_own, out_full, preferred_element_type=jnp.float32)
    middle = input_rows + attended
    factor_two, normed_two = norm_parts(middle, gain_two)
    mlp_rows = lax.all_gather(normed_two.astype(jnp.bfloat16), "col", axis=0, tiled=True)
    gate_act = jnp.dot(mlp_rows, gate_copy, preferred_element_type=jnp.float32)
    upward = jnp.dot(mlp_rows, up_copy, preferred_element_type=jnp.float32)
    sigmoid_gate = jax.nn.sigmoid(gate_act)
    silu_gate = gate_act * sigmoid_gate
    hidden = (silu_gate * upward).astype(jnp.bfloat16)
    output_rows = middle + lax.psum_scatter(
        jnp.dot(hidden, down_copy, preferred_element_type=jnp.float32),
        "col",
        scatter_dimension=0,
        tiled=True,
    )
    hidden_grad = jnp.dot(grad_rows, down_copy.T, preferred_element_type=jnp.float32)
    down_wgrad = jnp.dot(hidden.T, grad_rows, preferred_element_type=jnp.float32)
    gate_grad = (
        hidden_grad * upward * sigmoid_gate * (1.0 + gate_act * (1.0 - sigmoid_gate))
    ).astype(jnp.bfloat16)
    up_grad = (hidden_grad * silu_gate).astype(jnp.bfloat16)
    gate_wgrad = jnp.dot(mlp_rows.T, gate_grad, preferred_element_type=jnp.float32)
    up_wgrad = jnp.dot(mlp_rows.T, up_grad, preferred_element_type=jnp.float32)
    normed_two_grad = lax.psum_scatter(
        jnp.dot(gate_grad, gate_copy.T, preferred_element_type=jnp.float32)
        + jnp.dot(up_grad, up_copy.T, preferred_element_type=jnp.float32),
        "col",
        scatter_dimension=0,
        tiled=True,
    )
    middle_part, gain_two_grad = norm_backward(middle, factor_two, gain_two, normed_two_grad)
    middle_grad = out_grad.astype(jnp.float32) + middle_part
    middle_low = middle_grad.astype(jnp.bfloat16)
    middle_rows = lax.all_gather(middle_low, "col", axis=0, tiled=True)
    mixed_grad_slot = jnp.dot(middle_rows, out_copy.T, preferred_element_type=jnp.float32).astype(
        jnp.bfloat16
    )
    out_wgrad = jnp.dot(mixed_slot.T, middle_rows, preferred_element_type=jnp.float32)
    mixed_grad = mixed_grad_slot.reshape(group_rows, head_count, head_dim)[inverse]
    query_grad, key_grad, value_grad = attend_backward(
        query_orig, key_orig, value_orig, seq_ids, mixed_grad, log_norm
    )
    query_grad = (
        rotate_pairs(query_grad[slot_order], slot_pos, -1.0)
        .astype(jnp.bfloat16)
        .reshape(group_rows, head_count * head_dim)
    )
    query_wgrad = jnp.dot(normed_rows.T, query_grad, preferred_element_type=jnp.float32)
    shared_part = jnp.concatenate([key_grad, value_grad], axis=1)[slot_order]
    shared_cols = shared_part.shape[1]
    grad_parts = jnp.concatenate(
        [jnp.dot(query_grad, query_copy.T, preferred_element_type=jnp.float32), shared_part], axis=1
    )
    summed_parts = lax.psum_scatter(grad_parts, "col", scatter_dimension=0, tiled=True)
    width_cols = summed_parts.shape[1] - shared_cols
    normed_one_grad = summed_parts[:, :width_cols]
    shared_grad = summed_parts[:, width_cols:]
    shared_grad = shared_grad + kv_grad.astype(jnp.float32)
    key_own = rotate_pairs(shared_grad[:, None, :head_dim], own_pos, -1.0)[:, 0, :].astype(
        jnp.bfloat16
    )
    value_own = shared_grad[:, head_dim:].astype(jnp.bfloat16)
    key_wgrad = jnp.dot(normed_own.T, key_own, preferred_element_type=jnp.float32)
    value_wgrad = jnp.dot(normed_own.T, value_own, preferred_element_type=jnp.float32)
    normed_one_grad = (
        normed_one_grad
        + jnp.dot(key_own, key_copy.T, preferred_element_type=jnp.float32)
        + jnp.dot(value_own, value_copy.T, preferred_element_type=jnp.float32)
    )
    input_part, gain_one_grad = norm_backward(input_rows, factor_one, gain_one, normed_one_grad)
    input_grad = middle_grad + input_part
    summed = (
        lax.psum_scatter(gain_one_grad, "row", scatter_dimension=0, tiled=True),
        lax.psum_scatter(query_wgrad, "row", scatter_dimension=0, tiled=True),
        lax.psum_scatter(key_wgrad, "row", scatter_dimension=0, tiled=True),
        lax.psum_scatter(value_wgrad, "row", scatter_dimension=0, tiled=True),
        lax.psum_scatter(out_wgrad, "row", scatter_dimension=1, tiled=True),
        lax.psum_scatter(gain_two_grad, "row", scatter_dimension=0, tiled=True),
        lax.psum_scatter(gate_wgrad, "row", scatter_dimension=0, tiled=True),
        lax.psum_scatter(up_wgrad, "row", scatter_dimension=0, tiled=True),
        lax.psum_scatter(down_wgrad, "row", scatter_dimension=1, tiled=True),
    )
    gain_one_sum, key_sum, value_sum, gain_two_sum = lax.psum(
        (summed[0], summed[2], summed[3], summed[5]), "col"
    )
    return (
        output_rows.astype(jnp.bfloat16),
        input_grad,
        shared_own,
        gain_one_sum,
        summed[1],
        key_sum,
        value_sum,
        summed[4],
        gain_two_sum,
        summed[6],
        summed[7],
        summed[8],
    )


def solution(mesh):
    in_specs = (
        P(("row", "col"), None),
        P(("row", "col"), None),
        P(("row", "col"), None),
        P("row", None),
        P("row", None),
        P("row"),
        P("row", "col"),
        P("row", None),
        P("row", None),
        P("col", "row"),
        P("row"),
        P("row", "col"),
        P("row", "col"),
        P("col", "row"),
    )
    out_specs = (
        P(("row", "col"), None),
        P(("row", "col"), None),
        P(("row", "col"), None),
        P("row"),
        P("row", "col"),
        P("row", None),
        P("row", None),
        P("col", "row"),
        P("row"),
        P("row", "col"),
        P("row", "col"),
        P("col", "row"),
    )
    return jax.shard_map(local, mesh=mesh, in_specs=in_specs, out_specs=out_specs, check_vma=False)
```

profile of v0, /device:TPU:0, one launch (start us, length us, event | category | flops | bytes accessed | tf_op | source)
XLA Modules:
  0.0 1775.3 jit_solution(17734194517630113278)
XLA Ops:
  24.0 15.5 all-gather.17.cloned.1.call-done
  49.1 11.8 gather_fusion
  86.8 37.4 %all-gather.13.cloned.1.call-done = bf16[2048,2048]{0,1:T(8,128)(2,1)} async-done(((bf16[256,2048]{0,1:T(8,128)(2,1)}), bf16[2048,2048]{0,1:T(8,128)(2,1)}) %all-gather.13.cloned.1.call-update) | async-done | bytes 8388624 | tf_op jit(solution)/shard_map/all_gather | solution.py:178
  173.8 13.9 gather_fusion.1
  189.1 50.6 %while.27 = (s32[]{:T(128)}, bf16[4,512,2,128]{3,1,0,2:T(8,128)(2,1)}, f32[4,2,512]{2,1,0:T(2,128)S(1)}, s32[4]{0:T(128)S(1)}, s32[2048]{0:T(1024)S(1)}, /*index...) while((s32[]{:T(128)}, ...), condition=%wide.region_8.9_spmd, body=%wide.region_5.8_spmd.sunk | while | flops 1102183936 | bytes 30984376 | solution.py:80
  243.8 15.1 gather_fusion.4
  276.7 18.2 %all-to-all-done = bf16[8,256,256]{1,2,0:T(8,128)(2,1)S(1)} async-done(((bf16[8,256,256]{1,2,0:T(8,128)(2,1)}), bf16[8,256,256]{1,2,0:T(8,128)(2,1)S(1)}, u32[]{:S(2)}, u32[]{:S(2)}) %all-to-all-start) | async-done | bytes 1048608 | tf_op jit(solution)/shard_map/all_to_all | solution.py:198
  310.4 74.8 %all-gather.21.cloned.1.call-done = bf16[2048,2048]{0,1:T(8,128)(2,1)} async-done(((bf16[256,2048]{0,1:T(8,128)(2,1)}), bf16[2048,2048]{0,1:T(8,128)(2,1)}) %all-gather.21.cloned.1.call-update) | async-done | bytes 8388624 | tf_op jit(solution)/shard_map/all_gather | solution.py:202
  396.3 31.1 %all-gather.25.cloned.1.call-done = bf16[2048,704]{0,1:T(8,128)(2,1)} async-done(((bf16[512,704]{0,1:T(8,128)(2,1)}), bf16[2048,704]{0,1:T(8,128)(2,1)}) %all-gather.25.cloned.1.call-update) | async-done | bytes 2883600 | tf_op jit(solution)/shard_map/all_gather | solution.py:163
  438.4 32.4 %all-gather.27.cloned.1.call-done = bf16[704,2048]{1,0:T(8,128)(2,1)} async-done(((bf16[704,512]{1,0:T(8,128)(2,1)}), bf16[704,2048]{1,0:T(8,128)(2,1)}) %all-gather.27.cloned.1.call-update) | async-done | bytes 2883600 | tf_op jit(solution)/shard_map/all_gather | solution.py:164
  470.8 83.7 %all-gather.29.cloned.1.call-done = bf16[2048,2048]{1,0:T(8,128)(2,1)} async-done(((bf16[256,2048]{1,0:T(8,128)(2,1)}), bf16[2048,2048]{1,0:T(8,128)(2,1)}) %all-gather.29.cloned.1.call-update) | async-done | bytes 8388624 | tf_op jit(solution)/shard_map/all_gather | solution.py:179
  554.5 15.3 multiply_convert_fusion
  580.2 14.1 convolution_add_fusion
  595.9 165.3 %reduce-scatter.13.cloned.1.call-done = f32[256,2048]{0,1:T(8,128)} async-done(((f32[2048,2048]{0,1:T(8,128)}), f32[256,2048]{0,1:T(8,128)}) %reduce-scatter.13.cloned.1.call-update) | async-done | bytes 2097168 | tf_op jit(solution)/shard_map/reduce_scatter | solution.py:222
  766.0 81.0 %all-gather.31.cloned.1.call-done = bf16[2048,2048]{0,1:T(8,128)(2,1)} async-done(((bf16[256,2048]{0,1:T(8,128)(2,1)}), bf16[2048,2048]{0,1:T(8,128)(2,1)}) %all-gather.31.cloned.1.call-update) | async-done | bytes 8388624 | tf_op jit(solution)/shard_map/all_gather | solution.py:232
  858.0 15.1 gather_fusion.5
  873.1 77.5 %while.28 = (s32[]{:T(128)}, f32[2048,128]{1,0:T(8,128)S(1)}, f32[2048,128]{1,0:T(8,128)}, f32[4,512,2,128]{3,1,0,2:T(8,128)}, s32[4]{0:T(128)S(1)}, /*index=5*/...) while((s32[]{:T(128)}, f32[2048,128]{1,0:T(8,128)S(1)}, ...), condition=%wide.region_15.16_spmd.clone, body=%wide.region_13.15_spmd.clone.sunk | while | flops 2720398848 | bytes 83409176 | solution.py:119
  955.3 14.5 gather_fusion.6
  1007.6 184.5 %reduce-scatter.15.cloned.1.call-done = f32[256,2304]{0,1:T(8,128)} async-done(((f32[2048,2304]{0,1:T(8,128)}), f32[256,2304]{0,1:T(8,128)}) %reduce-scatter.15.cloned.1.call-update) | async-done | bytes 2359312 | tf_op jit(solution)/shard_map/reduce_scatter | solution.py:252
  1196.4 12.9 fusion.93
  1209.4 11.2 fusion.98
  1220.7 11.2 fusion.96
  1232.0 11.1 fusion.97
  1267.9 154.7 %reduce-scatter.11.cloned.1.call-done = f32[256,2048]{0,1:T(8,128)} async-done(((f32[2048,2048]{0,1:T(8,128)}), f32[256,2048]{0,1:T(8,128)}) %reduce-scatter.11.cloned.1.call-update) | async-done | bytes 2097168 | tf_op jit(solution)/shard_map/reduce_scatter | solution.py:208
  1427.5 17.1 all-reduce.4
  1449.0 14.1 all-reduce.2
  1463.2 27.2 %reduce-scatter.29.cloned.1.call-done = f32[704,512]{1,0:T(8,128)} async-done(((f32[704,2048]{1,0:T(8,128)}), f32[704,512]{1,0:T(8,128)}) %reduce-scatter.29.cloned.1.call-update) | async-done | bytes 1441808 | tf_op jit(solution)/shard_map/reduce_scatter | solution.py:279
  1490.4 69.1 %reduce-scatter.25.cloned.1.call-done = f32[512,704]{0,1:T(8,128)} async-done(((f32[2048,704]{0,1:T(8,128)}), f32[512,704]{0,1:T(8,128)}) %reduce-scatter.25.cloned.1.call-update) | async-done | bytes 1441808 | tf_op jit(solution)/shard_map/reduce_scatter | solution.py:277
  1559.5 69.1 %reduce-scatter.27.cloned.1.call-done = f32[512,704]{0,1:T(8,128)} async-done(((f32[2048,704]{0,1:T(8,128)}), f32[512,704]{0,1:T(8,128)}) %reduce-scatter.27.cloned.1.call-update) | async-done | bytes 1441808 | tf_op jit(solution)/shard_map/reduce_scatter | solution.py:278
  1628.6 38.8 %reduce-scatter.17.cloned.1.call-done = f32[512,256]{1,0:T(8,128)} async-done(((f32[2048,256]{1,0:T(8,128)}), f32[512,256]{1,0:T(8,128)}) %reduce-scatter.17.cloned.1.call-update) | async-done | bytes 524304 | tf_op jit(solution)/shard_map/reduce_scatter | solution.py:272
  1667.4 38.6 %reduce-scatter.23.cloned.1.call-done = f32[256,512]{1,0:T(8,128)} async-done(((f32[256,2048]{1,0:T(8,128)}), f32[256,512]{1,0:T(8,128)}) %reduce-scatter.23.cloned.1.call-update) | async-done | bytes 524304 | tf_op jit(solution)/shard_map/reduce_scatter | solution.py:275
  1706.0 58.9 %all-reduce.7.cloned.1.call-done = (f32[512,128]{1,0:T(8,128)}, f32[512,128]{1,0:T(8,128)}) async-done(((f32[512,128]{1,0:T(8,128)}, f32[512,128]{1,0:T(8,128)}), (f32[512,128]{1,0:T(8,128)}, f32[512,128]{1,0:T(8,128)})) %all-reduce.7.cloned.1.call-update) | async-done | bytes 524304 | tf_op jit(solution)/shard_map/psum | solution.py:281
  (361 shorter events, 385.4 us)
Async XLA Ops:
  7.2 32.3 %all-gather.17.cloned.1.call-start = ((), (), s32[]{:S(2)}) async-start(), calls=%async_computation.13 | async-start | bytes 1310720 | tf_op jit(solution)/shard_map/all_gather | solution.py:160
  9.0 115.2 %all-gather.13.cloned.1.call-start = ((), (), s32[]{:S(2)}) async-start(), calls=%async_computation.11 | async-start | bytes 9437184 | tf_op jit(solution)/shard_map/all_gather | solution.py:178
  20.9 275.0 %copy-start.2 = (bf16[256,2048]{0,1:T(8,128)(2,1)}, bf16[256,2048]{0,1:T(8,128)(2,1)S(1)}, u32[]{:S(2)}) copy-start(bf16[256,2048]{0,1:T(8,128)(2,1)S(1)} %copy.114) | copy-start | bytes 3145732
  23.2 128.1 %all-gather.15.cloned.1.call-start = ((), (), s32[]{:S(2)}) async-start(), calls=%async_computation.12 | async-start | bytes 1310720 | tf_op jit(solution)/shard_map/all_gather | solution.py:157
  24.0 252.7 %all-gather.19.cloned.1.call-start = ((), (), s32[]{:S(2)}) async-start(), calls=%async_computation.14 | async-start | bytes 9437184 | tf_op jit(solution)/shard_map/all_gather | solution.py:197
  39.5 270.9 %all-gather.23.cloned.1.call-start = ((), (), s32[]{:S(2)}) async-start(), calls=%async_computation.16 | async-start | bytes 3604480 | tf_op jit(solution)/shard_map/all_gather | solution.py:162
  49.1 194.7 %copy-start.38 = (s32[2048]{0:T(1024)}, s32[2048]{0:T(1024)S(1)}, u32[]{:S(2)}) copy-start(s32[2048]{0:T(1024)S(1)} %get-tuple-element.398) | copy-start | bytes 24580
  263.7 31.2 %all-to-all-start = ((bf16[8,256,256]{1,2,0:T(8,128)(2,1)}), bf16[8,256,256]{1,2,0:T(8,128)(2,1)S(1)}, u32[]{:S(2)}, u32[]{:S(2)}) async-start(bf16[8,256,256]{1,2,0:T(8,128)(2,1)} %copy.124), calls=%async_computation | async-start | bytes 2097152 | tf_op jit(solution)/shard_map/all_to_all | solution.py:198
  268.4 116.9 %all-gather.21.cloned.1.call-start = ((), (), s32[]{:S(2)}) async-start(), calls=%async_computation.15 | async-start | bytes 9437184 | tf_op jit(solution)/shard_map/all_gather | solution.py:202
  276.6 487.5 %copy-start.34 = (f32[4,1,512]{2,1,0:T(1,128)}, f32[4,1,512]{2,1,0:T(1,128)S(1)}, u32[]{:S(2)}) copy-start(f32[4,1,512]{2,1,0:T(1,128)S(1)} %convert_element_type.144) | copy-start | bytes 24580
  303.0 461.2 %copy-start = (f32[256,2048]{0,1:T(8,128)}, f32[256,2048]{0,1:T(8,128)S(1)}, u32[]{:S(2)}) copy-start(f32[256,2048]{0,1:T(8,128)S(1)} %get-tuple-element.395) | copy-start | bytes 6291460
  303.0 461.1 %copy-start.45 = (f32[256]{0:T(256)}, f32[256]{0:T(256)S(1)}, u32[]{:S(2)}) copy-start(f32[256]{0:T(256)S(1)} %add_rsqrt_fusion) | copy-start | bytes 3076
  304.6 122.8 %all-gather.25.cloned.1.call-start = ((), (), s32[]{:S(2)}) async-start(), calls=%async_computation.17 | async-start | bytes 3604480 | tf_op jit(solution)/shard_map/all_gather | solution.py:163
  307.0 163.8 %all-gather.27.cloned.1.call-start = ((), (), s32[]{:S(2)}) async-start(), calls=%async_computation.18 | async-start | bytes 3604480 | tf_op jit(solution)/shard_map/all_gather | solution.py:164
  309.6 244.8 %all-gather.29.cloned.1.call-start = ((), (), s32[]{:S(2)}) async-start(), calls=%async_computation.20 | async-start | bytes 9437184 | tf_op jit(solution)/shard_map/all_gather | solution.py:179
  310.4 450.7 %reduce-scatter.13.cloned.1.call-start = ((), (), s32[]{:S(2)}) async-start(), calls=%async_computation.21 | async-start | bytes 18874368 | tf_op jit(solution)/shard_map/reduce_scatter | solution.py:222
  594.3 252.7 %all-gather.31.cloned.1.call-start = ((), (), s32[]{:S(2)}) async-start(), calls=%async_computation.22 | async-start | bytes 9437184 | tf_op jit(solution)/shard_map/all_gather | solution.py:232
  595.8 170.0 %copy-start.14 = (bf16[256,2048]{0,1:T(8,128)(2,1)}, bf16[256,2048]{0,1:T(8,128)(2,1)S(1)}, u32[]{:S(2)}) copy-start(bf16[256,2048]{0,1:T(8,128)(2,1)S(1)} %copy.127) | copy-start | bytes 3145732
  765.9 426.2 %reduce-scatter.15.cloned.1.call-start = ((), (), s32[]{:S(2)}) async-start(), calls=%async_computation.23 | async-start | bytes 21233664 | tf_op jit(solution)/shard_map/reduce_scatter | solution.py:252
  1005.9 187.2 %copy-start.53 = (f32[64]{0:T(128)S(1)}, f32[64]{0:T(128)}, u32[]{:S(2)}) copy-start(f32[64]{0:T(128)} %copy-done.52) | copy-start | bytes 772
  1005.9 187.6 %copy-start.10 = (bf16[256,2048]{0,1:T(8,128)(2,1)S(1)}, bf16[256,2048]{0,1:T(8,128)(2,1)}, u32[]{:S(2)}) copy-start(bf16[256,2048]{0,1:T(8,128)(2,1)} %fusion.50) | copy-start | bytes 3145732
  1005.9 261.9 %reduce-scatter.19.cloned.1.call-start = ((), (), s32[]{:S(2)}) async-start(), calls=%async_computation.25 | async-start | bytes 1310720 | tf_op jit(solution)/shard_map/reduce_scatter | solution.py:273
  1194.9 73.0 %reduce-scatter.21.cloned.1.call-start = ((), (), s32[]{:S(2)}) async-start(), calls=%async_computation.26 | async-start | bytes 1310720 | tf_op jit(solution)/shard_map/reduce_scatter | solution.py:274
  1196.4 226.1 %reduce-scatter.11.cloned.1.call-start = ((), (), s32[]{:S(2)}) async-start(), calls=%async_computation.19 | async-start | bytes 18874368 | tf_op jit(solution)/shard_map/reduce_scatter | solution.py:208
  1209.4 281.0 %reduce-scatter.29.cloned.1.call-start = ((), (), s32[]{:S(2)}) async-start(), calls=%async_computation.30 | async-start | bytes 7208960 | tf_op jit(solution)/shard_map/reduce_scatter | solution.py:279
  1220.6 338.9 %reduce-scatter.25.cloned.1.call-start = ((), (), s32[]{:S(2)}) async-start(), calls=%async_computation.28 | async-start | bytes 7208960 | tf_op jit(solution)/shard_map/reduce_scatter | solution.py:277
  1231.9 396.7 %reduce-scatter.27.cloned.1.call-start = ((), (), s32[]{:S(2)}) async-start(), calls=%async_computation.29 | async-start | bytes 7208960 | tf_op jit(solution)/shard_map/reduce_scatter | solution.py:278
  1243.1 424.3 %reduce-scatter.17.cloned.1.call-start = ((), (), s32[]{:S(2)}) async-start(), calls=%async_computation.24 | async-start | bytes 2621440 | tf_op jit(solution)/shard_map/reduce_scatter | solution.py:272
  1250.7 455.3 %reduce-scatter.23.cloned.1.call-start = ((), (), s32[]{:S(2)}) async-start(), calls=%async_computation.27 | async-start | bytes 2621440 | tf_op jit(solution)/shard_map/reduce_scatter | solution.py:275
  1260.3 504.6 %all-reduce.7.cloned.1.call-start = ((), (), s32[]{:S(2)}) async-start(), calls=%async_computation.31 | async-start | bytes 1048576 | tf_op jit(solution)/shard_map/psum | solution.py:281
  1264.5 158.0 %copy-start.1 = (f32[256,2048]{0,1:T(8,128)S(1)}, f32[256,2048]{0,1:T(8,128)}, u32[]{:S(2)}) copy-start(f32[256,2048]{0,1:T(8,128)} %copy-done) | copy-start | bytes 6291460
  1264.5 158.0 %copy-start.35 = (f32[4,1,512]{2,1,0:T(1,128)S(1)}, f32[4,1,512]{2,1,0:T(1,128)}, u32[]{:S(2)}) copy-start(f32[4,1,512]{2,1,0:T(1,128)} %copy-done.34) | copy-start | bytes 24580
  (57 other events, 1183.3 us)
Sparse Core Ops, SparseCore 0:
  10.4 29.0 all-gather.16
  41.7 82.4 all-gather.12
  126.6 24.6 all-gather.14
  152.8 82.0 all-gather.18
  236.5 40.0 all-gather.22
  304.8 80.4 all-gather.20
  387.6 39.7 all-gather.24
  429.2 41.5 all-gather.26
  472.4 82.0 all-gather.28
  594.4 166.6 reduce-scatter.12
  766.0 80.9 all-gather.30
  1006.0 186.0 reduce-scatter.14
  1195.0 26.3 reduce-scatter.18
  1224.2 27.9 reduce-scatter.20
  1254.3 168.1 reduce-scatter.10
  1425.9 64.4 reduce-scatter.28
  1493.8 65.6 reduce-scatter.24
  1562.9 65.6 reduce-scatter.26
  1632.2 35.1 reduce-scatter.16
  1670.8 35.1 reduce-scatter.22
  1708.4 56.4 all-reduce.6
where the time goes:
time: 1780 us
  waiting for transfers between devices  1180 us (66%)
  matrix products  230 us (13%)
  local copies, waits for them, and re-layouts  159 us (9%)
  other arithmetic  96.3 us (5%)
  blocking collectives  69 us (4%)
    reduce_scatter x1, waiting for transfers between devices, local(): lax.psum_scatter(grad_parts, 'col', scatter_dimension=0, tiled=True)  184 us
    reduce_scatter x1, waiting for transfers between devices, local(): lax.psum_scatter(jnp.dot(gate_grad, gate_copy.T, preferred_element_type=j...  165 us
    reduce_scatter x1, waiting for transfers between devices, local(): lax.psum_scatter(jnp.dot(hidden, down_copy, preferred_element_type=jnp.fl...  155 us
    all_gather x1, waiting for transfers between devices, local(): lax.all_gather(out_grad, 'col', axis=0, tiled=True)  83.7 us
    all_gather x1, waiting for transfers between devices, local(): middle_rows = lax.all_gather(middle_low, 'col', axis=0, tiled=True)  81 us
    all_gather x1, waiting for transfers between devices, local(): lax.all_gather(normed_two.astype(jnp.bfloat16), 'col', axis=0, tiled=True)  74.8 us
    reduce_scatter x1, waiting for transfers between devices, local(): lax.psum_scatter(up_wgrad, 'row', scatter_dimension=0, tiled=True)  69.1 us
    reduce_scatter x1, waiting for transfers between devices, local(): lax.psum_scatter(gate_wgrad, 'row', scatter_dimension=0, tiled=True)  69.1 us
  transfers between devices with their start and end apart: 22, of which 18 were waited for; matrix products, arithmetic and copies ran while one was open for 16% of the time, Pallas kernels for 0%

commit v1 on v0

v1 whole, which is shorter than its diff:
```python
import functools

import jax
import jax.numpy as jnp
from jax import lax
from jax.experimental import pallas as pl
from jax.experimental.pallas import tpu as pltpu
from jax.sharding import Mesh, PartitionSpec as P

norm_eps = 1e-05
rope_base = 10000.0
masked_score = -1e30
log2_e = 1.4426950408889634
f32 = jnp.float32
bf = jnp.bfloat16
vmem_bytes = 60 * 1024 * 1024


def mm(left, right, left_dim=1, right_dim=0):
    return lax.dot_general(
        left, right, (((left_dim,), (right_dim,)), ((), ())), preferred_element_type=f32
    )


def core_swap(a):
    return lax.ppermute(a, "core", [(0, 1), (1, 0)])


def row_swap(a, k):
    n = lax.axis_size("row")
    return lax.ppermute(a, "row", [(i, i ^ k) for i in range(n)])


def gather_rows(a):
    n = lax.axis_size("row")
    if n != 4:
        return [a] + [row_swap(a, k) for k in range(1, n)]
    along_x, along_y = row_swap(a, 1), row_swap(a, 2)
    half = a.shape[0] // 2
    corner = jnp.concatenate([row_swap(along_x[:half], 2), row_swap(along_y[half:], 1)], axis=0)
    return [a, along_x, along_y, corner]


def exchange_rows(parts):
    return [parts[0]] + [row_swap(parts[k], k) for k in range(1, len(parts))]


def reduce_rows(parts, wire):
    n = len(parts)
    if n != 4:
        total = parts[0].astype(f32)
        for k in range(1, n):
            total = total + row_swap(parts[k].astype(wire), k).astype(f32)
        return total
    half = parts[0].shape[0] // 2
    low = [p[:half].astype(f32) for p in parts]
    high = [p[half:].astype(f32) for p in parts]
    from_x = row_swap(jnp.stack([low[1], low[3]]).astype(wire), 1).astype(f32)
    from_y = row_swap(jnp.stack([high[2], high[3]]).astype(wire), 2).astype(f32)
    last_y = row_swap((low[2] + from_x[1]).astype(wire), 2).astype(f32)
    last_x = row_swap((high[1] + from_y[1]).astype(wire), 1).astype(f32)
    return jnp.concatenate(
        [low[0] + from_x[0] + last_y, high[0] + from_y[0] + last_x], axis=0
    )


def by_row(pieces, axis=0):
    r = lax.axis_index("row")
    n = len(pieces)
    size = pieces[0].shape[axis]
    shape = list(pieces[0].shape)
    shape[axis] = size * n
    whole = jnp.zeros(shape, pieces[0].dtype)
    for k, piece in enumerate(pieces):
        whole = lax.dynamic_update_slice_in_dim(whole, piece, (r ^ k) * size, axis)
    return whole


def reduce_plane(own_part, other_part, wire):
    n = lax.axis_size("row")
    rows = own_part.shape[0] // n
    both = own_part.astype(f32) + core_swap(other_part).astype(f32)
    return reduce_rows([both[k * rows : (k + 1) * rows] for k in range(n)], wire)


def attend_kernel(scale, tile, n_ref, wq_ref, k_ref, vt_ref, bias_ref, cos_ref, sin_ref,
                  q_ref, qt_ref, mix_ref, mixt_ref, lse_ref, qt_all):
    rows, _, width, block = wq_ref.shape
    head = k_ref.shape[1]
    half = head // 2
    tiles = n_ref.shape[0] // tile
    step = pl.program_id(1)

    @pl.when(step == 0)
    def _():
        q = mm(n_ref[:, :width], wq_ref[0, 0])
        for r in range(1, rows):
            q = q + mm(n_ref[:, r * width : (r + 1) * width], wq_ref[r, 0])
        qt = q.T
        for h in range(block // head):
            first = qt[h * head : h * head + half]
            second = qt[h * head + half : (h + 1) * head]
            turned = jnp.concatenate(
                [
                    first * cos_ref[...] - second * sin_ref[...],
                    second * cos_ref[...] + first * sin_ref[...],
                ],
                axis=0,
            )
            qt_ref[h * head : (h + 1) * head, :] = turned.astype(bf)
            q_ref[:, h * head : (h + 1) * head] = turned.T.astype(bf)
            for i in range(tiles):
                qt_all[h * tiles + i] = turned[:, i * tile : (i + 1) * tile].astype(bf)

    for i in range(tiles):
        for h in range(block // head):

            @pl.when(step == h * tiles + i)
            def _(h=h, i=i):
                cols = slice(i * tile, (i + 1) * tile)
                spots = slice(h * head, (h + 1) * head)
                scores = mm(k_ref[...], qt_all[h * tiles + i]) * (scale * log2_e) + bias_ref[:, cols]
                highest = jnp.max(scores, axis=0, keepdims=True)
                weights = jnp.exp2(scores - highest)
                total = jnp.sum(weights, axis=0, keepdims=True)
                mixed = mm(vt_ref[...], weights.astype(bf)) / total
                mixt_ref[spots, cols] = mixed.astype(bf)
                mix_ref[cols, spots] = mixed.T.astype(bf)
                lse_ref[0, h : h + 1, cols] = highest + jnp.log2(total)


def attend(normed, wq, keys, values_t, bias, cosine_t, sine_t, tile):
    rows, blocks, width, block = wq.shape
    tokens, dim = normed.shape
    head = keys.shape[1]
    heads = block // head
    whole = lambda a: pl.BlockSpec(a.shape, lambda z, j: (0,) * a.ndim)
    return pl.pallas_call(
        functools.partial(attend_kernel, head**-0.5, tile),
        grid=(blocks, heads * (tokens // tile)),
        in_specs=[
            whole(normed),
            pl.BlockSpec((rows, 1, width, block), lambda z, j: (0, z, 0, 0)),
            whole(keys),
            whole(values_t),
            whole(bias),
            whole(cosine_t),
            whole(sine_t),
        ],
        out_specs=[
            pl.BlockSpec((tokens, block), lambda z, j: (0, z)),
            pl.BlockSpec((block, tokens), lambda z, j: (z, 0)),
            pl.BlockSpec((tokens, block), lambda z, j: (0, z)),
            pl.BlockSpec((block, tokens), lambda z, j: (z, 0)),
            pl.BlockSpec((1, heads, tokens), lambda z, j: (z, 0, 0)),
        ],
        out_shape=[
            jax.ShapeDtypeStruct((tokens, blocks * block), bf),
            jax.ShapeDtypeStruct((blocks * block, tokens), bf),
            jax.ShapeDtypeStruct((tokens, blocks * block), bf),
            jax.ShapeDtypeStruct((blocks * block, tokens), bf),
            jax.ShapeDtypeStruct((blocks, heads, tokens), f32),
        ],
        scratch_shapes=[pltpu.VMEM((heads * (tokens // tile), head, tile), bf)],
        compiler_params=pltpu.CompilerParams(vmem_limit_bytes=vmem_bytes),
        cost_estimate=pl.CostEstimate(
            flops=2 * tokens * blocks * block * (dim + 2 * keys.shape[0]),
            bytes_accessed=16 << 20,
            transcendentals=tokens * blocks * heads * keys.shape[0],
        ),
        name="attend",
    )(normed, wq, keys, values_t, bias, cosine_t, sine_t)


def out_kernel(own, m_ref, w_ref, own_ref, other_ref):
    full = mm(m_ref[...], w_ref[0])
    own_ref[...] = full[:own]
    other_ref[...] = full[own:]


def out_project(mixed, wo, own):
    rows, depth, width = wo.shape
    tokens = mixed.shape[0]
    return pl.pallas_call(
        functools.partial(out_kernel, own),
        grid=(rows,),
        in_specs=[
            pl.BlockSpec((tokens, depth), lambda r: (0, 0)),
            pl.BlockSpec((1, depth, width), lambda r: (r, 0, 0)),
        ],
        out_specs=[
            pl.BlockSpec((own, width), lambda r: (0, r)),
            pl.BlockSpec((tokens - own, width), lambda r: (0, r)),
        ],
        out_shape=[
            jax.ShapeDtypeStruct((own, rows * width), f32),
            jax.ShapeDtypeStruct((tokens - own, rows * width), f32),
        ],
        compiler_params=pltpu.CompilerParams(vmem_limit_bytes=vmem_bytes),
        cost_estimate=pl.CostEstimate(
            flops=2 * tokens * depth * rows * width, bytes_accessed=10 << 20, transcendentals=0
        ),
        name="out_project",
    )(mixed, wo)


def attend_back_kernel(scale, tile, ml_ref, wo_ref, wq_ref, nt_ref, k_ref, kt_ref, v_ref, bias_ref,
                       cos_ref, sin_ref, q_ref, qt_ref, mixt_ref, lse_ref,
                       dwq_ref, dwo_ref, dn_ref, dk_ref, dv_ref, do_all, dot_all, dq_all):
    rows, _, width, block = wq_ref.shape
    head = k_ref.shape[1]
    half = head // 2
    tiles = ml_ref.shape[0] // tile
    heads = block // head
    step = pl.program_id(1)

    @pl.when((pl.program_id(0) == 0) & (step == 0))
    def _():
        dk_ref[...] = jnp.zeros_like(dk_ref)
        dv_ref[...] = jnp.zeros_like(dv_ref)
        dn_ref[...] = jnp.zeros_like(dn_ref)

    @pl.when(step == 0)
    def _():
        grad = mm(ml_ref[:, :width], wo_ref[0, 0], 1, 1)
        for r in range(1, rows):
            grad = grad + mm(ml_ref[:, r * width : (r + 1) * width], wo_ref[r, 0], 1, 1)
        grad_t = grad.T
        do_all[...] = grad.astype(bf)
        dot_all[...] = grad_t.astype(bf)

    for i in range(tiles):
        for h in range(heads):

            @pl.when(step == h * tiles + i)
            def _(h=h, i=i):
                cols = slice(i * tile, (i + 1) * tile)
                spots = slice(h * head, (h + 1) * head)
                scores = mm(k_ref[...], qt_ref[spots, cols]) * (scale * log2_e) + bias_ref[:, cols]
                soft = jnp.exp2(scores - lse_ref[0, h : h + 1, cols])
                prob_grad = mm(v_ref[...], dot_all[spots, cols])
                row_dot = jnp.sum(soft * prob_grad, axis=0, keepdims=True)
                score_grad = (soft * (prob_grad - row_dot)).astype(bf)
                dv_ref[...] += mm(soft.astype(bf), do_all[cols, spots])
                dk_ref[...] += mm(score_grad, q_ref[cols, spots]) * scale
                dqt = mm(kt_ref[...], score_grad) * scale
                first, second = dqt[:half], dqt[half:]
                cosine, sine = cos_ref[:, cols], sin_ref[:, cols]
                turned = jnp.concatenate(
                    [first * cosine + second * sine, second * cosine - first * sine], axis=0
                )
                dq_all[cols, spots] = turned.T.astype(bf)

    @pl.when(step == tiles * heads - 1)
    def _():
        dq = dq_all[...]
        for r in range(rows):
            span = slice(r * width, (r + 1) * width)
            dwq_ref[r, 0] = mm(nt_ref[span, :], dq).astype(bf)
            dwo_ref[r, 0] = mm(mixt_ref[...], ml_ref[:, span]).astype(bf)
            dn_ref[:, span] += mm(dq, wq_ref[r, 0], 1, 1)


def attend_back(middle_low, wo, wq, normed_t, keys, keys_t, values, bias, cosine_t, sine_t,
                q, qt, mixed_t, lse, tile):
    rows, blocks, width, block = wq.shape
    tokens, dim = middle_low.shape
    keys_in, head = keys.shape
    heads = block // head
    whole = lambda a: pl.BlockSpec(a.shape, lambda z, j: (0,) * a.ndim)
    return pl.pallas_call(
        functools.partial(attend_back_kernel, head**-0.5, tile),
        grid=(blocks, heads * (tokens // tile)),
        in_specs=[
            whole(middle_low),
            pl.BlockSpec((rows, 1, block, width), lambda z, j: (0, z, 0, 0)),
            pl.BlockSpec((rows, 1, width, block), lambda z, j: (0, z, 0, 0)),
            whole(normed_t),
            whole(keys),
            whole(keys_t),
            whole(values),
            whole(bias),
            whole(cosine_t),
            whole(sine_t),
            pl.BlockSpec((tokens, block), lambda z, j: (0, z)),
            pl.BlockSpec((block, tokens), lambda z, j: (z, 0)),
            pl.BlockSpec((block, tokens), lambda z, j: (z, 0)),
            pl.BlockSpec((1, heads, tokens), lambda z, j: (z, 0, 0)),
        ],
        out_specs=[
            pl.BlockSpec((rows, 1, width, block), lambda z, j: (0, z, 0, 0)),
            pl.BlockSpec((rows, 1, block, width), lambda z, j: (0, z, 0, 0)),
            pl.BlockSpec((tokens, dim), lambda z, j: (0, 0)),
            pl.BlockSpec((keys_in, head), lambda z, j: (0, 0)),
            pl.BlockSpec((keys_in, head), lambda z, j: (0, 0)),
        ],
        out_shape=[
            jax.ShapeDtypeStruct((rows, blocks, width, block), bf),
            jax.ShapeDtypeStruct((rows, blocks, block, width), bf),
            jax.ShapeDtypeStruct((tokens, dim), f32),
            jax.ShapeDtypeStruct((keys_in, head), f32),
            jax.ShapeDtypeStruct((keys_in, head), f32),
        ],
        scratch_shapes=[
            pltpu.VMEM((tokens, block), bf),
            pltpu.VMEM((block, tokens), bf),
            pltpu.VMEM((tokens, block), bf),
        ],
        compiler_params=pltpu.CompilerParams(vmem_limit_bytes=vmem_bytes),
        cost_estimate=pl.CostEstimate(
            flops=2 * tokens * blocks * block * (4 * dim + 5 * keys_in),
            bytes_accessed=32 << 20,
            transcendentals=tokens * blocks * heads * keys_in,
        ),
        name="attend_back",
    )(middle_low, wo, wq, normed_t, keys, keys_t, values, bias, cosine_t, sine_t, q, qt, mixed_t, lse)


def mlp_kernel(x_ref, g_ref, gate_ref, up_ref, down_ref, hid_ref, gg_ref, ug_ref, dx_ref):
    gate = mm(x_ref[...], gate_ref[...], 1, 1)
    up = mm(x_ref[...], up_ref[...], 1, 1)
    hidden_grad = mm(g_ref[...], down_ref[...], 1, 1)
    sig = jax.nn.sigmoid(gate)
    silu = gate * sig
    hid_ref[...] = (silu * up).astype(bf)
    gate_grad = (hidden_grad * up * sig * (1.0 + gate * (1.0 - sig))).astype(bf)
    up_grad = (hidden_grad * silu).astype(bf)
    gg_ref[...] = gate_grad
    ug_ref[...] = up_grad
    dx_ref[...] = (mm(gate_grad, gate_ref[...]) + mm(up_grad, up_ref[...])).astype(bf)


def mlp(x, g, gate_w, up_w, down_w, tile):
    tokens, dim = x.shape
    units = gate_w.shape[0]
    rows_of = lambda width: pl.BlockSpec((tile, width), lambda t: (t, 0))
    weight = pl.BlockSpec((units, dim), lambda t: (0, 0))
    return pl.pallas_call(
        mlp_kernel,
        grid=(tokens // tile,),
        in_specs=[rows_of(dim), rows_of(dim), weight, weight, weight],
        out_specs=[rows_of(units), rows_of(units), rows_of(units), rows_of(dim)],
        out_shape=[jax.ShapeDtypeStruct((tokens, units), bf)] * 3
        + [jax.ShapeDtypeStruct((tokens, dim), bf)],
        compiler_params=pltpu.CompilerParams(vmem_limit_bytes=vmem_bytes),
        cost_estimate=pl.CostEstimate(
            flops=10 * tokens * units * dim, bytes_accessed=24 << 20, transcendentals=tokens * units
        ),
        name="mlp",
    )(x, g, gate_w, up_w, down_w)


def rotate(values, cosine, sine):
    half = values.shape[1] // 2
    first, second = values[:, :half], values[:, half:]
    return jnp.concatenate([first * cosine - second * sine, second * cosine + first * sine], axis=1)


def norm_backward(values, factor, gain, grad_rows):
    weighted = grad_rows * gain
    inner_mean = jnp.mean(weighted * values, axis=-1, keepdims=True)
    input_part = factor * weighted - values * factor * factor * factor * inner_mean
    gain_part = jnp.sum(grad_rows * values * factor, axis=0)
    return (input_part, gain_part)


def local(layer_input, out_grad, kv_grad, lengths, token_deal, attn_gain, query_weight, key_weight,
          value_weight, out_weight, mlp_gain, gate_weight, up_weight, down_weight):
    r, z, c = lax.axis_index("row"), lax.axis_index("z"), lax.axis_index("core")
    n_rows, n_z = lax.axis_size("row"), lax.axis_size("z")
    own, dim = layer_input.shape
    width, block = query_weight.shape
    head = key_weight.shape[1]
    units = gate_weight.shape[1]
    piece = units // n_rows
    pick = lambda a, i, axis=0: lax.dynamic_index_in_dim(a, i, axis, keepdims=False)
    first_core = c == 0

    wq_z = lax.all_gather(query_weight.astype(bf), "z", axis=0)
    wo_z = lax.all_gather(out_weight.astype(bf), "z", axis=0)
    mlp_own = jnp.stack(
        [gate_weight.astype(bf).T, up_weight.astype(bf).T, down_weight.astype(bf)]
    ).reshape(3, n_rows, piece, width)
    mlp_parts = by_row(exchange_rows([pick(mlp_own, r ^ k, 1) for k in range(n_rows)]), axis=2)
    gate_w, up_w, down_w = [
        lax.all_gather(mlp_parts[i], "z", axis=0).reshape(n_z * piece, dim) for i in range(3)
    ]
    gains = jnp.concatenate([attn_gain, mlp_gain]).astype(bf).reshape(-1, head)
    small = jnp.concatenate([jnp.where(first_core, key_weight, value_weight).astype(bf), gains])
    small = by_row(exchange_rows([small] * n_rows)).reshape(n_rows, -1, head)
    kv_w = small[:, :width].reshape(dim, head)
    gains = small[:, width:].reshape(n_rows, 2, width).astype(f32)
    gain_one, gain_two = gains[:, 0].reshape(dim), gains[:, 1].reshape(dim)

    chip = 2 * own
    deal = token_deal[0]
    ends = jnp.cumsum(lengths[0])

    def start_of(initial):
        return jnp.sum(jnp.where(ends[None, :] <= initial[:, None], lengths[0][None, :], 0), axis=1)

    chip_slots = lax.dynamic_slice_in_dim(deal, z * chip, chip, 0)
    swap_halves = lambda a: jnp.where(first_core, a, jnp.roll(a, own, axis=0))
    initial = swap_halves(chip_slots)
    start = start_of(initial)
    angles = (initial - start).astype(f32)[:, None] * (
        rope_base ** (-jnp.arange(head // 2, dtype=f32) / (head // 2))
    )
    cosine, sine = jnp.cos(angles), jnp.sin(angles)
    bias = jnp.where(
        (deal[:, None] >= start[None, :]) & (deal[:, None] <= initial[None, :]), 0.0, masked_score
    ).astype(f32)
    kv_cosine, kv_sine = jnp.where(first_core, cosine, 1.0), jnp.where(first_core, sine, 0.0)

    chip_input = jnp.concatenate([layer_input, core_swap(layer_input)]).astype(f32)
    factor_chip = lax.rsqrt(jnp.mean(chip_input * chip_input, axis=-1, keepdims=True) + norm_eps)
    normed = (chip_input * factor_chip * gain_one).astype(bf)
    input_rows, factor_one = chip_input[:own], factor_chip[:own]
    kv_own = swap_halves(rotate(mm(normed, kv_w), kv_cosine, kv_sine).astype(bf))
    kv_mine = lax.all_gather(kv_own, "z", axis=0, tiled=True)
    kv_other = core_swap(kv_mine)
    keys = jnp.where(first_core, kv_mine, kv_other)
    values = jnp.where(first_core, kv_other, kv_mine)
    shared_own = lax.dynamic_slice_in_dim(
        jnp.concatenate([keys, values], axis=1), (2 * z + c) * own, own, 0
    )

    wq = by_row([a[None] for a in gather_rows(wq_z)])
    wo = by_row([a[None] for a in gather_rows(wo_z)])
    tile = own
    q, qt, mixed, mixed_t, lse = attend(
        normed, wq, keys, values.T, bias, cosine.T, sine.T, tile
    )
    att_own, att_other = out_project(mixed, wo.reshape(n_rows, n_z * block, width), own)
    middle = input_rows + (att_own + core_swap(att_other))
    factor_two = lax.rsqrt(jnp.mean(middle * middle, axis=-1, keepdims=True) + norm_eps)
    normed_two = (middle * factor_two * gain_two).astype(bf)

    grads_own = jnp.concatenate(gather_rows(out_grad))
    grads_other = core_swap(grads_own)
    rows_own = jnp.concatenate(gather_rows(normed_two))
    rows_other = core_swap(rows_own)
    hid_a, gg_a, ug_a, dx_a = mlp(rows_own, grads_own, gate_w, up_w, down_w, own)
    hid_b, gg_b, ug_b, dx_b = mlp(rows_other, grads_other, gate_w, up_w, down_w, own)
    normed_two_grad = reduce_plane(dx_a, dx_b, bf)
    down_part = (mm(hid_a, grads_own, 0, 0) + mm(hid_b, grads_other, 0, 0)).astype(bf)
    gate_part = (mm(gg_a, rows_own, 0, 0) + mm(gg_b, rows_other, 0, 0)).astype(bf)
    up_part = (mm(ug_a, rows_own, 0, 0) + mm(ug_b, rows_other, 0, 0)).astype(bf)
    output_rows = middle + reduce_plane(
        mm(hid_a, down_w).astype(bf), mm(hid_b, down_w).astype(bf), bf
    )
    mlp_sums = jnp.stack(
        [
            lax.psum_scatter(a, "z", scatter_dimension=0, tiled=True)
            for a in (gate_part, up_part, down_part)
        ]
    ).reshape(3, piece, n_rows, width)
    mlp_grads = by_row(exchange_rows([pick(mlp_sums, r ^ k, 2) for k in range(n_rows)]), axis=1)
    mlp_grads = mlp_grads.astype(f32)

    middle_part, gain_two_grad = norm_backward(middle, factor_two, gain_two, normed_two_grad)
    middle_grad = out_grad.astype(f32) + middle_part
    low_own = middle_grad.astype(bf)
    middle_low = jnp.concatenate([low_own, core_swap(low_own)])

    dwq, dwo, dn, dk, dv = attend_back(
        middle_low, wo, wq, normed.T, keys, keys.T, values, bias, cosine.T, sine.T,
        q, qt, mixed_t, lse, tile,
    )
    dwo_rows = reduce_rows([pick(dwo, r ^ k) for k in range(n_rows)], bf).astype(bf)
    dwq_rows = reduce_rows([pick(dwq, r ^ k) for k in range(n_rows)], bf).astype(bf)
    out_wgrad = lax.psum_scatter(dwo_rows, "z", scatter_dimension=0, tiled=False).astype(f32)
    query_wgrad = lax.psum_scatter(dwq_rows, "z", scatter_dimension=0, tiled=False).astype(f32)

    kv_sum = jnp.where(first_core, dk, dv) + core_swap(jnp.where(first_core, dv, dk))
    kv_sum = lax.all_to_all(
        kv_sum.astype(bf).reshape(n_z, chip, head), "z", split_axis=0, concat_axis=0, tiled=False
    )
    kv_grad32 = kv_grad.astype(f32)
    kv_left, kv_right = kv_grad[:, :head], kv_grad[:, head:]
    kv_given = jnp.concatenate(
        [
            jnp.where(first_core, kv_left, kv_right),
            core_swap(jnp.where(first_core, kv_right, kv_left)),
        ]
    ).astype(f32)
    kv_sum = swap_halves(jnp.sum(kv_sum.astype(f32), axis=0)) + kv_given
    kv_low = rotate(kv_sum, kv_cosine, -kv_sine).astype(bf)
    kv_wgrad = mm(normed, kv_low, 0, 0)
    dn = dn + mm(kv_low, kv_w, 1, 1)
    normed_one_grad = dn[:own] + core_swap(dn[own:])
    input_part, gain_one_grad = norm_backward(input_rows, factor_one, gain_one, normed_one_grad)
    input_grad = middle_grad + input_part

    gain_rows = jnp.stack(
        [gain_one_grad.reshape(n_rows, width), gain_two_grad.reshape(n_rows, width)], axis=1
    ).reshape(n_rows, -1, head)
    small = jnp.concatenate([kv_wgrad.reshape(n_rows, width, head), gain_rows], axis=1)
    small = reduce_rows([pick(small, r ^ k) for k in range(n_rows)], f32)
    k = 1
    while k < n_z:
        small = small + lax.ppermute(small, "z", [(i, i ^ k) for i in range(n_z)])
        k *= 2
    small_other = core_swap(small)
    key_wgrad = jnp.where(first_core, small[:width], small_other[:width])
    value_wgrad = jnp.where(first_core, small_other[:width], small[:width])
    gain_sums = (small[width:] + small_other[width:]).reshape(2, width)
    return (
        output_rows.astype(bf),
        input_grad,
        shared_own,
        gain_sums[0],
        query_wgrad,
        key_wgrad,
        value_wgrad,
        out_wgrad,
        gain_sums[1],
        mlp_grads[0].T,
        mlp_grads[1].T,
        mlp_grads[2],
    )


def solution(mesh):
    n_rows, n_cols = mesh.shape["row"], mesh.shape["col"]
    split = Mesh(mesh.devices.reshape(n_rows, n_cols // 2, 2), ("row", "z", "core"))
    everywhere, col = ("row", "z", "core"), ("z", "core")
    in_specs = (
        P(everywhere, None),
        P(everywhere, None),
        P(everywhere, None),
        P("row", None),
        P("row", None),
        P("row"),
        P("row", col),
        P("row", None),
        P("row", None),
        P(col, "row"),
        P("row"),
        P("row", col),
        P("row", col),
        P(col, "row"),
    )
    out_specs = (
        P(everywhere, None),
        P(everywhere, None),
        P(everywhere, None),
        P("row"),
        P("row", col),
        P("row", None),
        P("row", None),
        P(col, "row"),
        P("row"),
        P("row", col),
        P("row", col),
        P(col, "row"),
    )
    return jax.shard_map(
        local, mesh=split, in_specs=in_specs, out_specs=out_specs, check_vma=False
    )
```

time: 1780 us -> 717 us (0.40)
  waiting for transfers between devices: 1180 us -> 145 us
  matrix products: 230 us -> 55.8 us
  Pallas kernels: 0 us -> 141 us
  starting transfers between devices: 5.87 us -> 63.5 us
  blocking collectives: 69 us -> 19.1 us
  other arithmetic: 96.3 us -> 123 us
    reduce_scatter x10 -> x5, waiting for transfers between devices: 747 us -> 0.03 us  [the longest x1 0.02 us: local(): lax.psum_scatter(dwo_rows, 'z', scatter_dimension=0, tiled=False)]
    all_gather x10 -> x5, waiting for transfers between devices: 357 us -> 5.29 us  [the longest x3 5.28 us: local(): lax.all_gather(mlp_parts[i], 'z', axis=0).reshape(n_z * piece, dim)]
    dot_general x49 -> x11, matrix products: 230 us -> 55.8 us  [mm(): lax.dot_general(left, right, (((left_dim,), (right_dim,)), ((), ())), pre...]
    pallas_call x0 -> x5, Pallas kernels: none -> 141 us  [the longest x1 53 us: attend_back(): pl.pallas_call(functools.partial(attend_back_kernel, head ** (-0.5), tile...]
    ppermute x0 -> x59, waiting for transfers between devices: none -> 139 us  [the longest x45 128 us: row_swap(): return lax.ppermute(a, 'row', [(i, i ^ k) for i in range(n)])]
    gather x11 -> x0, local copies, waits for them, and re-layouts: 97.8 us -> none  [the longest x2 17.1 us: local(): mixed_orig[slot_order].reshape(group_rows, head_count * head_dim)]
    psum x1 -> x0, waiting for transfers between devices: 58.9 us -> none  [local(): lax.psum((summed[0], summed[2], summed[3], summed[5]), 'col')]
    ppermute x0 -> x59, starting transfers between devices: none -> 58.1 us  [the longest x45 52.1 us: row_swap(): return lax.ppermute(a, 'row', [(i, i ^ k) for i in range(n)])]
  transfers between devices with their start and end apart: 22 -> 70, of which waited for: 18 -> 25; matrix products, arithmetic and copies ran while one was open for 16% -> 42% of each run, Pallas kernels for 0% -> 16%
where the time goes in v1:
time: 717 us; the launch traced here: 709 us
  local copies, waits for them, and re-layouts  146 us (20%)
  waiting for transfers between devices  145 us (20%)
  Pallas kernels  141 us (20%)
  other arithmetic  123 us (17%)
  starting transfers between devices  63.5 us (9%)
  matrix products  55.8 us (8%)
  blocking collectives  19.1 us (3%)
  between operations  15.5 us (2%)
    ppermute x45, waiting for transfers between devices, row_swap(): return lax.ppermute(a, 'row', [(i, i ^ k) for i in range(n)])  128 us
    dot_general x11, matrix products, mm(): lax.dot_general(left, right, (((left_dim,), (right_dim,)), ((), ())), pre...  55.8 us
    pallas_call x1, Pallas kernels, attend_back(): pl.pallas_call(functools.partial(attend_back_kernel, head ** (-0.5), tile...  53 us
    ppermute x45, starting transfers between devices, row_swap(): return lax.ppermute(a, 'row', [(i, i ^ k) for i in range(n)])  52.1 us
    pallas_call x2, Pallas kernels, mlp(): pl.pallas_call(mlp_kernel, grid=(tokens // tile,), in_specs=[rows_of(dim)...  51.1 us
    unnamed x153, local copies, waits for them, and re-layouts  34.9 us
    pallas_call x1, Pallas kernels, attend(): pl.pallas_call(functools.partial(attend_kernel, head ** (-0.5), tile), gr...  30.8 us
    dynamic_update_slice x17, local copies, waits for them, and re-layouts, by_row(): whole = lax.dynamic_update_slice_in_dim(whole, piece, (r ^ k) * size, axis)  20.2 us
  transfers between devices with their start and end apart: 70, of which 25 were waited for; matrix products, arithmetic and copies ran while one was open for 42% of the time, Pallas kernels for 16%

profile of v1, /device:TPU:0, one launch (start us, length us, event | category | flops | bytes accessed | tf_op | source)
XLA Modules:
  0.0 709.2 jit_solution(13452055858007613306)
XLA Ops:
  22.9 8.1 %collective-permute-done.22 = bf16[3,176,512]{2,1,0:T(8,128)(2,1)} collective-permute-done((bf16[3,176,512]{2,1,0:T(8,128)(2,1)S(1)}, bf16[3,176,512]{2,1,0:T(8,128)(2,1)}, u32[]{:S(2)}, u32[]{:S(2)}) %collective-permute-start.22) | collective-permute-done | bytes 540704 | tf_op jit(solution)/shard_map/ppermute | solution.py:31
  32.9 10.2 %collective-permute-done.23 = bf16[3,176,512]{2,1,0:T(8,128)(2,1)S(1)} collective-permute-done((bf16[3,176,512]{2,1,0:T(8,128)(2,1)S(1)}, bf16[3,176,512]{2,1,0:T(8,128)(2,1)S(1)}, u32[]{:S(2)}, u32[]{:S(2)}) %collective-permute-start.23) | collective-permute-done | bytes 540704 | tf_op jit(solution)/shard_map/ppermute | solution.py:31
  62.0 19.1 %all_gather.26 = bf16[2048,128]{1,0:T(8,128)(2,1)} all-gather(bf16[512,128]{1,0:T(8,128)(2,1)S(1)} %maximum_select_fusion.1), channel_id=1, replica_groups=mesh['row'=4,'z'=4,'core'=2] {'z'}, dimensions={0}, use_global_device_ids=true | all-gather | bytes 655360 | tf_op jit(solution)/shard_map/all_gather | solution.py:420
  101.6 5.8 collective-permute-done.4
  112.3 17.6 %collective-permute-done.9 = bf16[4,256,512]{2,1,0:T(8,128)(2,1)} collective-permute-done((bf16[4,256,512]{2,1,0:T(8,128)(2,1)}, bf16[4,256,512]{2,1,0:T(8,128)(2,1)}, u32[]{:S(2)}, u32[]{:S(2)}) %collective-permute-start.9) | collective-permute-done | bytes 1048608 | tf_op jit(solution)/shard_map/ppermute | solution.py:31
  145.7 30.8 %attend.1 = (bf16[512,1024]{1,0:T(8,128)(2,1)}, bf16[1024,512]{1,0:T(8,128)(2,1)}, bf16[512,1024]{1,0:T(8,128)(2,1)}, bf16[1024,512]{1,0:T(8,128)(2,1)}, f32[4,2,512]{2,1,0:T(2,128)}) custom-call(bf16[512,2048]{1,0:T(8,128)(2,1)} %copy.102.n_ref, bf16[4,4,512,256]{3,2,1,0:T(8,128)(2,1)} %fusion.33.wq_ref, bf16[2048,128]{1,0:T(8,128)(2,1)} %get-tuple-element.165.k_ref, ...), custom_call_target="tpu_custom_call" | custom-call | flops 6442450944 | bytes 16777216 | tf_op jit(solution)/shard_map/attend/pallas_call | solution.py:138
  177.7 6.3 out_project.1
  201.7 11.6 %collective-permute-done.18 = bf16[256,2048]{1,0:T(8,128)(2,1)} collective-permute-done((bf16[256,2048]{1,0:T(8,128)(2,1)}, bf16[256,2048]{1,0:T(8,128)(2,1)}, u32[]{:S(2)}, u32[]{:S(2)}) %collective-permute-start.18) | collective-permute-done | bytes 1048608 | tf_op jit(solution)/shard_map/ppermute | solution.py:31
  225.2 10.5 %collective-permute-done.14 = bf16[256,2048]{0,1:T(8,128)(2,1)S(1)} collective-permute-done((bf16[256,2048]{0,1:T(8,128)(2,1)}, bf16[256,2048]{0,1:T(8,128)(2,1)S(1)}, u32[]{:S(2)}, u32[]{:S(2)}) %collective-permute-start.14) | collective-permute-done | bytes 1048608 | tf_op jit(solution)/shard_map/ppermute | solution.py:31
  236.7 11.0 %collective-permute-done.20 = bf16[128,2048]{1,0:T(8,128)(2,1)} collective-permute-done((bf16[128,2048]{1,0:T(8,128)(2,1)}, bf16[128,2048]{1,0:T(8,128)(2,1)}, u32[]{:S(2)}, u32[]{:S(2)}) %collective-permute-start.20) | collective-permute-done | bytes 524320 | tf_op jit(solution)/shard_map/ppermute | solution.py:31
  265.4 6.5 copy.109.x_ref
  272.0 5.3 all-gather.12.cloned.1.call-done
  277.3 25.5 %mlp.2 = (bf16[1024,704]{1,0:T(8,128)(2,1)}, bf16[1024,704]{1,0:T(8,128)(2,1)}, bf16[1024,704]{1,0:T(8,128)(2,1)}, bf16[1024,2048]{1,0:T(8,128)(2,1)}) custom-call(bf16[1024,2048]{1,0:T(8,128)(2,1)} %copy.109.x_ref, bf16[1024,2048]{1,0:T(8,128)(2,1)} %constant_dynamic-update-slice_fusion.5.g_ref, bf16[704,2048]{1,0:T(8,128)(2,1)} %bitcast.259, ...), custom_call_target="tpu_custom_call" | custom-call | flops 14763950080 | bytes 25165824 | tf_op jit(solution)/shard_map/mlp/pallas_call | solution.py:338
  302.8 6.5 copy.111.x_ref
  309.3 25.5 %mlp.3 = (bf16[1024,704]{1,0:T(8,128)(2,1)}, bf16[1024,704]{1,0:T(8,128)(2,1)}, bf16[1024,704]{1,0:T(8,128)(2,1)}, bf16[1024,2048]{1,0:T(8,128)(2,1)}) custom-call(bf16[1024,2048]{1,0:T(8,128)(2,1)} %copy.111.x_ref, bf16[1024,2048]{1,0:T(8,128)(2,1)} %collective-permute-done.26.g_ref, bf16[704,2048]{1,0:T(8,128)(2,1)} %bitcast.260, ...), custom_call_target="tpu_custom_call" | custom-call | flops 14763950080 | bytes 25165824 | tf_op jit(solution)/shard_map/mlp/pallas_call | solution.py:338
  334.8 6.4 fusion.86
  341.3 7.3 %add_convert_fusion.1 = bf16[704,2048]{1,0:T(8,128)(2,1)} fusion(f32[704,2048]{1,0:T(8,128)S(1)} %fusion.86, bf16[1024,704]{1,0:T(8,128)(2,1)S(1)} %copy-done.69, bf16[1024,2048]{0,1:T(8,128)(2,1)} %constant_dynamic-update-slice_fusion), kind=kOutput, calls=%fused_computation.3 | convolution fusion | flops 2955673600 | bytes 14286848 | tf_op jit(solution)/shard_map/dot_general | solution.py:20
  348.7 6.5 copy.115
  355.1 6.2 fusion.85
  361.3 7.3 %add_convert_fusion.2 = bf16[704,2048]{1,0:T(8,128)(2,1)} fusion(f32[704,2048]{1,0:T(8,128)S(1)} %fusion.85, bf16[1024,704]{1,0:T(8,128)(2,1)S(1)} %copy-done.68, bf16[1024,2048]{0,1:T(8,128)(2,1)} %constant_dynamic-update-slice_fusion), kind=kOutput, calls=%fused_computation.4 | convolution fusion | flops 2955673600 | bytes 14286848 | tf_op jit(solution)/shard_map/dot_general | solution.py:20
  372.4 6.4 copy.114
  378.8 7.8 %convolution_convert_fusion = bf16[1024,2048]{0,1:T(8,128)(2,1)} fusion(bf16[1024,704]{1,0:T(8,128)(2,1)} %get-tuple-element.36, bf16[704,2048]{1,0:T(8,128)(2,1)} %bitcast.265), kind=kOutput, calls=%fused_computation.8 | convolution fusion | flops 2954887168 | bytes 8519680 | tf_op jit(solution)/shard_map/dot_general | solution.py:20
  387.1 7.7 %convert_add_fusion = (f32[1024,2048]{0,1:T(8,128)S(1)}, bf16[1024,2048]{0,1:T(8,128)(2,1)}) fusion(bf16[1024,2048]{0,1:T(8,128)(2,1)} %collective-permute-done.32, bf16[1024,2048]{0,1:T(8,128)(2,1)} %copy.114), kind=kLoop, calls=%fused_computation | loop fusion | flops 8388608 | bytes 20971520 | tf_op jit(solution)/shard_map/add | solution.py:82
  412.0 11.7 %collective-permute-done.35 = bf16[2,128,2048]{1,2,0:T(8,128)(2,1)S(1)} collective-permute-done((bf16[2,128,2048]{1,2,0:T(8,128)(2,1)S(1)}, bf16[2,128,2048]{1,2,0:T(8,128)(2,1)S(1)}, u32[]{:S(2)}, u32[]{:S(2)}) %collective-permute-start.35) | collective-permute-done | bytes 1048608 | tf_op jit(solution)/shard_map/ppermute | solution.py:31
  428.9 7.2 %add_convert_fusion = bf16[704,2048]{1,0:T(8,128)(2,1)} fusion(f32[704,2048]{1,0:T(8,128)S(1)} %fusion.87, bf16[1024,704]{1,0:T(8,128)(2,1)S(1)} %copy-done.67, bf16[1024,2048]{1,0:T(8,128)(2,1)} %constant_dynamic-update-slice_fusion.5.g_ref), kind=kOutput, calls=%fused_computation.2 | convolution fusion | flops 2955673600 | bytes 14286848 | tf_op jit(solution)/shard_map/dot_general | solution.py:20
  447.0 7.8 %fusion.78 = (bf16[1024,2048]{0,1:T(8,128)(2,1)S(1)}, f32[1024,2048]{0,1:T(8,128)}) fusion(bf16[1024,2048]{0,1:T(8,128)(2,1)} %collective-permute-done.27, bf16[1024,2048]{0,1:T(8,128)(2,1)S(1)} %copy-done.28), kind=kLoop, calls=%fused_computation.246 | loop fusion | flops 8388608 | bytes 20971520 | tf_op jit(solution)/shard_map/convert.36
  466.6 53.0 %attend_back.1 = (bf16[4,4,512,256]{3,2,1,0:T(8,128)(2,1)}, bf16[4,4,256,512]{3,2,1,0:T(8,128)(2,1)}, f32[512,2048]{1,0:T(8,128)}, f32[2048,128]{1,0:T(8,128)}, f32[2048,128]{1,0:T(8,128)}) custom-call(bf16[512,2048]{1,0:T(8,128)(2,1)} %copy.116.ml_ref, bf16[4,4,256,512]{3,2,1,0:T(8,128)(2,1)} %fusion.34.wo_ref, bf16[4,4,512,256]{3,2,1,0:T(8,128)(2,1)} %fusion.33.wq_ref, ...), custom_call_target="tpu_custom_call" | custom-call | flops 19327352832 | bytes 33554432 | tf_op jit(solution)/shard_map/attend_back/pallas_call | solution.py:271
  551.2 5.3 copy.118
  624.7 8.3 %collective-permute-done.51 = bf16[2,512,256]{2,1,0:T(8,128)(2,1)} collective-permute-done((bf16[2,512,256]{2,1,0:T(8,128)(2,1)}, bf16[2,512,256]{2,1,0:T(8,128)(2,1)}, u32[]{:S(2)}, u32[]{:S(2)}) %collective-permute-start.51) | collective-permute-done | bytes 524320 | tf_op jit(solution)/shard_map/ppermute | solution.py:31
  650.6 6.9 collective-permute-done.43
  678.8 9.2 %collective-permute-done.46 = f32[520,128]{1,0:T(8,128)} collective-permute-done((f32[520,128]{1,0:T(8,128)}, f32[520,128]{1,0:T(8,128)}, u32[]{:S(2)}, u32[]{:S(2)}) %collective-permute-start.46) | collective-permute-done | bytes 266272 | tf_op jit(solution)/shard_map/ppermute | solution.py:502
  689.2 5.5 subtract_add_fusion
  (443 shorter events, 322.8 us)
Async XLA Ops:
  7.2 73.8 %all-gather.14.cloned.1.call-start = ((), (), s32[]{:S(2)}) async-start(), calls=%async_computation.14 | async-start | bytes 1310720 | tf_op jit(solution)/shard_map/all_gather | solution.py:379
  9.1 74.5 %all-gather.16.cloned.1.call-start = ((), (), s32[]{:S(2)}) async-start(), calls=%async_computation.15 | async-start | bytes 1310720 | tf_op jit(solution)/shard_map/all_gather | solution.py:380
  11.0 261.0 %all-gather.8.cloned.1.call-start = ((), (), s32[]{:S(2)}) async-start(), calls=%async_computation.6 | async-start | bytes 3604480 | tf_op jit(solution)/shard_map/all_gather | solution.py:386
  47.9 224.0 %all-gather.10.cloned.1.call-start = ((), (), s32[]{:S(2)}) async-start(), calls=%async_computation.7 | async-start | bytes 3604480 | tf_op jit(solution)/shard_map/all_gather | solution.py:386
  83.7 46.2 %collective-permute-start.9 = (bf16[4,256,512]{2,1,0:T(8,128)(2,1)}, bf16[4,256,512]{2,1,0:T(8,128)(2,1)}, u32[]{:S(2)}, u32[]{:S(2)}) collective-permute-start(bf16[4,256,512]{2,1,0:T(8,128)(2,1)} %bitcast.236), channel_id=1, source_target_pairs={{0,8},{8,0},{16,24},{24,16},{1,9},{9,1},{17,25},{25,17},{2,10},{10... | collective-permute-start | bytes 3145736 | tf_op jit(solution)/shard_map/ppermute | solution.py:31
  84.2 47.9 %collective-permute-start.10 = (bf16[4,256,512]{2,1,0:T(8,128)(2,1)}, bf16[4,256,512]{2,1,0:T(8,128)(2,1)}, u32[]{:S(2)}, u32[]{:S(2)}) collective-permute-start(bf16[4,256,512]{2,1,0:T(8,128)(2,1)} %bitcast.237), channel_id=1, source_target_pairs={{0,16},{8,24},{16,0},{24,8},{1,17},{9,25},{17,1},{25,9},{2,18},{10... | collective-permute-start | bytes 3145736 | tf_op jit(solution)/shard_map/ppermute | solution.py:31
  88.8 188.5 %all-gather.12.cloned.1.call-start = ((), (), s32[]{:S(2)}) async-start(), calls=%async_computation.8 | async-start | bytes 3604480 | tf_op jit(solution)/shard_map/all_gather | solution.py:386
  108.5 36.2 %collective-permute-start.6 = (bf16[2,512,256]{2,1,0:T(8,128)(2,1)S(1)}, bf16[2,512,256]{2,1,0:T(8,128)(2,1)S(1)}, u32[]{:S(2)}, u32[]{:S(2)}) collective-permute-start(bf16[2,512,256]{2,1,0:T(8,128)(2,1)S(1)} %slice.472), channel_id=1, source_target_pairs={{0,16},{8,24},{16,0},{24,8},{1,17},{9,25},{17,1},{25,9},{2,18},{10... | collective-permute-start | bytes 1572872 | tf_op jit(solution)/shard_map/ppermute | solution.py:31
  110.8 33.9 %collective-permute-start.7 = (bf16[2,512,256]{2,1,0:T(8,128)(2,1)S(1)}, bf16[2,512,256]{2,1,0:T(8,128)(2,1)S(1)}, u32[]{:S(2)}, u32[]{:S(2)}) collective-permute-start(bf16[2,512,256]{2,1,0:T(8,128)(2,1)S(1)} %slice.473), channel_id=1, source_target_pairs={{0,8},{8,0},{16,24},{24,16},{1,9},{9,1},{17,25},{25,17},{2,10},{10... | collective-permute-start | bytes 1572872 | tf_op jit(solution)/shard_map/ppermute | solution.py:31
  131.0 45.6 %collective-permute-start.11 = (bf16[2,256,512]{2,1,0:T(8,128)(2,1)S(1)}, bf16[2,256,512]{2,1,0:T(8,128)(2,1)S(1)}, u32[]{:S(2)}, u32[]{:S(2)}) collective-permute-start(bf16[2,256,512]{2,1,0:T(8,128)(2,1)S(1)} %slice.481), channel_id=1, source_target_pairs={{0,16},{8,24},{16,0},{24,8},{1,17},{9,25},{17,1},{25,9},{2,18},{10... | collective-permute-start | bytes 1572872 | tf_op jit(solution)/shard_map/ppermute | solution.py:31
  134.0 42.6 %collective-permute-start.12 = (bf16[2,256,512]{2,1,0:T(8,128)(2,1)}, bf16[2,256,512]{2,1,0:T(8,128)(2,1)S(1)}, u32[]{:S(2)}, u32[]{:S(2)}) collective-permute-start(bf16[2,256,512]{2,1,0:T(8,128)(2,1)} %slice.482), channel_id=1, source_target_pairs={{0,8},{8,0},{16,24},{24,16},{1,9},{9,1},{17,25},{25,17},{2,10},{10... | collective-permute-start | bytes 1572872 | tf_op jit(solution)/shard_map/ppermute | solution.py:31
  199.3 36.4 %collective-permute-start.14 = (bf16[256,2048]{0,1:T(8,128)(2,1)}, bf16[256,2048]{0,1:T(8,128)(2,1)S(1)}, u32[]{:S(2)}, u32[]{:S(2)}) collective-permute-start(bf16[256,2048]{0,1:T(8,128)(2,1)} %get-tuple-element.107), channel_id=1, source_target_pairs={{0,8},{8,0},{16,24},{24,16},{1,9},{9,1},{17,25},{25,17},{2,10},{10... | collective-permute-start | bytes 3145736 | tf_op jit(solution)/shard_map/ppermute | solution.py:31
  200.6 49.0 %collective-permute-start.15 = (bf16[256,2048]{0,1:T(8,128)(2,1)}, bf16[256,2048]{0,1:T(8,128)(2,1)}, u32[]{:S(2)}, u32[]{:S(2)}) collective-permute-start(bf16[256,2048]{0,1:T(8,128)(2,1)} %get-tuple-element.107), channel_id=1, source_target_pairs={{0,16},{8,24},{16,0},{24,8},{1,17},{9,25},{17,1},{25,9},{2,18},{10... | collective-permute-start | bytes 3145736 | tf_op jit(solution)/shard_map/ppermute | solution.py:31
  218.4 324.5 %reduce-scatter.12.cloned.1.call-start = ((), (), s32[]{:S(2)}) async-start(), calls=%async_computation.12 | async-start | bytes 3604480 | tf_op jit(solution)/shard_map/reduce_scatter | solution.py:454
  219.8 44.3 %collective-permute-start.21 = (bf16[128,2048]{1,0:T(8,128)(2,1)S(1)}, bf16[128,2048]{1,0:T(8,128)(2,1)S(1)}, u32[]{:S(2)}, u32[]{:S(2)}) collective-permute-start(bf16[128,2048]{1,0:T(8,128)(2,1)S(1)} %slice.487), channel_id=1, source_target_pairs={{0,8},{8,0},{16,24},{24,16},{1,9},{9,1},{17,25},{25,17},{2,10},{10... | collective-permute-start | bytes 1572872 | tf_op jit(solution)/shard_map/ppermute | solution.py:31
  264.1 38.7 %collective-permute-start.25 = (bf16[1024,2048]{0,1:T(8,128)(2,1)}, bf16[1024,2048]{0,1:T(8,128)(2,1)}, u32[]{:S(2)}, u32[]{:S(2)}) collective-permute-start(bf16[1024,2048]{0,1:T(8,128)(2,1)} %constant_dynamic-update-slice_fusion), channel_id=1, source_target_pairs={{0,1},{1,0},{2,3},{3,2},{4,5},{5,4},{6,7},{7,6},{8,9},{9,8},{10,11... | collective-permute-start | bytes 12582920 | tf_op jit(solution)/shard_map/ppermute | solution.py:26
  264.9 44.4 %collective-permute-start.26 = (bf16[1024,2048]{1,0:T(8,128)(2,1)}, bf16[1024,2048]{1,0:T(8,128)(2,1)}, u32[]{:S(2)}, u32[]{:S(2)}) collective-permute-start(bf16[1024,2048]{1,0:T(8,128)(2,1)} %constant_dynamic-update-slice_fusion.5.g_ref), channel_id=1, source_target_pairs={{0,1},{1,0},{2,3},{3,2},{4,5},{5,4},{6,7},{7,6},{8,9},{9,8},{10,11... | collective-permute-start | bytes 12582920 | tf_op jit(solution)/shard_map/ppermute | solution.py:26
  348.6 197.6 %reduce-scatter.10.cloned.1.call-start = ((), (), s32[]{:S(2)}) async-start(), calls=%async_computation.11 | async-start | bytes 3604480 | tf_op jit(solution)/shard_map/reduce_scatter | solution.py:454
  368.6 215.3 %reduce-scatter.14.cloned.1.call-start = ((), (), s32[]{:S(2)}) async-start(), calls=%async_computation.13 | async-start | bytes 3604480 | tf_op jit(solution)/shard_map/reduce_scatter | solution.py:454
  386.6 59.1 %collective-permute-start.27 = (bf16[1024,2048]{0,1:T(8,128)(2,1)}, bf16[1024,2048]{0,1:T(8,128)(2,1)}, u32[]{:S(2)}, u32[]{:S(2)}) collective-permute-start(bf16[1024,2048]{0,1:T(8,128)(2,1)} %convolution_convert_fusion), channel_id=1, source_target_pairs={{0,1},{1,0},{2,3},{3,2},{4,5},{5,4},{6,7},{7,6},{8,9},{9,8},{10,11... | collective-permute-start | bytes 12582920 | tf_op jit(solution)/shard_map/ppermute | solution.py:26
  456.3 67.9 %collective-permute-start.30 = (bf16[2,128,2048]{1,2,0:T(8,128)(2,1)}, bf16[2,128,2048]{1,2,0:T(8,128)(2,1)}, u32[]{:S(2)}, u32[]{:S(2)}) collective-permute-start(bf16[2,128,2048]{1,2,0:T(8,128)(2,1)} %pad_maximum_fusion.4), channel_id=1, source_target_pairs={{0,16},{8,24},{16,0},{24,8},{1,17},{9,25},{17,1},{25,9},{2,18},{10... | collective-permute-start | bytes 3145736 | tf_op jit(solution)/shard_map/ppermute | solution.py:31
  458.5 68.5 %collective-permute-start.28 = (bf16[2,128,2048]{1,2,0:T(8,128)(2,1)}, bf16[2,128,2048]{1,2,0:T(8,128)(2,1)}, u32[]{:S(2)}, u32[]{:S(2)}) collective-permute-start(bf16[2,128,2048]{1,2,0:T(8,128)(2,1)} %pad_maximum_fusion.3), channel_id=1, source_target_pairs={{0,8},{8,0},{16,24},{24,16},{1,9},{9,1},{17,25},{25,17},{2,10},{10... | collective-permute-start | bytes 3145736 | tf_op jit(solution)/shard_map/ppermute | solution.py:31
  522.0 48.3 %collective-permute-start.39 = (bf16[256,128]{1,0:T(8,128)(2,1)S(1)}, bf16[256,128]{1,0:T(8,128)(2,1)S(1)}, u32[]{:S(2)}, u32[]{:S(2)}) collective-permute-start(bf16[256,128]{1,0:T(8,128)(2,1)S(1)} %get-tuple-element.185), channel_id=1, source_target_pairs={{0,1},{1,0},{2,3},{3,2},{4,5},{5,4},{6,7},{7,6},{8,9},{9,8},{10,11... | collective-permute-start | bytes 196616 | tf_op jit(solution)/shard_map/ppermute | solution.py:26
  539.5 129.1 %reduce-scatter.8.cloned.1.call-start = ((), (), s32[]{:S(2)}) async-start(), calls=%async_computation.10 | async-start | bytes 1310720 | tf_op jit(solution)/shard_map/reduce_scatter | solution.py:472
  559.3 44.6 %collective-permute-start.50 = (bf16[2,2,512,256]{3,2,1,0:T(8,128)(2,1)}, bf16[2,2,512,256]{3,2,1,0:T(8,128)(2,1)}, u32[]{:S(2)}, u32[]{:S(2)}) collective-permute-start(bf16[2,2,512,256]{3,2,1,0:T(8,128)(2,1)} %pad_maximum_fusion.8), channel_id=1, source_target_pairs={{0,16},{8,24},{16,0},{24,8},{1,17},{9,25},{17,1},{25,9},{2,18},{10... | collective-permute-start | bytes 3145736 | tf_op jit(solution)/shard_map/ppermute | solution.py:31
  561.5 44.5 %collective-permute-start.48 = (bf16[2,2,512,256]{3,2,1,0:T(8,128)(2,1)}, bf16[2,2,512,256]{3,2,1,0:T(8,128)(2,1)}, u32[]{:S(2)}, u32[]{:S(2)}) collective-permute-start(bf16[2,2,512,256]{3,2,1,0:T(8,128)(2,1)} %pad_maximum_fusion.7), channel_id=1, source_target_pairs={{0,8},{8,0},{16,24},{24,16},{1,9},{9,1},{17,25},{25,17},{2,10},{10... | collective-permute-start | bytes 3145736 | tf_op jit(solution)/shard_map/ppermute | solution.py:31
  576.5 37.9 %collective-permute-start.40 = (f32[256,2048]{0,1:T(8,128)}, f32[256,2048]{0,1:T(8,128)}, u32[]{:S(2)}, u32[]{:S(2)}) collective-permute-start(f32[256,2048]{0,1:T(8,128)} %slice.520), channel_id=1, source_target_pairs={{0,1},{1,0},{2,3},{3,2},{4,5},{5,4},{6,7},{7,6},{8,9},{9,8},{10,11... | collective-permute-start | bytes 6291464 | tf_op jit(solution)/shard_map/ppermute | solution.py:26
  595.5 47.2 %collective-permute-start.29 = (bf16[128,2048]{0,1:T(8,128)(2,1)}, bf16[128,2048]{0,1:T(8,128)(2,1)}, u32[]{:S(2)}, u32[]{:S(2)}) collective-permute-start(bf16[128,2048]{0,1:T(8,128)(2,1)} %get-tuple-element.120), channel_id=1, source_target_pairs={{0,16},{8,24},{16,0},{24,8},{1,17},{9,25},{17,1},{25,9},{2,18},{10... | collective-permute-start | bytes 1572872 | tf_op jit(solution)/shard_map/ppermute | solution.py:31
  597.5 47.0 %collective-permute-start.31 = (bf16[128,2048]{0,1:T(8,128)(2,1)}, bf16[128,2048]{0,1:T(8,128)(2,1)}, u32[]{:S(2)}, u32[]{:S(2)}) collective-permute-start(bf16[128,2048]{0,1:T(8,128)(2,1)} %get-tuple-element.121), channel_id=1, source_target_pairs={{0,8},{8,0},{16,24},{24,16},{1,9},{9,1},{17,25},{25,17},{2,10},{10... | collective-permute-start | bytes 1572872 | tf_op jit(solution)/shard_map/ppermute | solution.py:31
  602.3 74.6 %reduce-scatter.6.cloned.1.call-start = ((), (), s32[]{:S(2)}) async-start(), calls=%async_computation.9 | async-start | bytes 1310720 | tf_op jit(solution)/shard_map/reduce_scatter | solution.py:473
  603.9 44.8 %collective-permute-start.56 = (bf16[3,176,512]{2,1,0:T(8,128)(2,1)}, bf16[3,176,512]{2,1,0:T(8,128)(2,1)}, u32[]{:S(2)}, u32[]{:S(2)}) collective-permute-start(bf16[3,176,512]{2,1,0:T(8,128)(2,1)} %get-tuple-element.151), channel_id=1, source_target_pairs={{0,8},{8,0},{16,24},{24,16},{1,9},{9,1},{17,25},{25,17},{2,10},{10... | collective-permute-start | bytes 1622024 | tf_op jit(solution)/shard_map/ppermute | solution.py:31
  624.0 35.0 %collective-permute-start.57 = (bf16[3,176,512]{2,1,0:T(8,128)(2,1)}, bf16[3,176,512]{2,1,0:T(8,128)(2,1)}, u32[]{:S(2)}, u32[]{:S(2)}) collective-permute-start(bf16[3,176,512]{2,1,0:T(8,128)(2,1)} %get-tuple-element.150), channel_id=1, source_target_pairs={{0,16},{8,24},{16,0},{24,8},{1,17},{9,25},{17,1},{25,9},{2,18},{10... | collective-permute-start | bytes 1622024 | tf_op jit(solution)/shard_map/ppermute | solution.py:31
  (108 other events, 1498.2 us)
Sparse Core Ops, SparseCore 0:
  10.1 30.6 all-gather.13
  43.0 31.7 all-gather.15
  76.3 59.6 all-gather.7
  137.4 57.7 all-gather.9
  218.6 58.6 all-gather.11
  348.7 54.9 reduce-scatter.11
  406.1 56.0 reduce-scatter.9
  464.5 56.0 reduce-scatter.13
  602.5 26.7 reduce-scatter.7
  638.1 26.6 reduce-scatter.5

commit v2 on v1

v2 whole, which is shorter than its diff:
```python
import functools

import jax
import jax.numpy as jnp
from jax import lax
from jax.experimental import pallas as pl
from jax.experimental.pallas import tpu as pltpu
from jax.sharding import Mesh, PartitionSpec as P

norm_eps = 1e-05
rope_base = 10000.0
masked_score = -1e30
log2_e = 1.4426950408889634
f32 = jnp.float32
bf = jnp.bfloat16
vmem_bytes = 60 * 1024 * 1024


def mm(left, right, left_dim=1, right_dim=0):
    return lax.dot_general(
        left, right, (((left_dim,), (right_dim,)), ((), ())), preferred_element_type=f32
    )


def core_swap(a):
    return lax.ppermute(a, "core", [(0, 1), (1, 0)])


def axis_swap(a, axis, k):
    return lax.ppermute(a, axis, [(i, i ^ k) for i in range(lax.axis_size(axis))])


def row_swap(a, k):
    return axis_swap(a, "row", k)


def after(values, earlier):
    return lax.optimization_barrier((values, earlier))[0]


def gather_rows(a, cover=()):
    n = lax.axis_size("row")
    if n != 4:
        return [a] + [row_swap(a, k) for k in range(1, n)], cover
    along_x, along_y, cover = lax.optimization_barrier((row_swap(a, 1), row_swap(a, 2), cover))
    half = a.shape[0] // 2
    corner = jnp.concatenate([row_swap(along_x[:half], 2), row_swap(along_y[half:], 1)], axis=0)
    return [a, along_x, along_y, corner], cover


def exchange_rows(parts):
    return [parts[0]] + [row_swap(parts[k], k) for k in range(1, len(parts))]


def part_sum(parts, k, cut=slice(None)):
    return sum(term[cut].astype(f32) for term in parts[k])


def halves_of(parts):
    half = parts[0][0].shape[0] // 2
    return slice(0, half), slice(half, None)


def row_messages(parts):
    n = len(parts)
    if n != 4:
        return tuple(part_sum(parts, k).astype(bf) for k in range(1, n))
    low, high = halves_of(parts)
    return (
        jnp.stack([part_sum(parts, 1, low), part_sum(parts, 3, low)]).astype(bf),
        jnp.stack([part_sum(parts, 2, high), part_sum(parts, 3, high)]).astype(bf),
    )


def swap_first(messages):
    return tuple(row_swap(message, k) for k, message in enumerate(messages, 1))


def row_turned(parts, received):
    if len(parts) != 4:
        return ()
    low, high = halves_of(parts)
    from_x, from_y = received
    return (
        (part_sum(parts, 1, high) + from_y[1].astype(f32)).astype(bf),
        (part_sum(parts, 2, low) + from_x[1].astype(f32)).astype(bf),
    )


def row_total(parts, received, last):
    if len(parts) != 4:
        return part_sum(parts, 0) + sum(a.astype(f32) for a in received)
    from_x, from_y = received
    last_x, last_y = last
    first = jnp.concatenate([from_x[0], from_y[0]]).astype(f32)
    return part_sum(parts, 0) + first + jnp.concatenate([last_y, last_x]).astype(f32)


def by_row(pieces, axis=0):
    r = lax.axis_index("row")
    size = pieces[0].shape[axis]
    shape = list(pieces[0].shape)
    shape[axis] = size * len(pieces)
    whole = jnp.zeros(shape, pieces[0].dtype)
    for k, piece in enumerate(pieces):
        whole = lax.dynamic_update_slice_in_dim(whole, piece, (r ^ k) * size, axis)
    return whole


def reduce_z(a):
    n, z = lax.axis_size("z"), lax.axis_index("z")
    size = a.shape[0] // n
    a = jnp.concatenate([lax.dynamic_slice_in_dim(a, (z ^ k) * size, size, 0) for k in range(n)])
    k = n // 2
    while k >= 1:
        half = a.shape[0] // 2
        a = a[:half] + axis_swap(a[half:].astype(bf), "z", k).astype(f32)
        k //= 2
    return a


def row_parts(total, rows):
    return [total[k * rows : (k + 1) * rows] for k in range(total.shape[0] // rows)]


def call(kernel, out_shape, name, flops, bytes_moved, transcendentals=0, **more):
    return pl.pallas_call(
        kernel,
        out_shape=out_shape,
        compiler_params=pltpu.CompilerParams(vmem_limit_bytes=vmem_bytes),
        cost_estimate=pl.CostEstimate(
            flops=flops, bytes_accessed=bytes_moved, transcendentals=transcendentals
        ),
        name=name,
        **more,
    )


def span_of(k, width):
    return pl.ds(pl.multiple_of((lax.axis_index("row") ^ k) * width, 128), width)


def scale_of(values):
    return lax.rsqrt(jnp.mean(values * values, axis=-1, keepdims=True) + norm_eps)


def norm_one_kernel(a_ref, b_ref, gain_ref, out_ref):
    own = a_ref.shape[0]
    for i, ref in enumerate((a_ref, b_ref)):
        values = ref[...].astype(f32)
        out_ref[i * own : (i + 1) * own, :] = (values * scale_of(values) * gain_ref[...]).astype(bf)


def norm_one(a, b, gain):
    own, dim = a.shape
    return call(
        norm_one_kernel, jax.ShapeDtypeStruct((2 * own, dim), bf), "norm_one", 8 * own * dim, 8 * own * dim
    )(a, b, gain)


def norm_two_kernel(x_ref, a_ref, b_ref, gain_ref, middle_ref, out_ref):
    middle = x_ref[...].astype(f32) + (a_ref[...] + b_ref[...])
    middle_ref[...] = middle
    out_ref[...] = (middle * scale_of(middle) * gain_ref[...]).astype(bf)


def norm_two(x, a, b, gain):
    own, dim = x.shape
    return call(
        norm_two_kernel,
        [jax.ShapeDtypeStruct((own, dim), f32), jax.ShapeDtypeStruct((own, dim), bf)],
        "norm_two",
        8 * own * dim,
        16 * own * dim,
    )(x, a, b, gain)


def through_norm(values, gain, grad):
    factor = scale_of(values)
    weighted = grad * gain
    inner = jnp.mean(weighted * values, axis=-1, keepdims=True)
    gain_part = jnp.sum(grad * values * factor, axis=0, keepdims=True)
    return factor * weighted - values * (factor * factor * factor * inner), gain_part


def norm_two_back_kernel(middle_ref, grad_ref, out_grad_ref, gain_ref, sum_ref, low_ref, gain_grad_ref):
    part, gain_grad_ref[...] = through_norm(middle_ref[...], gain_ref[...], grad_ref[...])
    total = out_grad_ref[...].astype(f32) + part
    sum_ref[...] = total
    low_ref[...] = total.astype(bf)


def norm_two_back(middle, grad, out_grad, gain):
    own, dim = middle.shape
    return call(
        norm_two_back_kernel,
        [
            jax.ShapeDtypeStruct((own, dim), f32),
            jax.ShapeDtypeStruct((own, dim), bf),
            jax.ShapeDtypeStruct((1, dim), f32),
        ],
        "norm_two_back",
        16 * own * dim,
        16 * own * dim,
    )(middle, grad, out_grad, gain)


def norm_one_back_kernel(x_ref, a_ref, b_ref, gain_ref, sum_ref, out_ref, gain_grad_ref):
    part, gain_grad_ref[...] = through_norm(
        x_ref[...].astype(f32), gain_ref[...], a_ref[...] + b_ref[...]
    )
    out_ref[...] = sum_ref[...] + part


def norm_one_back(x, a, b, gain, middle_grad):
    own, dim = x.shape
    return call(
        norm_one_back_kernel,
        [jax.ShapeDtypeStruct((own, dim), f32), jax.ShapeDtypeStruct((1, dim), f32)],
        "norm_one_back",
        16 * own * dim,
        18 * own * dim,
    )(x, a, b, gain, middle_grad)


def attend_kernel(scale, tile, rows, *refs):
    n_ref, wq_refs = refs[0], refs[1 : 1 + rows]
    k_ref, vt_ref, bias_ref, cos_ref, sin_ref = refs[1 + rows : 6 + rows]
    q_ref, qt_ref, mix_ref, lse_ref, qt_all = refs[6 + rows :]
    _, width, block = wq_refs[0].shape
    head = k_ref.shape[1]
    half = head // 2
    tiles = n_ref.shape[0] // tile
    step = pl.program_id(1)

    @pl.when(step == 0)
    def _():
        q = mm(n_ref[:, span_of(0, width)], wq_refs[0][0])
        for k in range(1, rows):
            q = q + mm(n_ref[:, span_of(k, width)], wq_refs[k][0])
        qt = q.T
        for h in range(block // head):
            first = qt[h * head : h * head + half]
            second = qt[h * head + half : (h + 1) * head]
            turned = jnp.concatenate(
                [
                    first * cos_ref[...] - second * sin_ref[...],
                    second * cos_ref[...] + first * sin_ref[...],
                ],
                axis=0,
            )
            qt_ref[h * head : (h + 1) * head, :] = turned.astype(bf)
            q_ref[:, h * head : (h + 1) * head] = turned.T.astype(bf)
            for i in range(tiles):
                qt_all[h * tiles + i] = turned[:, i * tile : (i + 1) * tile].astype(bf)

    for i in range(tiles):
        for h in range(block // head):

            @pl.when(step == h * tiles + i)
            def _(h=h, i=i):
                cols = slice(i * tile, (i + 1) * tile)
                spots = slice(h * head, (h + 1) * head)
                scores = mm(k_ref[...], qt_all[h * tiles + i]) * (scale * log2_e) + bias_ref[:, cols]
                highest = jnp.max(scores, axis=0, keepdims=True)
                weights = jnp.exp2(scores - highest)
                total = jnp.sum(weights, axis=0, keepdims=True)
                mixed = mm(vt_ref[...], weights.astype(bf)) / total
                mix_ref[cols, spots] = mixed.T.astype(bf)
                lse_ref[0, h : h + 1, cols] = highest + jnp.log2(total)


def full_spec(a):
    return pl.BlockSpec(a.shape, lambda *_: (0,) * a.ndim)


def attend(normed, wq, keys, values_t, bias, cosine_t, sine_t, tile):
    rows = len(wq)
    blocks, width, block = wq[0].shape
    tokens, dim = normed.shape
    head = keys.shape[1]
    heads = block // head
    small = (keys, values_t, bias, cosine_t, sine_t)
    return call(
        functools.partial(attend_kernel, head**-0.5, tile, rows),
        [
            jax.ShapeDtypeStruct((tokens, blocks * block), bf),
            jax.ShapeDtypeStruct((blocks * block, tokens), bf),
            jax.ShapeDtypeStruct((tokens, blocks * block), bf),
            jax.ShapeDtypeStruct((blocks, heads, tokens), f32),
        ],
        "attend",
        2 * tokens * blocks * block * (dim + 2 * keys.shape[0]),
        16 << 20,
        tokens * blocks * heads * keys.shape[0],
        grid=(blocks, heads * (tokens // tile)),
        in_specs=[full_spec(normed)]
        + [pl.BlockSpec((1, width, block), lambda z, j: (z, 0, 0))] * rows
        + [full_spec(a) for a in small],
        out_specs=[
            pl.BlockSpec((tokens, block), lambda z, j: (0, z)),
            pl.BlockSpec((block, tokens), lambda z, j: (z, 0)),
            pl.BlockSpec((tokens, block), lambda z, j: (0, z)),
            pl.BlockSpec((1, heads, tokens), lambda z, j: (z, 0, 0)),
        ],
        scratch_shapes=[pltpu.VMEM((heads * (tokens // tile), head, tile), bf)],
    )(normed, *wq, *small)


def out_kernel(own, rows, m_ref, *refs):
    wo_refs, own_ref, other_ref = refs[:rows], refs[rows], refs[rows + 1]
    _, width, block = wo_refs[0].shape
    z = pl.program_id(0)
    for k in range(rows):
        part = mm(m_ref[...], wo_refs[k][0], 1, 1)
        for ref, rest in ((own_ref, part[:own]), (other_ref, part[own:])):
            span = span_of(k, width)

            @pl.when(z == 0)
            def _():
                ref[:, span] = rest

            @pl.when(z != 0)
            def _():
                ref[:, span] += rest


def out_project(mixed, wo, own):
    rows = len(wo)
    blocks, width, block = wo[0].shape
    tokens = mixed.shape[0]
    out = jax.ShapeDtypeStruct((own, rows * width), f32)
    return call(
        functools.partial(out_kernel, own, rows),
        [out, out],
        "out_project",
        2 * tokens * blocks * block * rows * width,
        10 << 20,
        grid=(blocks,),
        in_specs=[pl.BlockSpec((tokens, block), lambda z: (0, z))]
        + [pl.BlockSpec((1, width, block), lambda z: (z, 0, 0))] * rows,
        out_specs=[pl.BlockSpec((own, rows * width), lambda z: (0, 0))] * 2,
    )(mixed, *wo)


def attend_back_kernel(scale, tile, rows, *refs):
    ml_ref, wo_refs = refs[0], refs[1 : 1 + rows]
    (k_ref, kt_ref, v_ref, bias_ref, cos_ref, sin_ref, q_ref, qt_ref, lse_ref) = refs[1 + rows : 10 + rows]
    dq_ref, dk_ref, dv_ref, do_all, dot_all = refs[10 + rows :]
    _, width, block = wo_refs[0].shape
    head = k_ref.shape[1]
    half = head // 2
    tiles = ml_ref.shape[0] // tile
    heads = block // head
    step = pl.program_id(1)

    @pl.when((pl.program_id(0) == 0) & (step == 0))
    def _():
        dk_ref[...] = jnp.zeros_like(dk_ref)
        dv_ref[...] = jnp.zeros_like(dv_ref)

    @pl.when(step == 0)
    def _():
        grad = mm(ml_ref[:, span_of(0, width)], wo_refs[0][0])
        for k in range(1, rows):
            grad = grad + mm(ml_ref[:, span_of(k, width)], wo_refs[k][0])
        do_all[...] = grad.astype(bf)
        dot_all[...] = grad.T.astype(bf)

    for i in range(tiles):
        for h in range(heads):

            @pl.when(step == h * tiles + i)
            def _(h=h, i=i):
                cols = slice(i * tile, (i + 1) * tile)
                spots = slice(h * head, (h + 1) * head)
                scores = mm(k_ref[...], qt_ref[spots, cols]) * (scale * log2_e) + bias_ref[:, cols]
                soft = jnp.exp2(scores - lse_ref[0, h : h + 1, cols])
                prob_grad = mm(v_ref[...], dot_all[spots, cols])
                row_dot = jnp.sum(soft * prob_grad, axis=0, keepdims=True)
                score_grad = (soft * (prob_grad - row_dot)).astype(bf)
                dv_ref[...] += mm(soft.astype(bf), do_all[cols, spots])
                dk_ref[...] += mm(score_grad, q_ref[cols, spots]) * scale
                dqt = mm(kt_ref[...], score_grad) * scale
                first, second = dqt[:half], dqt[half:]
                cosine, sine = cos_ref[:, cols], sin_ref[:, cols]
                turned = jnp.concatenate(
                    [first * cosine + second * sine, second * cosine - first * sine], axis=0
                )
                dq_ref[cols, spots] = turned.T.astype(bf)


def attend_back(middle_low, wo, keys, keys_t, values, bias, cosine_t, sine_t, q, qt, lse, tile):
    rows = len(wo)
    blocks, width, block = wo[0].shape
    tokens, dim = middle_low.shape
    keys_in, head = keys.shape
    heads = block // head
    small = (keys, keys_t, values, bias, cosine_t, sine_t)
    return call(
        functools.partial(attend_back_kernel, head**-0.5, tile, rows),
        [
            jax.ShapeDtypeStruct((tokens, blocks * block), bf),
            jax.ShapeDtypeStruct((keys_in, head), f32),
            jax.ShapeDtypeStruct((keys_in, head), f32),
        ],
        "attend_back",
        2 * tokens * blocks * block * (dim + 5 * keys_in),
        32 << 20,
        tokens * blocks * heads * keys_in,
        grid=(blocks, heads * (tokens // tile)),
        in_specs=[full_spec(middle_low)]
        + [pl.BlockSpec((1, width, block), lambda z, j: (z, 0, 0))] * rows
        + [full_spec(a) for a in small]
        + [
            pl.BlockSpec((tokens, block), lambda z, j: (0, z)),
            pl.BlockSpec((block, tokens), lambda z, j: (z, 0)),
            pl.BlockSpec((1, heads, tokens), lambda z, j: (z, 0, 0)),
        ],
        out_specs=[
            pl.BlockSpec((tokens, block), lambda z, j: (0, z)),
            pl.BlockSpec((keys_in, head), lambda z, j: (0, 0)),
            pl.BlockSpec((keys_in, head), lambda z, j: (0, 0)),
        ],
        scratch_shapes=[pltpu.VMEM((tokens, block), bf), pltpu.VMEM((block, tokens), bf)],
    )(middle_low, *wo, *small, q, qt, lse)


def outer_kernel(rows, width, a_ref, b_ref, out_ref):
    for k in range(rows):
        out_ref[k, 0] = mm(a_ref[:, span_of(k, width)], b_ref[...], 0, 0).astype(bf)


def outer(a, b, rows, blocks):
    tokens, dim = a.shape
    width, block = dim // rows, b.shape[1] // blocks
    return call(
        functools.partial(outer_kernel, rows, width),
        jax.ShapeDtypeStruct((rows, blocks, width, block), bf),
        "outer",
        2 * tokens * dim * b.shape[1],
        8 << 20,
        grid=(blocks,),
        in_specs=[full_spec(a), pl.BlockSpec((tokens, block), lambda z: (0, z))],
        out_specs=pl.BlockSpec((rows, 1, width, block), lambda z: (0, z, 0, 0)),
    )(a, b)


def query_back_kernel(own, rows, n_ref, dq_ref, *refs):
    wq_refs, dw_ref, own_ref, other_ref = refs[:rows], refs[rows], refs[rows + 1], refs[rows + 2]
    _, width, block = wq_refs[0].shape
    z = pl.program_id(0)
    for k in range(rows):
        span = span_of(k, width)
        dw_ref[k, 0] = mm(n_ref[:, span], dq_ref[...], 0, 0).astype(bf)
        part = mm(dq_ref[...], wq_refs[k][0], 1, 1)
        for ref, rest in ((own_ref, part[:own]), (other_ref, part[own:])):

            @pl.when(z == 0)
            def _():
                ref[:, span] = rest

            @pl.when(z != 0)
            def _():
                ref[:, span] += rest


def query_back(normed, dq, wq, own):
    rows = len(wq)
    blocks, width, block = wq[0].shape
    tokens, dim = normed.shape
    out = jax.ShapeDtypeStruct((own, dim), f32)
    return call(
        functools.partial(query_back_kernel, own, rows),
        [jax.ShapeDtypeStruct((rows, blocks, width, block), bf), out, out],
        "query_back",
        4 * tokens * dim * blocks * block,
        16 << 20,
        grid=(blocks,),
        in_specs=[full_spec(normed), pl.BlockSpec((tokens, block), lambda z: (0, z))]
        + [pl.BlockSpec((1, width, block), lambda z: (z, 0, 0))] * rows,
        out_specs=[pl.BlockSpec((rows, 1, width, block), lambda z: (0, z, 0, 0))]
        + [pl.BlockSpec((own, dim), lambda z: (0, 0))] * 2,
    )(normed, dq, *wq)


def fetch(source, target, sems, which):
    copies = []
    units = source.shape[2]
    for z in range(source.shape[0]):
        for slot, i in enumerate(which):
            copies.append(
                pltpu.make_async_copy(
                    source.at[z, i], target.at[slot, pl.ds(z * units, units)], sems.at[z, slot]
                )
            )
    for copy in copies:
        copy.start()
    for copy in copies:
        copy.wait()


def mlp_kernel(added, x_ref, g_ref, w_ref, *refs):
    prior_ref = refs[0] if added else None
    hid_ref, gg_ref, ug_ref, dx_ref, w_all, sems = refs[1:] if added else refs

    @pl.when(pl.program_id(0) == 0)
    def _():
        fetch(w_ref, w_all, sems, (0, 1, 2))

    gate = mm(x_ref[...], w_all[0], 1, 1)
    up = mm(x_ref[...], w_all[1], 1, 1)
    hidden_grad = mm(g_ref[...], w_all[2], 1, 1)
    sig = jax.nn.sigmoid(gate)
    silu = gate * sig
    hid_ref[...] = (silu * up).astype(bf)
    gate_grad = (hidden_grad * up * sig * (1.0 + gate * (1.0 - sig))).astype(bf)
    up_grad = (hidden_grad * silu).astype(bf)
    gg_ref[...] = gate_grad
    ug_ref[...] = up_grad
    dx = mm(gate_grad, w_all[0]) + mm(up_grad, w_all[1])
    if added:
        dx = dx + prior_ref[...].astype(f32)
    dx_ref[...] = dx.astype(bf)


def mlp(x, g, weights, prior, tile):
    tokens, dim = x.shape
    parts, _, few, _ = weights.shape
    units = parts * few
    rows_of = lambda width: pl.BlockSpec((tile, width), lambda t: (t, 0))
    added = prior is not None
    return call(
        functools.partial(mlp_kernel, added),
        [jax.ShapeDtypeStruct((tokens, units), bf)] * 3 + [jax.ShapeDtypeStruct((tokens, dim), bf)],
        "mlp",
        10 * tokens * units * dim,
        24 << 20,
        tokens * units,
        grid=(tokens // tile,),
        in_specs=[rows_of(dim), rows_of(dim), pl.BlockSpec(memory_space=pl.ANY)]
        + [rows_of(dim)] * added,
        out_specs=[rows_of(units), rows_of(units), rows_of(units), rows_of(dim)],
        scratch_shapes=[
            pltpu.VMEM((3, units, dim), bf),
            pltpu.SemaphoreType.DMA((parts, 3)),
        ],
    )(x, g, weights, *([prior] if added else []))


def mlp_weights_kernel(added, tiles, *refs):
    first, second, w_ref = refs[:5], refs[5:10], refs[10]
    priors = refs[11:13] if added else (None, None)
    dw_ref, out_a, out_b, total, down, sems = refs[13:] if added else refs[11:]
    step = pl.program_id(0)

    @pl.when(step == 0)
    def _():
        fetch(w_ref, down, sems, (2,))
        total[...] = jnp.zeros_like(total)

    def body(terms, prior, out):
        x_ref, g_ref, hid_ref, gg_ref, ug_ref = terms
        total[0] += mm(gg_ref[...], x_ref[...], 0, 0)
        total[1] += mm(ug_ref[...], x_ref[...], 0, 0)
        total[2] += mm(hid_ref[...], g_ref[...], 0, 0)
        part = mm(hid_ref[...], down[0])
        if prior is not None:
            part = part + prior[...].astype(f32)
        out[...] = part.astype(bf)

    @pl.when(step < tiles)
    def _():
        body(first, priors[0], out_a)

    @pl.when(step >= tiles)
    def _():
        body(second, priors[1], out_b)

    @pl.when(step == 2 * tiles - 1)
    def _():
        few = dw_ref.shape[2]
        for z in range(dw_ref.shape[0]):
            for i in range(3):
                dw_ref[z, i] = total[i, z * few : (z + 1) * few, :].astype(bf)


def mlp_weights(first, second, weights, priors, tile):
    tokens, dim = first[0].shape
    parts, _, few, _ = weights.shape
    units = parts * few
    tiles = tokens // tile
    added = priors is not None
    early = lambda width: pl.BlockSpec((tile, width), lambda t: (jnp.minimum(t, tiles - 1), 0))
    late = lambda width: pl.BlockSpec((tile, width), lambda t: (jnp.maximum(t - tiles, 0), 0))
    rows = jax.ShapeDtypeStruct((tokens, dim), bf)
    return call(
        functools.partial(mlp_weights_kernel, added, tiles),
        [jax.ShapeDtypeStruct((parts, 3, few, dim), bf), rows, rows],
        "mlp_weights",
        16 * tokens * units * dim,
        32 << 20,
        grid=(2 * tiles,),
        in_specs=[early(dim), early(dim), early(units), early(units), early(units)]
        + [late(dim), late(dim), late(units), late(units), late(units)]
        + [pl.BlockSpec(memory_space=pl.ANY)]
        + [early(dim), late(dim)] * added,
        out_specs=[
            pl.BlockSpec((parts, 3, few, dim), lambda t: (0, 0, 0, 0)),
            early(dim),
            late(dim),
        ],
        scratch_shapes=[
            pltpu.VMEM((3, units, dim), f32),
            pltpu.VMEM((1, units, dim), bf),
            pltpu.SemaphoreType.DMA((parts, 1)),
        ],
    )(*first, *second, weights, *(priors if added else []))


def rotate(values, cosine, sine):
    half = values.shape[1] // 2
    first, second = values[:, :half], values[:, half:]
    return jnp.concatenate([first * cosine - second * sine, second * cosine + first * sine], axis=1)


def local(layer_input, out_grad, kv_grad, lengths, token_deal, attn_gain, query_weight, key_weight,
          value_weight, out_weight, mlp_gain, gate_weight, up_weight, down_weight):
    r, z, c = lax.axis_index("row"), lax.axis_index("z"), lax.axis_index("core")
    n_rows, n_z = lax.axis_size("row"), lax.axis_size("z")
    own, dim = layer_input.shape
    width, block = query_weight.shape
    head = key_weight.shape[1]
    units = gate_weight.shape[1]
    piece = units // n_rows
    pick = lambda a, i, axis=0: lax.dynamic_index_in_dim(a, i, axis, keepdims=False)
    first_core = c == 0

    wq_z = lax.all_gather(query_weight.astype(bf), "z", axis=0)
    mlp_own = jnp.stack(
        [gate_weight.astype(bf).T, up_weight.astype(bf).T, down_weight.astype(bf)]
    ).reshape(3, n_rows, piece, width)
    mlp_parts = exchange_rows([pick(mlp_own, r ^ k, 1) for k in range(n_rows)])
    gains = jnp.concatenate([attn_gain, mlp_gain]).astype(bf).reshape(-1, head)
    small = jnp.concatenate([jnp.where(first_core, key_weight, value_weight).astype(bf), gains])
    small = by_row(exchange_rows([small] * n_rows)).reshape(n_rows, -1, head)
    kv_w = small[:, :width].reshape(dim, head)
    gains = small[:, width:].reshape(n_rows, 2, width).astype(f32)
    gain_one, gain_two = gains[:, 0].reshape(1, dim), gains[:, 1].reshape(1, dim)

    chip = 2 * own
    deal = token_deal[0]
    ends = jnp.cumsum(lengths[0])

    def start_of(initial):
        return jnp.sum(jnp.where(ends[None, :] <= initial[:, None], lengths[0][None, :], 0), axis=1)

    swap_halves = lambda a: jnp.where(first_core, a, jnp.roll(a, own, axis=0))
    initial = swap_halves(lax.dynamic_slice_in_dim(deal, z * chip, chip, 0))
    start = start_of(initial)
    angles = (initial - start).astype(f32)[:, None] * (
        rope_base ** (-jnp.arange(head // 2, dtype=f32) / (head // 2))
    )
    cosine, sine = jnp.cos(angles), jnp.sin(angles)
    bias = jnp.where(
        (deal[:, None] >= start[None, :]) & (deal[:, None] <= initial[None, :]),
        0.0,
        masked_score,
    ).astype(f32)
    kv_cosine, kv_sine = jnp.where(first_core, cosine, 1.0), jnp.where(first_core, sine, 0.0)

    normed = norm_one(layer_input, core_swap(layer_input), gain_one)
    kv_own = swap_halves(rotate(mm(normed, kv_w), kv_cosine, kv_sine).astype(bf))
    mlp_parts = after(mlp_parts, kv_own)
    kv_mine = lax.all_gather(after(kv_own, wq_z), "z", axis=0, tiled=True)
    kv_other = core_swap(kv_mine)
    keys = jnp.where(first_core, kv_mine, kv_other)
    values = jnp.where(first_core, kv_other, kv_mine)
    mine = lambda a: lax.dynamic_slice_in_dim(a, z * chip + c * own, own, 0)
    shared_own = jnp.concatenate([mine(keys), mine(values)], axis=1)

    wo_z = lax.all_gather(after(out_weight.astype(bf).T, kv_mine), "z", axis=0)
    wq_z = after(wq_z, mlp_parts)
    mlp_parts = by_row(mlp_parts, axis=2)
    late_units = piece * 4 // 11
    cuts = [slice(0, piece - late_units), slice(piece - late_units, piece)]
    few = [cut.stop - cut.start for cut in cuts]
    mlp_w = []
    for cut in cuts:
        earlier = mlp_w[-1] if mlp_w else wo_z
        mlp_w.append(lax.all_gather(after(mlp_parts[:, cut], earlier), "z", axis=0))
    aligned = all(n % 16 == 0 for n in few)
    if not aligned:
        mlp_w = [
            w.transpose(1, 0, 2, 3).reshape(1, 3, n_z * n, dim) for w, n in zip(mlp_w, few)
        ]

    wq, _ = gather_rows(wq_z)
    wo_z = after(wo_z, wq)
    tile = own
    attended = attend(normed, wq, keys, values.T, bias, cosine.T, sine.T, tile)
    wo, (q, qt, mixed, lse) = gather_rows(wo_z, attended)
    att_own, att_other = out_project(mixed, wo, own)
    middle, normed_two = norm_two(layer_input, att_own, core_swap(att_other), gain_two)

    grads_own, normed_two = gather_rows(after(out_grad, wo[3]), normed_two)
    grads_own = jnp.concatenate(grads_own)
    grads_other = core_swap(grads_own)
    rows_own = jnp.concatenate(gather_rows(normed_two)[0])
    rows_other = core_swap(rows_own)
    early_b = mlp(rows_other, grads_other, mlp_w[0], None, own)
    early_a = mlp(rows_own, grads_own, mlp_w[0], None, own)
    early_sum, out_b, out_a = mlp_weights(
        (rows_other, grads_other, *early_b[:3]), (rows_own, grads_own, *early_a[:3]), mlp_w[0], None, own
    )
    rows_other, early_sum = lax.optimization_barrier((rows_other, early_sum))
    late_b = mlp(rows_other, grads_other, mlp_w[1], early_b[3], own)
    late_a = mlp(rows_own, grads_own, mlp_w[1], early_a[3], own)

    def plane_parts(mine, others):
        received = core_swap(others)
        return [list(pair) for pair in zip(row_parts(mine, own), row_parts(received, own))]

    grad_parts = plane_parts(late_a[3], late_b[3])
    grad_messages = row_messages(grad_parts)
    late, grad_messages = lax.optimization_barrier(((*late_b[:3], *late_a[:3]), grad_messages))
    late_sum, out_b, out_a = mlp_weights(
        (rows_other, grads_other, *late[:3]), (rows_own, grads_own, *late[3:]), mlp_w[1], (out_b, out_a), own
    )
    received, (late_sum, out_b, out_a) = lax.optimization_barrier(
        (swap_first(grad_messages), (late_sum, out_b, out_a))
    )
    grad_last = swap_first(row_turned(grad_parts, received))
    normed_two_grad = row_total(grad_parts, received, grad_last)
    out_parts = plane_parts(out_a, out_b)
    out_messages = row_messages(out_parts)
    sums = []
    for total, n in zip((early_sum, late_sum), few):
        if not aligned:
            total = total.reshape(3, n_z, n, dim).transpose(1, 0, 2, 3)
        if sums:
            total = after(total, sums[-1])
        sums.append(lax.psum_scatter(total, "z", scatter_dimension=0, tiled=False))

    normed_two_grad, out_messages = lax.optimization_barrier((normed_two_grad, out_messages))
    middle_grad, low_own, gain_two_grad = norm_two_back(middle, normed_two_grad, out_grad, gain_two)
    middle_low = jnp.concatenate([low_own, core_swap(low_own)])

    dwo = outer(middle_low, mixed, n_rows, n_z)
    dwo_parts = [[dwo[k]] for k in range(n_rows)]
    dwo_messages, middle_low = lax.optimization_barrier((row_messages(dwo_parts), middle_low))
    attended = attend_back(
        middle_low, wo, keys, keys.T, values, bias, cosine.T, sine.T, q, qt, lse, tile
    )
    out_received, dwo_received, (dq, dk, dv) = lax.optimization_barrier(
        (swap_first(out_messages), swap_first(dwo_messages), attended)
    )
    kv_to = jnp.where(first_core, dv, dk).astype(bf)
    kv_to, dq = lax.optimization_barrier((kv_to, dq))
    kv_sum = jnp.where(first_core, dk, dv) + core_swap(kv_to).astype(f32)
    kv_sum = reduce_z(kv_sum)
    dwq, dn_own, dn_other = query_back(normed, dq, wq, own)
    dwo_last, dwq = lax.optimization_barrier((swap_first(row_turned(dwo_parts, dwo_received)), dwq))
    dwo_rows = row_total(dwo_parts, dwo_received, dwo_last).astype(bf)
    dwq_parts = [[dwq[k]] for k in range(n_rows)]
    dwq_received, dwo_rows = lax.optimization_barrier((swap_first(row_messages(dwq_parts)), dwo_rows))
    dwq_last = swap_first(row_turned(dwq_parts, dwq_received))
    dwq_rows = row_total(dwq_parts, dwq_received, dwq_last).astype(bf)
    out_turned = after(row_turned(out_parts, out_received), dwq_received)
    output_rows = middle + row_total(out_parts, out_received, swap_first(out_turned))
    sum_z = lambda a: lax.psum_scatter(a.reshape(-1, block), "z", scatter_dimension=0, tiled=True)
    dwo_sum = sum_z(after(dwo_rows, sums[-1]))
    dwq_sum = sum_z(after(dwq_rows, dwo_sum)).astype(f32)
    dwo_sum = dwo_sum.astype(f32)

    kv_left, kv_right = kv_grad[:, :head], kv_grad[:, head:]
    kv_given = jnp.concatenate(
        [
            jnp.where(first_core, kv_left, kv_right),
            core_swap(jnp.where(first_core, kv_right, kv_left)),
        ]
    ).astype(f32)
    kv_low = rotate(swap_halves(kv_sum) + kv_given, kv_cosine, -kv_sine).astype(bf)
    kv_wgrad = mm(normed, kv_low, 0, 0)
    dn_kv = mm(kv_low, kv_w, 1, 1)
    input_grad, gain_one_grad = norm_one_back(
        layer_input, dn_own + dn_kv[:own], core_swap(dn_other + dn_kv[own:]), gain_one, middle_grad
    )

    mlp_sums = after(jnp.concatenate(sums, axis=1), dwq_rows).reshape(3, piece, n_rows, width)
    mlp_grads = by_row(exchange_rows([pick(mlp_sums, r ^ k, 2) for k in range(n_rows)]), axis=1)
    mlp_grads = mlp_grads.astype(f32)

    gain_rows = jnp.stack(
        [gain_one_grad.reshape(n_rows, width), gain_two_grad.reshape(n_rows, width)], axis=1
    ).reshape(n_rows, -1, head)
    small = jnp.concatenate([kv_wgrad.reshape(n_rows, width, head), gain_rows], axis=1)
    small = exchange_rows([pick(small, r ^ k) for k in range(n_rows)])
    small = functools.reduce(jnp.add, small)
    k = 1
    while k < n_z:
        small = small + axis_swap(small, "z", k)
        k *= 2
    small_other = core_swap(small)
    key_wgrad = jnp.where(first_core, small[:width], small_other[:width])
    value_wgrad = jnp.where(first_core, small_other[:width], small[:width])
    gain_sums = (small[width:] + small_other[width:]).reshape(2, width)
    return (
        output_rows.astype(bf),
        input_grad,
        shared_own,
        gain_sums[0],
        dwq_sum,
        key_wgrad,
        value_wgrad,
        dwo_sum.T,
        gain_sums[1],
        mlp_grads[0].T,
        mlp_grads[1].T,
        mlp_grads[2],
    )


def solution(mesh):
    n_rows, n_cols = mesh.shape["row"], mesh.shape["col"]
    split = Mesh(mesh.devices.reshape(n_rows, n_cols // 2, 2), ("row", "z", "core"))
    everywhere, col = ("row", "z", "core"), ("z", "core")
    in_specs = (
        P(everywhere, None),
        P(everywhere, None),
        P(everywhere, None),
        P("row", None),
        P("row", None),
        P("row"),
        P("row", col),
        P("row", None),
        P("row", None),
        P(col, "row"),
        P("row"),
        P("row", col),
        P("row", col),
        P(col, "row"),
    )
    out_specs = (
        P(everywhere, None),
        P(everywhere, None),
        P(everywhere, None),
        P("row"),
        P("row", col),
        P("row", None),
        P("row", None),
        P(col, "row"),
        P("row"),
        P("row", col),
        P("row", col),
        P(col, "row"),
    )
    return jax.shard_map(
        local, mesh=split, in_specs=in_specs, out_specs=out_specs, check_vma=False
    )
```

time: 717 us -> 655 us (0.914)
  Pallas kernels: 141 us -> 240 us
  other arithmetic: 123 us -> 58.5 us
  local copies, waits for them, and re-layouts: 146 us -> 83.6 us
  matrix products: 55.8 us -> 3.89 us
  waiting for transfers between devices: 145 us -> 173 us
    pallas_call x5 -> x15, Pallas kernels: 141 us -> 240 us  [the longest x4 67.9 us: mlp(): call(functools.partial(mlp_kernel, added), [jax.ShapeDtypeStruct((tokens,...]
    dot_general x11 -> x3, matrix products: 55.8 us -> 3.89 us  [mm(): lax.dot_general(left, right, (((left_dim,), (right_dim,)), ((), ())), pre...]
    pallas_call x5 -> x0, local copies, waits for them, and re-layouts: 24.1 us -> none  [the longest x2 12.8 us: mlp(): pl.pallas_call(mlp_kernel, grid=(tokens // tile,), in_specs=[rows_of(dim)...]
    add x11 -> x9, other arithmetic: 26 us -> 8.02 us  [the longest x1 3.64 us: row_total(): part_sum(parts, 0) + first + jnp.concatenate([last_y, last_x]).astype(f32)]
    reduce_scatter x5 -> x4, waiting for transfers between devices: 0.03 us -> 17.7 us  [the longest x2 17.6 us: local(): sums.append(lax.psum_scatter(total, 'z', scatter_dimension=0, tiled=False))]
    convert_element_type x19 -> x9, other arithmetic: 39.2 us -> 21.5 us  [the longest x4 9.87 us: row_turned(): (part_sum(parts, 2, low) + from_x[1].astype(f32)).astype(bf)]
    another operation x6 -> x3, local copies, waits for them, and re-layouts: 15.1 us -> 2.41 us  [the longest x2 2.36 us: row_messages(): jnp.stack([part_sum(parts, 2, high), part_sum(parts, 3, high)]).astype(bf)]
    another operation x16 -> x11, other arithmetic: 22.2 us -> 10 us  [the longest x4 4.93 us: row_messages(): jnp.stack([part_sum(parts, 2, high), part_sum(parts, 3, high)]).astype(bf)]
  transfers between devices with their start and end apart: 70 -> 68, of which waited for: 25 -> 28; matrix products, arithmetic and copies ran while one was open for 42% -> 21% of each run, Pallas kernels for 16% -> 35%
where the time goes in v2:
time: 655 us; the launch traced here: 647 us
  Pallas kernels  240 us (37%)
  waiting for transfers between devices  173 us (26%)
  local copies, waits for them, and re-layouts  83.6 us (13%)
  other arithmetic  58.5 us (9%)
  starting transfers between devices  56.6 us (9%)
  blocking collectives  16.2 us (2%)
  between operations  15.4 us (2%)
    ppermute x48, waiting for transfers between devices, axis_swap(): lax.ppermute(a, axis, [(i, i ^ k) for i in range(lax.axis_size(axis))])  142 us
    pallas_call x4, Pallas kernels, mlp(): call(functools.partial(mlp_kernel, added), [jax.ShapeDtypeStruct((tokens,...  67.9 us
    ppermute x48, starting transfers between devices, axis_swap(): lax.ppermute(a, axis, [(i, i ^ k) for i in range(lax.axis_size(axis))])  54.5 us
    pallas_call x2, Pallas kernels, mlp_weights(): call(functools.partial(mlp_weights_kernel, added, tiles), [jax.ShapeDtype...  48.4 us
    pallas_call x1, Pallas kernels, attend_back(): call(functools.partial(attend_back_kernel, head ** (-0.5), tile, rows), [...  41.2 us
    pallas_call x1, Pallas kernels, attend(): call(functools.partial(attend_kernel, head ** (-0.5), tile, rows), [jax.S...  31.7 us
    unnamed x76, local copies, waits for them, and re-layouts  23.2 us
    reduce_scatter x2, waiting for transfers between devices, local(): sums.append(lax.psum_scatter(total, 'z', scatter_dimension=0, tiled=False))  17.6 us
  transfers between devices with their start and end apart: 68, of which 28 were waited for; matrix products, arithmetic and copies ran while one was open for 21% of the time, Pallas kernels for 35%

profile of v2, /device:TPU:0, one launch (start us, length us, event | category | flops | bytes accessed | tf_op | source)
XLA Modules:
  0.0 647.4 jit_solution(12560003042093840041)
XLA Ops:
  37.7 8.9 %collective-permute-done.5 = bf16[3,176,512]{2,1,0:T(8,128)(2,1)} collective-permute-done((bf16[3,176,512]{2,1,0:T(8,128)(2,1)}, bf16[3,176,512]{2,1,0:T(8,128)(2,1)}, u32[]{:S(2)}, u32[]{:S(2)}) %collective-permute-start.5) | collective-permute-done | bytes 540704 | tf_op jit(solution)/shard_map/ppermute | solution.py:30
  50.5 16.2 %all_gather.29 = bf16[2048,128]{1,0:T(8,128)(2,1)} all-gather(bf16[512,128]{1,0:T(8,128)(2,1)S(1)} %maximum_select_fusion.1), channel_id=1, replica_groups=mesh['row'=4,'z'=4,'core'=2] {'z'}, dimensions={0}, use_global_device_ids=true | all-gather | bytes 655360 | tf_op jit(solution)/shard_map/all_gather | solution.py:675
  84.4 10.6 %all-gather.11.cloned.1.call-done = bf16[2048,256]{0,1:T(8,128)(2,1)} async-done(((bf16[512,256]{0,1:T(8,128)(2,1)}), bf16[2048,256]{0,1:T(8,128)(2,1)}) %all-gather.11.cloned.1.call-update) | async-done | bytes 1048592 | tf_op jit(solution)/shard_map/all_gather | solution.py:682
  107.3 31.7 %attend.1 = (bf16[512,1024]{1,0:T(8,128)(2,1)}, bf16[1024,512]{1,0:T(8,128)(2,1)}, bf16[512,1024]{1,0:T(8,128)(2,1)}, f32[4,2,512]{2,1,0:T(2,128)}) custom-call(bf16[512,2048]{1,0:T(8,128)(2,1)} %norm_one.1.refs_0_.n_ref, bf16[4,512,256]{2,1,0:T(8,128)(2,1)} %bitcast.198, bf16[4,512,256]{2,1,0:T(8,128)(2,1)} %collective-permute-done.7.refs_2_.refs_1_, ...), custom_call_target="tpu_custom_call" | custom-call | flops 6442450944 | bytes 16777216 | tf_op jit(solution)/shard_map/attend/pallas_call | solution.py:284
  141.7 10.6 %collective-permute-done.14 = bf16[2,512,256]{2,1,0:T(8,128)(2,1)S(1)} collective-permute-done((bf16[2,512,256]{2,1,0:T(8,128)(2,1)S(1)}, bf16[2,512,256]{2,1,0:T(8,128)(2,1)S(1)}, u32[]{:S(2)}, u32[]{:S(2)}) %collective-permute-start.14) | collective-permute-done | bytes 524320 | tf_op jit(solution)/shard_map/ppermute | solution.py:30
  154.3 10.1 %out_project.1 = (f32[256,2048]{1,0:T(8,128)}, f32[256,2048]{1,0:T(8,128)}) custom-call(bf16[512,1024]{1,0:T(8,128)(2,1)} %get-tuple-element.133.m_ref.b_ref, bf16[4,512,256]{2,1,0:T(8,128)(2,1)} %bitcast.173, bf16[4,512,256]{2,1,0:T(8,128)(2,1)} %collective-permute-done.11.refs_1_.refs_2_, bf16[4,512,256]{2,1,0:T(8,128)(2,1)} %collective-permute-done.12.refs_2_.refs_3_, ...), custom_call_target="tpu_custom_call" | custom-call | flops 2147483648 | bytes 10485760 | tf_op jit(solution)/shard_map/out_project/pallas_call | solution.py:333
  169.0 4.7 norm_two.1
  173.7 16.7 %collective-permute-done.18 = bf16[256,2048]{1,0:T(8,128)(2,1)} collective-permute-done((bf16[256,2048]{1,0:T(8,128)(2,1)}, bf16[256,2048]{1,0:T(8,128)(2,1)}, u32[]{:S(2)}, u32[]{:S(2)}) %collective-permute-start.18) | collective-permute-done | bytes 1048608 | tf_op jit(solution)/shard_map/ppermute | solution.py:30
  206.2 21.5 %collective-permute-done.24 = bf16[128,2048]{1,0:T(8,128)(2,1)S(1)} collective-permute-done((bf16[128,2048]{1,0:T(8,128)(2,1)S(1)}, bf16[128,2048]{1,0:T(8,128)(2,1)S(1)}, u32[]{:S(2)}, u32[]{:S(2)}) %collective-permute-start.24) | collective-permute-done | bytes 524320 | tf_op jit(solution)/shard_map/ppermute | solution.py:30
  232.5 8.4 %collective-permute-done.21 = bf16[128,2048]{1,0:T(8,128)(2,1)S(1)} collective-permute-done((bf16[128,2048]{1,0:T(8,128)(2,1)S(1)}, bf16[128,2048]{1,0:T(8,128)(2,1)S(1)}, u32[]{:S(2)}, u32[]{:S(2)}) %collective-permute-start.21) | collective-permute-done | bytes 524320 | tf_op jit(solution)/shard_map/ppermute | solution.py:30
  246.6 17.8 %mlp.5 = (bf16[1024,448]{1,0:T(8,128)(2,1)}, bf16[1024,448]{1,0:T(8,128)(2,1)}, bf16[1024,448]{1,0:T(8,128)(2,1)}, bf16[1024,2048]{1,0:T(8,128)(2,1)}) custom-call(bf16[1024,2048]{1,0:T(8,128)(2,1)} %constant_dynamic-update-slice_fusion.4.x_ref.refs_5_, bf16[1024,2048]{1,0:T(8,128)(2,1)} %constant_dynamic-update-slice_fusion.9.g_ref.refs_6_, ...), custom_call_target="tpu_custom_call" | custom-call | flops 9395240960 | bytes 25165824 | tf_op jit(solution)/shard_map/mlp/pallas_call | solution.py:533
  264.4 17.8 %mlp.4 = (bf16[1024,448]{1,0:T(8,128)(2,1)}, bf16[1024,448]{1,0:T(8,128)(2,1)}, bf16[1024,448]{1,0:T(8,128)(2,1)}, bf16[1024,2048]{1,0:T(8,128)(2,1)}) custom-call(bf16[1024,2048]{1,0:T(8,128)(2,1)} %collective-permute-done.23.x_ref.refs_0_, bf16[1024,2048]{1,0:T(8,128)(2,1)} %collective-permute-done.26.g_ref.refs_1_, bf16[4,3,112,2048]{3,2,1,0:T(8,128)(2,1)} %bitcast.191), custom_call_target="tpu_custom_call" | custom-call | flops 9395240960 | bytes 25165824 | tf_op jit(solution)/shard_map/mlp/pallas_call | solution.py:533
  282.2 26.9 %mlp_weights.2 = (bf16[4,3,112,2048]{3,2,1,0:T(8,128)(2,1)}, bf16[1024,2048]{1,0:T(8,128)(2,1)}, bf16[1024,2048]{1,0:T(8,128)(2,1)}) custom-call(bf16[1024,2048]{1,0:T(8,128)(2,1)} %collective-permute-done.23.x_ref.refs_0_, bf16[1024,2048]{1,0:T(8,128)(2,1)} %collective-permute-done.26.g_ref.refs_1_, bf16[1024,448]{1,0:T(8,128)(2,1)} %get-tuple-element.147.refs_2_, ...), custom_call_target="tpu_custom_call" | custom-call | flops 15032385536 | bytes 33554432 | tf_op jit(solution)/shard_map/mlp_weights/pallas_call | solution.py:597
  309.0 16.0 %mlp.6 = (bf16[1024,256]{1,0:T(8,128)(2,1)}, bf16[1024,256]{1,0:T(8,128)(2,1)}, bf16[1024,256]{1,0:T(8,128)(2,1)}, bf16[1024,2048]{1,0:T(8,128)(2,1)}) custom-call(bf16[1024,2048]{1,0:T(8,128)(2,1)} %collective-permute-done.23.x_ref.refs_0_, bf16[1024,2048]{1,0:T(8,128)(2,1)} %collective-permute-done.26.g_ref.refs_1_, bf16[4,3,64,2048]{3,2,1,0:T(8,128)(2,1)} %bitcast.193, ...), custom_call_target="tpu_custom_call" | custom-call | flops 5368709120 | bytes 25165824 | tf_op jit(solution)/shard_map/mlp/pallas_call | solution.py:533
  325.7 16.4 %mlp.7 = (bf16[1024,256]{1,0:T(8,128)(2,1)}, bf16[1024,256]{1,0:T(8,128)(2,1)}, bf16[1024,256]{1,0:T(8,128)(2,1)}, bf16[1024,2048]{1,0:T(8,128)(2,1)}) custom-call(bf16[1024,2048]{1,0:T(8,128)(2,1)} %constant_dynamic-update-slice_fusion.4.x_ref.refs_5_, bf16[1024,2048]{1,0:T(8,128)(2,1)} %constant_dynamic-update-slice_fusion.9.g_ref.refs_6_, ...), custom_call_target="tpu_custom_call" | custom-call | flops 5368709120 | bytes 25165824 | tf_op jit(solution)/shard_map/mlp/pallas_call | solution.py:533
  347.5 21.6 %mlp_weights.3 = (bf16[4,3,64,2048]{3,2,1,0:T(8,128)(2,1)}, bf16[1024,2048]{1,0:T(8,128)(2,1)}, bf16[1024,2048]{1,0:T(8,128)(2,1)}) custom-call(bf16[1024,2048]{1,0:T(8,128)(2,1)} %collective-permute-done.23.x_ref.refs_0_, bf16[1024,2048]{1,0:T(8,128)(2,1)} %collective-permute-done.26.g_ref.refs_1_, bf16[1024,256]{1,0:T(8,128)(2,1)} %get-tuple-element.168.refs_2_, ...), custom_call_target="tpu_custom_call" | custom-call | flops 8589934592 | bytes 33554432 | tf_op jit(solution)/shard_map/mlp_weights/pallas_call | solution.py:597
  378.4 9.7 %collective-permute-done.31 = bf16[128,2048]{1,0:T(8,128)(2,1)S(1)} collective-permute-done((bf16[128,2048]{1,0:T(8,128)(2,1)S(1)}, bf16[128,2048]{1,0:T(8,128)(2,1)S(1)}, u32[]{:S(2)}, u32[]{:S(2)}) %collective-permute-start.31) | collective-permute-done | bytes 524320 | tf_op jit(solution)/shard_map/ppermute | solution.py:30
  397.2 5.3 norm_two_back.1
  404.8 17.6 %reduce-scatter.5.cloned.1.call-done = bf16[1,3,112,2048]{3,2,1,0:T(8,128)(2,1)} async-done(((bf16[4,3,112,2048]{3,2,1,0:T(8,128)(2,1)}), bf16[1,3,112,2048]{3,2,1,0:T(8,128)(2,1)}) %reduce-scatter.5.cloned.1.call-update) | async-done | bytes 1376272 | tf_op jit(solution)/shard_map/reduce_scatter | solution.py:743
  428.9 6.6 %outer.1 = bf16[4,4,512,256]{3,2,1,0:T(8,128)(2,1)} custom-call(bf16[512,2048]{1,0:T(8,128)(2,1)} %constant_dynamic-update-slice_fusion.14.a_ref.refs_0_, bf16[512,1024]{1,0:T(8,128)(2,1)} %get-tuple-element.133.m_ref.b_ref), custom_call_target="tpu_custom_call" | custom-call | flops 2147483648 | bytes 8388608 | tf_op jit(solution)/shard_map/outer/pallas_call | solution.py:437
  441.3 41.2 %attend_back.1 = (bf16[512,1024]{1,0:T(8,128)(2,1)}, f32[2048,128]{1,0:T(8,128)}, f32[2048,128]{1,0:T(8,128)}) custom-call(bf16[512,2048]{1,0:T(8,128)(2,1)} %constant_dynamic-update-slice_fusion.14.a_ref.refs_0_, bf16[4,512,256]{2,1,0:T(8,128)(2,1)} %bitcast.174, bf16[4,512,256]{2,1,0:T(8,128)(2,1)} %collective-permute-done.11.refs_1_.refs_2_, ...), custom_call_target="tpu_custom_call" | custom-call | flops 12884901888 | bytes 33554432 | tf_op jit(solution)/shard_map/attend_back/pallas_call | solution.py:400
  490.3 13.9 %query_back.1 = (bf16[4,4,512,256]{3,2,1,0:T(8,128)(2,1)}, f32[256,2048]{1,0:T(8,128)}, f32[256,2048]{1,0:T(8,128)}) custom-call(bf16[512,2048]{1,0:T(8,128)(2,1)} %norm_one.1.refs_0_.n_ref, bf16[512,1024]{1,0:T(8,128)(2,1)} %get-tuple-element.203.dq_ref, bf16[4,512,256]{2,1,0:T(8,128)(2,1)} %bitcast.199, ...), custom_call_target="tpu_custom_call" | custom-call | flops 4294967296 | bytes 16777216 | tf_op jit(solution)/shard_map/query_back/pallas_call | solution.py:473
  516.0 11.7 %collective-permute-done.45 = bf16[1024,128]{1,0:T(8,128)(2,1)S(1)} collective-permute-done((bf16[1024,128]{1,0:T(8,128)(2,1)S(1)}, bf16[1024,128]{1,0:T(8,128)(2,1)S(1)}, u32[]{:S(2)}, u32[]{:S(2)}) %collective-permute-start.45) | collective-permute-done | bytes 262176 | tf_op jit(solution)/shard_map/ppermute | solution.py:30
  529.2 3.7 collective-permute-done.46
  542.3 10.3 %collective-permute-done.40 = bf16[2,2,512,256]{3,2,1,0:T(8,128)(2,1)S(1)} collective-permute-done((bf16[2,2,512,256]{3,2,1,0:T(8,128)(2,1)S(1)}, bf16[2,2,512,256]{3,2,1,0:T(8,128)(2,1)S(1)}, u32[]{:S(2)}, u32[]{:S(2)}) %collective-permute-start.40) | collective-permute-done | bytes 1048608 | tf_op jit(solution)/shard_map/ppermute | solution.py:30
  560.9 8.6 %collective-permute-done.55 = bf16[2,512,256]{2,1,0:T(8,128)(2,1)} collective-permute-done((bf16[2,512,256]{2,1,0:T(8,128)(2,1)}, bf16[2,512,256]{2,1,0:T(8,128)(2,1)}, u32[]{:S(2)}, u32[]{:S(2)}) %collective-permute-start.55) | collective-permute-done | bytes 524320 | tf_op jit(solution)/shard_map/ppermute | solution.py:30
  574.5 4.9 reshape.192
  579.5 6.2 norm_one_back.1
  590.0 6.0 constant_dynamic-slice_fusion.2
  604.3 4.1 add_convert_fusion
  614.5 6.0 collective-permute-done.58
  623.3 10.6 %collective-permute-done.53 = f32[520,128]{1,0:T(8,128)S(1)} collective-permute-done((f32[520,128]{1,0:T(8,128)S(1)}, f32[520,128]{1,0:T(8,128)S(1)}, u32[]{:S(2)}, u32[]{:S(2)}) %collective-permute-start.53) | collective-permute-done | bytes 266272 | tf_op jit(solution)/shard_map/ppermute | solution.py:30
  (327 shorter events, 209.6 us)
Async XLA Ops:
  7.2 39.7 %all-gather.9.cloned.1.call-start = ((), (), s32[]{:S(2)}) async-start(), calls=%async_computation.8 | async-start | bytes 1310720 | tf_op jit(solution)/shard_map/all_gather | solution.py:639
  16.9 78.2 %all-gather.11.cloned.1.call-start = ((), (), s32[]{:S(2)}) async-start(), calls=%async_computation.9 | async-start | bytes 1310720 | tf_op jit(solution)/shard_map/all_gather | solution.py:682
  46.9 25.1 %collective-permute-start.8 = (bf16[4,512,256]{2,1,0:T(8,128)(2,1)}, bf16[4,512,256]{2,1,0:T(8,128)(2,1)S(1)}, u32[]{:S(2)}, u32[]{:S(2)}) collective-permute-start(bf16[4,512,256]{2,1,0:T(8,128)(2,1)} %bitcast.196), channel_id=1, source_target_pairs={{0,16},{8,24},{16,0},{24,8},{1,17},{9,25},{17,1},{25,9},{2,18},{10... | collective-permute-start | bytes 3145736 | tf_op jit(solution)/shard_map/ppermute | solution.py:30
  48.3 25.2 %collective-permute-start.7 = (bf16[4,512,256]{2,1,0:T(8,128)(2,1)}, bf16[4,512,256]{2,1,0:T(8,128)(2,1)}, u32[]{:S(2)}, u32[]{:S(2)}) collective-permute-start(bf16[4,512,256]{2,1,0:T(8,128)(2,1)} %bitcast.197), channel_id=1, source_target_pairs={{0,8},{8,0},{16,24},{24,16},{1,9},{9,1},{17,25},{25,17},{2,10},{10... | collective-permute-start | bytes 3145736 | tf_op jit(solution)/shard_map/ppermute | solution.py:30
  66.8 179.6 %all-gather.13.cloned.1.call-start = ((), (), s32[]{:S(2)}) async-start(), calls=%async_computation.10 | async-start | bytes 6881280 | tf_op jit(solution)/shard_map/all_gather | solution.py:691
  101.1 37.9 %collective-permute-start.12 = (bf16[4,512,256]{2,1,0:T(8,128)(2,1)}, bf16[4,512,256]{2,1,0:T(8,128)(2,1)}, u32[]{:S(2)}, u32[]{:S(2)}) collective-permute-start(bf16[4,512,256]{2,1,0:T(8,128)(2,1)} %bitcast.171), channel_id=1, source_target_pairs={{0,16},{8,24},{16,0},{24,8},{1,17},{9,25},{17,1},{25,9},{2,18},{10... | collective-permute-start | bytes 3145736 | tf_op jit(solution)/shard_map/ppermute | solution.py:30
  102.5 36.5 %collective-permute-start.11 = (bf16[4,512,256]{2,1,0:T(8,128)(2,1)}, bf16[4,512,256]{2,1,0:T(8,128)(2,1)}, u32[]{:S(2)}, u32[]{:S(2)}) collective-permute-start(bf16[4,512,256]{2,1,0:T(8,128)(2,1)} %bitcast.172), channel_id=1, source_target_pairs={{0,8},{8,0},{16,24},{24,16},{1,9},{9,1},{17,25},{25,17},{2,10},{10... | collective-permute-start | bytes 3145736 | tf_op jit(solution)/shard_map/ppermute | solution.py:30
  104.0 205.1 %all-gather.15.cloned.1.call-start = ((), (), s32[]{:S(2)}) async-start(), calls=%async_computation.11 | async-start | bytes 3932160 | tf_op jit(solution)/shard_map/all_gather | solution.py:691
  164.5 25.9 %collective-permute-start.18 = (bf16[256,2048]{1,0:T(8,128)(2,1)}, bf16[256,2048]{1,0:T(8,128)(2,1)}, u32[]{:S(2)}, u32[]{:S(2)}) collective-permute-start(bf16[256,2048]{1,0:T(8,128)(2,1)} %out_grad_ref.1), channel_id=1, source_target_pairs={{0,16},{8,24},{16,0},{24,8},{1,17},{9,25},{17,1},{25,9},{2,18},{10... | collective-permute-start | bytes 3145736 | tf_op jit(solution)/shard_map/ppermute | solution.py:30
  166.2 25.6 %collective-permute-start.17 = (bf16[256,2048]{1,0:T(8,128)(2,1)}, bf16[256,2048]{1,0:T(8,128)(2,1)}, u32[]{:S(2)}, u32[]{:S(2)}) collective-permute-start(bf16[256,2048]{1,0:T(8,128)(2,1)} %out_grad_ref.1), channel_id=1, source_target_pairs={{0,8},{8,0},{16,24},{24,16},{1,9},{9,1},{17,25},{25,17},{2,10},{10... | collective-permute-start | bytes 3145736 | tf_op jit(solution)/shard_map/ppermute | solution.py:30
  191.8 36.7 %collective-permute-start.20 = (bf16[256,2048]{1,0:T(8,128)(2,1)}, bf16[256,2048]{1,0:T(8,128)(2,1)S(1)}, u32[]{:S(2)}, u32[]{:S(2)}) collective-permute-start(bf16[256,2048]{1,0:T(8,128)(2,1)} %get-tuple-element.141), channel_id=1, source_target_pairs={{0,16},{8,24},{16,0},{24,8},{1,17},{9,25},{17,1},{25,9},{2,18},{10... | collective-permute-start | bytes 3145736 | tf_op jit(solution)/shard_map/ppermute | solution.py:30
  192.1 36.4 %collective-permute-start.19 = (bf16[256,2048]{1,0:T(8,128)(2,1)}, bf16[256,2048]{1,0:T(8,128)(2,1)S(1)}, u32[]{:S(2)}, u32[]{:S(2)}) collective-permute-start(bf16[256,2048]{1,0:T(8,128)(2,1)} %get-tuple-element.141), channel_id=1, source_target_pairs={{0,8},{8,0},{16,24},{24,16},{1,9},{9,1},{17,25},{25,17},{2,10},{10... | collective-permute-start | bytes 3145736 | tf_op jit(solution)/shard_map/ppermute | solution.py:30
  195.9 31.8 %collective-permute-start.24 = (bf16[128,2048]{1,0:T(8,128)(2,1)S(1)}, bf16[128,2048]{1,0:T(8,128)(2,1)S(1)}, u32[]{:S(2)}, u32[]{:S(2)}) collective-permute-start(bf16[128,2048]{1,0:T(8,128)(2,1)S(1)} %slice.384), channel_id=1, source_target_pairs={{0,16},{8,24},{16,0},{24,8},{1,17},{9,25},{17,1},{25,9},{2,18},{10... | collective-permute-start | bytes 1572872 | tf_op jit(solution)/shard_map/ppermute | solution.py:30
  199.8 29.4 %collective-permute-start.25 = (bf16[128,2048]{1,0:T(8,128)(2,1)S(1)}, bf16[128,2048]{1,0:T(8,128)(2,1)S(1)}, u32[]{:S(2)}, u32[]{:S(2)}) collective-permute-start(bf16[128,2048]{1,0:T(8,128)(2,1)S(1)} %slice.385), channel_id=1, source_target_pairs={{0,8},{8,0},{16,24},{24,16},{1,9},{9,1},{17,25},{25,17},{2,10},{10... | collective-permute-start | bytes 1572872 | tf_op jit(solution)/shard_map/ppermute | solution.py:30
  230.0 34.3 %collective-permute-start.26 = (bf16[1024,2048]{1,0:T(8,128)(2,1)}, bf16[1024,2048]{1,0:T(8,128)(2,1)}, u32[]{:S(2)}, u32[]{:S(2)}) collective-permute-start(bf16[1024,2048]{1,0:T(8,128)(2,1)} %constant_dynamic-update-slice_fusion.9.g_ref.refs_6_), channel_id=1, source_target_pairs={{0,1},{1,0},{2,3},{3,2},{4,5},{5,4},{6,7},{7,6},{8,9},{9,8},{10,11... | collective-permute-start | bytes 12582920 | tf_op jit(solution)/shard_map/ppermute | solution.py:26
  246.3 176.1 %reduce-scatter.5.cloned.1.call-start = ((), (), s32[]{:S(2)}) async-start(), calls=%async_computation.4 | async-start | bytes 6881280 | tf_op jit(solution)/shard_map/reduce_scatter | solution.py:743
  325.7 230.5 %reduce-scatter.7.cloned.1.call-start = ((), (), s32[]{:S(2)}) async-start(), calls=%async_computation.5 | async-start | bytes 3932160 | tf_op jit(solution)/shard_map/reduce_scatter | solution.py:743
  345.4 25.3 %collective-permute-start.28 = (bf16[2,128,2048]{2,1,0:T(8,128)(2,1)S(1)}, bf16[2,128,2048]{2,1,0:T(8,128)(2,1)}, u32[]{:S(2)}, u32[]{:S(2)}) collective-permute-start(bf16[2,128,2048]{2,1,0:T(8,128)(2,1)S(1)} %pad_maximum_fusion.2), channel_id=1, source_target_pairs={{0,8},{8,0},{16,24},{24,16},{1,9},{9,1},{17,25},{25,17},{2,10},{10... | collective-permute-start | bytes 3145736 | tf_op jit(solution)/shard_map/ppermute | solution.py:30
  346.0 25.3 %collective-permute-start.29 = (bf16[2,128,2048]{2,1,0:T(8,128)(2,1)S(1)}, bf16[2,128,2048]{2,1,0:T(8,128)(2,1)}, u32[]{:S(2)}, u32[]{:S(2)}) collective-permute-start(bf16[2,128,2048]{2,1,0:T(8,128)(2,1)S(1)} %pad_maximum_fusion.3), channel_id=1, source_target_pairs={{0,16},{8,24},{16,0},{24,8},{1,17},{9,25},{17,1},{25,9},{2,18},{10... | collective-permute-start | bytes 3145736 | tf_op jit(solution)/shard_map/ppermute | solution.py:30
  402.5 130.4 %collective-permute-start.47 = (bf16[256,128]{1,0:T(8,128)(2,1)S(1)}, bf16[256,128]{1,0:T(8,128)(2,1)S(1)}, u32[]{:S(2)}, u32[]{:S(2)}) collective-permute-start(bf16[256,128]{1,0:T(8,128)(2,1)S(1)} %get-tuple-element.283), channel_id=1, source_target_pairs={{0,1},{1,0},{2,3},{3,2},{4,5},{5,4},{6,7},{7,6},{8,9},{9,8},{10,11... | collective-permute-start | bytes 196616 | tf_op jit(solution)/shard_map/ppermute | solution.py:26
  422.5 180.0 %reduce-scatter.9.cloned.1.call-start = ((), (), s32[]{:S(2)}) async-start(), calls=%async_computation.6 | async-start | bytes 1310720 | tf_op jit(solution)/shard_map/reduce_scatter | solution.py:771
  422.5 60.0 %collective-permute-start.33 = (bf16[2,128,2048]{2,1,0:T(8,128)(2,1)}, bf16[2,128,2048]{2,1,0:T(8,128)(2,1)}, u32[]{:S(2)}, u32[]{:S(2)}) collective-permute-start(bf16[2,128,2048]{2,1,0:T(8,128)(2,1)} %pad_maximum_fusion.4), channel_id=1, source_target_pairs={{0,8},{8,0},{16,24},{24,16},{1,9},{9,1},{17,25},{25,17},{2,10},{10... | collective-permute-start | bytes 3145736 | tf_op jit(solution)/shard_map/ppermute | solution.py:30
  424.0 58.5 %collective-permute-start.34 = (bf16[2,128,2048]{2,1,0:T(8,128)(2,1)}, bf16[2,128,2048]{2,1,0:T(8,128)(2,1)}, u32[]{:S(2)}, u32[]{:S(2)}) collective-permute-start(bf16[2,128,2048]{2,1,0:T(8,128)(2,1)} %pad_maximum_fusion.5), channel_id=1, source_target_pairs={{0,16},{8,24},{16,0},{24,8},{1,17},{9,25},{17,1},{25,9},{2,18},{10... | collective-permute-start | bytes 3145736 | tf_op jit(solution)/shard_map/ppermute | solution.py:30
  440.1 42.4 %collective-permute-start.36 = (bf16[2,2,512,256]{3,2,1,0:T(8,128)(2,1)}, bf16[2,2,512,256]{3,2,1,0:T(8,128)(2,1)}, u32[]{:S(2)}, u32[]{:S(2)}) collective-permute-start(bf16[2,2,512,256]{3,2,1,0:T(8,128)(2,1)} %pad_maximum_fusion.6), channel_id=1, source_target_pairs={{0,8},{8,0},{16,24},{24,16},{1,9},{9,1},{17,25},{25,17},{2,10},{10... | collective-permute-start | bytes 3145736 | tf_op jit(solution)/shard_map/ppermute | solution.py:30
  440.7 41.9 %collective-permute-start.37 = (bf16[2,2,512,256]{3,2,1,0:T(8,128)(2,1)}, bf16[2,2,512,256]{3,2,1,0:T(8,128)(2,1)}, u32[]{:S(2)}, u32[]{:S(2)}) collective-permute-start(bf16[2,2,512,256]{3,2,1,0:T(8,128)(2,1)} %stack.108), channel_id=1, source_target_pairs={{0,16},{8,24},{16,0},{24,8},{1,17},{9,25},{17,1},{25,9},{2,18},{10... | collective-permute-start | bytes 3145736 | tf_op jit(solution)/shard_map/ppermute | solution.py:30
  487.3 28.5 %collective-permute-start.39 = (bf16[2,512,256]{2,1,0:T(8,128)(2,1)}, bf16[2,512,256]{2,1,0:T(8,128)(2,1)}, u32[]{:S(2)}, u32[]{:S(2)}) collective-permute-start(bf16[2,512,256]{2,1,0:T(8,128)(2,1)} %get-tuple-element.249), channel_id=1, source_target_pairs={{0,16},{8,24},{16,0},{24,8},{1,17},{9,25},{17,1},{25,9},{2,18},{10... | collective-permute-start | bytes 1572872 | tf_op jit(solution)/shard_map/ppermute | solution.py:30
  488.8 27.0 %collective-permute-start.38 = (bf16[2,512,256]{2,1,0:T(8,128)(2,1)S(1)}, bf16[2,512,256]{2,1,0:T(8,128)(2,1)}, u32[]{:S(2)}, u32[]{:S(2)}) collective-permute-start(bf16[2,512,256]{2,1,0:T(8,128)(2,1)S(1)} %get-tuple-element.250), channel_id=1, source_target_pairs={{0,8},{8,0},{16,24},{24,16},{1,9},{9,1},{17,25},{25,17},{2,10},{10... | collective-permute-start | bytes 1572872 | tf_op jit(solution)/shard_map/ppermute | solution.py:30
  528.0 24.6 %collective-permute-start.40 = (bf16[2,2,512,256]{3,2,1,0:T(8,128)(2,1)S(1)}, bf16[2,2,512,256]{3,2,1,0:T(8,128)(2,1)S(1)}, u32[]{:S(2)}, u32[]{:S(2)}) collective-permute-start(bf16[2,2,512,256]{3,2,1,0:T(8,128)(2,1)S(1)} %pad_maximum_fusion.7), channel_id=1, source_target_pairs={{0,8},{8,0},{16,24},{24,16},{1,9},{9,1},{17,25},{25,17},{2,10},{10... | collective-permute-start | bytes 3145736 | tf_op jit(solution)/shard_map/ppermute | solution.py:30
  539.3 40.2 %collective-permute-start.48 = (f32[256,2048]{1,0:T(8,128)}, f32[256,2048]{1,0:T(8,128)}, u32[]{:S(2)}, u32[]{:S(2)}) collective-permute-start(f32[256,2048]{1,0:T(8,128)} %get-tuple-element.245), channel_id=1, source_target_pairs={{0,1},{1,0},{2,3},{3,2},{4,5},{5,4},{6,7},{7,6},{8,9},{9,8},{10,11... | collective-permute-start | bytes 6291464 | tf_op jit(solution)/shard_map/ppermute | solution.py:26
  557.6 80.9 %reduce-scatter.11.cloned.1.call-start = ((), (), s32[]{:S(2)}) async-start(), calls=%async_computation.7 | async-start | bytes 1310720 | tf_op jit(solution)/shard_map/reduce_scatter | solution.py:771
  558.5 44.0 %collective-permute-start.42 = (bf16[128,2048]{1,0:T(8,128)(2,1)}, bf16[128,2048]{1,0:T(8,128)(2,1)}, u32[]{:S(2)}, u32[]{:S(2)}) collective-permute-start(bf16[128,2048]{1,0:T(8,128)(2,1)} %get-tuple-element.210), channel_id=1, source_target_pairs={{0,16},{8,24},{16,0},{24,8},{1,17},{9,25},{17,1},{25,9},{2,18},{10... | collective-permute-start | bytes 1572872 | tf_op jit(solution)/shard_map/ppermute | solution.py:30
  560.2 44.2 %collective-permute-start.43 = (bf16[128,2048]{1,0:T(8,128)(2,1)}, bf16[128,2048]{1,0:T(8,128)(2,1)}, u32[]{:S(2)}, u32[]{:S(2)}) collective-permute-start(bf16[128,2048]{1,0:T(8,128)(2,1)} %get-tuple-element.211), channel_id=1, source_target_pairs={{0,8},{8,0},{16,24},{24,16},{1,9},{9,1},{17,25},{25,17},{2,10},{10... | collective-permute-start | bytes 1572872 | tf_op jit(solution)/shard_map/ppermute | solution.py:30
  (67 other events, 1048.2 us)
Sparse Core Ops, SparseCore 0:
  17.0 29.6 all-gather.8
  66.9 28.1 all-gather.10
  104.1 99.9 all-gather.12
  246.5 62.1 all-gather.14
  325.8 96.5 reduce-scatter.4
  424.6 60.8 reduce-scatter.6
  557.8 26.4 reduce-scatter.8
  602.6 30.3 reduce-scatter.10

commit v3 on v2

--- a/solution.py
+++ b/solution.py
@@ -38,14 +38,18 @@
     return lax.optimization_barrier((values, earlier))[0]
 
 
-def gather_rows(a, cover=()):
+def gather_first(a):
     n = lax.axis_size("row")
-    if n != 4:
-        return [a] + [row_swap(a, k) for k in range(1, n)], cover
-    along_x, along_y, cover = lax.optimization_barrier((row_swap(a, 1), row_swap(a, 2), cover))
+    return tuple(row_swap(a, k) for k in range(1, 3 if n == 4 else n))
+
+
+def gather_rest(a, first):
+    if lax.axis_size("row") != 4:
+        return [a, *first]
+    along_x, along_y = first
     half = a.shape[0] // 2
     corner = jnp.concatenate([row_swap(along_x[:half], 2), row_swap(along_y[half:], 1)], axis=0)
-    return [a, along_x, along_y, corner], cover
+    return [a, along_x, along_y, corner]
 
 
 def exchange_rows(parts):
@@ -107,16 +111,19 @@
     return whole
 
 
-def reduce_z(a):
+def reduce_z(a, cover):
     n, z = lax.axis_size("z"), lax.axis_index("z")
     size = a.shape[0] // n
     a = jnp.concatenate([lax.dynamic_slice_in_dim(a, (z ^ k) * size, size, 0) for k in range(n)])
     k = n // 2
     while k >= 1:
         half = a.shape[0] // 2
-        a = a[:half] + axis_swap(a[half:].astype(bf), "z", k).astype(f32)
+        received = axis_swap(a[half:].astype(bf), "z", k)
+        if k == n // 2:
+            received, cover = lax.optimization_barrier((received, cover))
+        a = a[:half] + received.astype(f32)
         k //= 2
-    return a
+    return a, cover
 
 
 def row_parts(total, rows):
@@ -672,15 +679,17 @@
     normed = norm_one(layer_input, core_swap(layer_input), gain_one)
     kv_own = swap_halves(rotate(mm(normed, kv_w), kv_cosine, kv_sine).astype(bf))
     mlp_parts = after(mlp_parts, kv_own)
-    kv_mine = lax.all_gather(after(kv_own, wq_z), "z", axis=0, tiled=True)
+    wo_low = after(out_weight.astype(bf).T, wq_z)
+    wo_z = lax.all_gather(wo_low, "z", axis=0)
+    kv_mine = lax.all_gather(after(kv_own, wo_low), "z", axis=0, tiled=True)
+    wq_z = after(wq_z, mlp_parts)
+    wq_first, kv_mine = lax.optimization_barrier((gather_first(wq_z), kv_mine))
     kv_other = core_swap(kv_mine)
     keys = jnp.where(first_core, kv_mine, kv_other)
     values = jnp.where(first_core, kv_other, kv_mine)
     mine = lambda a: lax.dynamic_slice_in_dim(a, z * chip + c * own, own, 0)
     shared_own = jnp.concatenate([mine(keys), mine(values)], axis=1)
 
-    wo_z = lax.all_gather(after(out_weight.astype(bf).T, kv_mine), "z", axis=0)
-    wq_z = after(wq_z, mlp_parts)
     mlp_parts = by_row(mlp_parts, axis=2)
     late_units = piece * 4 // 11
     cuts = [slice(0, piece - late_units), slice(piece - late_units, piece)]
@@ -695,18 +704,20 @@
             w.transpose(1, 0, 2, 3).reshape(1, 3, n_z * n, dim) for w, n in zip(mlp_w, few)
         ]
 
-    wq, _ = gather_rows(wq_z)
-    wo_z = after(wo_z, wq)
+    wq = gather_rest(wq_z, wq_first)
+    wo_z, grads = after((wo_z, out_grad), wq)
     tile = own
     attended = attend(normed, wq, keys, values.T, bias, cosine.T, sine.T, tile)
-    wo, (q, qt, mixed, lse) = gather_rows(wo_z, attended)
+    wo_first, grads_first, (q, qt, mixed, lse) = lax.optimization_barrier(
+        (gather_first(wo_z), gather_first(grads), attended)
+    )
+    wo = gather_rest(wo_z, wo_first)
     att_own, att_other = out_project(mixed, wo, own)
     middle, normed_two = norm_two(layer_input, att_own, core_swap(att_other), gain_two)
 
-    grads_own, normed_two = gather_rows(after(out_grad, wo[3]), normed_two)
-    grads_own = jnp.concatenate(grads_own)
+    grads_own = jnp.concatenate(gather_rest(grads, after(grads_first, wo)))
     grads_other = core_swap(grads_own)
-    rows_own = jnp.concatenate(gather_rows(normed_two)[0])
+    rows_own = jnp.concatenate(gather_rest(normed_two, gather_first(normed_two)))
     rows_other = core_swap(rows_own)
     early_b = mlp(rows_other, grads_other, mlp_w[0], None, own)
     early_a = mlp(rows_own, grads_own, mlp_w[0], None, own)
@@ -734,13 +745,14 @@
     normed_two_grad = row_total(grad_parts, received, grad_last)
     out_parts = plane_parts(out_a, out_b)
     out_messages = row_messages(out_parts)
-    sums = []
-    for total, n in zip((early_sum, late_sum), few):
+
+    def sum_mlp(total):
         if not aligned:
-            total = total.reshape(3, n_z, n, dim).transpose(1, 0, 2, 3)
-        if sums:
-            total = after(total, sums[-1])
-        sums.append(lax.psum_scatter(total, "z", scatter_dimension=0, tiled=False))
+            total = total.reshape(3, n_z, -1, dim).transpose(1, 0, 2, 3)
+        return lax.psum_scatter(total, "z", scatter_dimension=0, tiled=False)
+
+    early_sum = sum_mlp(early_sum)
+    late_sum = sum_mlp(after(late_sum, early_sum))
 
     normed_two_grad, out_messages = lax.optimization_barrier((normed_two_grad, out_messages))
     middle_grad, low_own, gain_two_grad = norm_two_back(middle, normed_two_grad, out_grad, gain_two)
@@ -758,18 +770,19 @@
     kv_to = jnp.where(first_core, dv, dk).astype(bf)
     kv_to, dq = lax.optimization_barrier((kv_to, dq))
     kv_sum = jnp.where(first_core, dk, dv) + core_swap(kv_to).astype(f32)
-    kv_sum = reduce_z(kv_sum)
-    dwq, dn_own, dn_other = query_back(normed, dq, wq, own)
+    dwq, *dn = query_back(normed, dq, wq, own)
+    kv_sum, (dn_own, dn_other) = reduce_z(kv_sum, dn)
     dwo_last, dwq = lax.optimization_barrier((swap_first(row_turned(dwo_parts, dwo_received)), dwq))
     dwo_rows = row_total(dwo_parts, dwo_received, dwo_last).astype(bf)
     dwq_parts = [[dwq[k]] for k in range(n_rows)]
-    dwq_received, dwo_rows = lax.optimization_barrier((swap_first(row_messages(dwq_parts)), dwo_rows))
-    dwq_last = swap_first(row_turned(dwq_parts, dwq_received))
+    dwq_received = swap_first(row_messages(dwq_parts))
+    dwq_turned = row_turned(dwq_parts, dwq_received)
+    dwq_last = swap_first(dwq_turned)
     dwq_rows = row_total(dwq_parts, dwq_received, dwq_last).astype(bf)
-    out_turned = after(row_turned(out_parts, out_received), dwq_received)
+    out_turned = after(row_turned(out_parts, out_received), dwq_turned)
     output_rows = middle + row_total(out_parts, out_received, swap_first(out_turned))
     sum_z = lambda a: lax.psum_scatter(a.reshape(-1, block), "z", scatter_dimension=0, tiled=True)
-    dwo_sum = sum_z(after(dwo_rows, sums[-1]))
+    dwo_sum = sum_z(after(dwo_rows, late_sum))
     dwq_sum = sum_z(after(dwq_rows, dwo_sum)).astype(f32)
     dwo_sum = dwo_sum.astype(f32)
 
@@ -787,8 +800,11 @@
         layer_input, dn_own + dn_kv[:own], core_swap(dn_other + dn_kv[own:]), gain_one, middle_grad
     )
 
-    mlp_sums = after(jnp.concatenate(sums, axis=1), dwq_rows).reshape(3, piece, n_rows, width)
-    mlp_grads = by_row(exchange_rows([pick(mlp_sums, r ^ k, 2) for k in range(n_rows)]), axis=1)
+    sums = [a.reshape(3, -1, dim) for a in after((early_sum, late_sum), dwq_turned)]
+    to_row = lambda k: jnp.concatenate(
+        [lax.dynamic_slice_in_dim(a, (r ^ k) * width, width, 2) for a in sums], axis=1
+    )
+    mlp_grads = by_row(exchange_rows([to_row(k) for k in range(n_rows)]), axis=1)
     mlp_grads = mlp_grads.astype(f32)
 
     gain_rows = jnp.stack(

time: 655 us -> 637 us (0.973)
  waiting for transfers between devices: 173 us -> 157 us
  local copies, waits for them, and re-layouts: 83.6 us -> 72.6 us
  blocking collectives: 16.2 us -> 23.3 us
    all_gather x1, waiting for transfers between devices: 10.6 us -> 0.01 us  [local(): wo_z = lax.all_gather(wo_low, 'z', axis=0)]
    all_gather x1, blocking collectives: 16.2 us -> 23.3 us  [local(): kv_mine = lax.all_gather(after(kv_own, wo_low), 'z', axis=0, tiled=True)]
    unnamed x76 -> x79, local copies, waits for them, and re-layouts: 23.2 us -> 20.4 us
  transfers between devices with their start and end apart: 68 -> 68, of which waited for: 28 -> 27; matrix products, arithmetic and copies ran while one was open for 21% -> 20% of each run, Pallas kernels for 35% -> 35%
where the time goes in v3:
time: 637 us; the launch traced here: 630 us
  Pallas kernels  239 us (38%)
  waiting for transfers between devices  157 us (25%)
  local copies, waits for them, and re-layouts  72.6 us (11%)
  other arithmetic  60.6 us (10%)
  starting transfers between devices  58.1 us (9%)
  blocking collectives  23.3 us (4%)
  between operations  15.5 us (2%)
    ppermute x48, waiting for transfers between devices, axis_swap(): lax.ppermute(a, axis, [(i, i ^ k) for i in range(lax.axis_size(axis))])  138 us
    pallas_call x4, Pallas kernels, mlp(): call(functools.partial(mlp_kernel, added), [jax.ShapeDtypeStruct((tokens,...  68.2 us
    ppermute x48, starting transfers between devices, axis_swap(): lax.ppermute(a, axis, [(i, i ^ k) for i in range(lax.axis_size(axis))])  55.8 us
    pallas_call x2, Pallas kernels, mlp_weights(): call(functools.partial(mlp_weights_kernel, added, tiles), [jax.ShapeDtype...  48.3 us
    pallas_call x1, Pallas kernels, attend_back(): call(functools.partial(attend_back_kernel, head ** (-0.5), tile, rows), [...  41.2 us
    pallas_call x1, Pallas kernels, attend(): call(functools.partial(attend_kernel, head ** (-0.5), tile, rows), [jax.S...  30.8 us
    all_gather x1, blocking collectives, local(): kv_mine = lax.all_gather(after(kv_own, wo_low), 'z', axis=0, tiled=True)  23.3 us
    unnamed x79, local copies, waits for them, and re-layouts  20.4 us
  transfers between devices with their start and end apart: 68, of which 27 were waited for; matrix products, arithmetic and copies ran while one was open for 20% of the time, Pallas kernels for 35%

profile of v3, /device:TPU:0, one launch (start us, length us, event | category | flops | bytes accessed | tf_op | source)
XLA Modules:
  0.0 629.6 jit_solution(13078444156397588050)
XLA Ops:
  30.2 3.7 norm_one.1.refs_0_.n_ref
  37.7 8.9 %collective-permute-done.1 = bf16[3,176,512]{2,1,0:T(8,128)(2,1)} collective-permute-done((bf16[3,176,512]{2,1,0:T(8,128)(2,1)}, bf16[3,176,512]{2,1,0:T(8,128)(2,1)}, u32[]{:S(2)}, u32[]{:S(2)}) %collective-permute-start.1) | collective-permute-done | bytes 540704 | tf_op jit(solution)/shard_map/ppermute | solution.py:30
  53.0 23.3 %all_gather.31 = bf16[2048,128]{1,0:T(8,128)(2,1)} all-gather(bf16[512,128]{1,0:T(8,128)(2,1)S(1)} %maximum_select_fusion.1), channel_id=1, replica_groups=mesh['row'=4,'z'=4,'core'=2] {'z'}, dimensions={0}, use_global_device_ids=true | all-gather | bytes 655360 | tf_op jit(solution)/shard_map/all_gather | solution.py:684
  100.5 30.8 %attend.1 = (bf16[512,1024]{1,0:T(8,128)(2,1)}, bf16[1024,512]{1,0:T(8,128)(2,1)}, bf16[512,1024]{1,0:T(8,128)(2,1)}, f32[4,2,512]{2,1,0:T(2,128)}) custom-call(bf16[512,2048]{1,0:T(8,128)(2,1)} %norm_one.1.refs_0_.n_ref, bf16[4,512,256]{2,1,0:T(8,128)(2,1)} %bitcast.185, bf16[4,512,256]{2,1,0:T(8,128)(2,1)} %collective-permute-done.7.refs_2_.refs_1_, ...), custom_call_target="tpu_custom_call" | custom-call | flops 6442450944 | bytes 16777216 | tf_op jit(solution)/shard_map/attend/pallas_call | solution.py:291
  131.3 8.9 %collective-permute-done.12.refs_2_.refs_3_ = bf16[4,512,256]{2,1,0:T(8,128)(2,1)} collective-permute-done((bf16[4,512,256]{2,1,0:T(8,128)(2,1)}, bf16[4,512,256]{2,1,0:T(8,128)(2,1)}, u32[]{:S(2)}, u32[]{:S(2)}) %collective-permute-start.12) | collective-permute-done | bytes 1048608 | tf_op jit(solution)/shard_map/ppermute | solution.py:30
  146.3 9.7 %collective-permute-done.16 = bf16[2,512,256]{2,1,0:T(8,128)(2,1)S(1)} collective-permute-done((bf16[2,512,256]{2,1,0:T(8,128)(2,1)S(1)}, bf16[2,512,256]{2,1,0:T(8,128)(2,1)S(1)}, u32[]{:S(2)}, u32[]{:S(2)}) %collective-permute-start.16) | collective-permute-done | bytes 524320 | tf_op jit(solution)/shard_map/ppermute | solution.py:30
  158.5 10.1 %out_project.1 = (f32[256,2048]{1,0:T(8,128)}, f32[256,2048]{1,0:T(8,128)}) custom-call(bf16[512,1024]{1,0:T(8,128)(2,1)} %get-tuple-element.136.m_ref.b_ref, bf16[4,512,256]{2,1,0:T(8,128)(2,1)} %bitcast.160, bf16[4,512,256]{2,1,0:T(8,128)(2,1)} %collective-permute-done.11.refs_1_.refs_2_, bf16[4,512,256]{2,1,0:T(8,128)(2,1)} %collective-permute-done.12.refs_2_.refs_3_, ...), custom_call_target="tpu_custom_call" | custom-call | flops 2147483648 | bytes 10485760 | tf_op jit(solution)/shard_map/out_project/pallas_call | solution.py:340
  173.1 4.6 norm_two.1
  190.4 24.1 %collective-permute-done.25 = bf16[128,2048]{1,0:T(8,128)(2,1)S(1)} collective-permute-done((bf16[128,2048]{1,0:T(8,128)(2,1)S(1)}, bf16[128,2048]{1,0:T(8,128)(2,1)S(1)}, u32[]{:S(2)}, u32[]{:S(2)}) %collective-permute-start.25) | collective-permute-done | bytes 524320 | tf_op jit(solution)/shard_map/ppermute | solution.py:30
  221.9 7.9 %collective-permute-done.21 = bf16[128,2048]{1,0:T(8,128)(2,1)S(1)} collective-permute-done((bf16[128,2048]{1,0:T(8,128)(2,1)S(1)}, bf16[128,2048]{1,0:T(8,128)(2,1)S(1)}, u32[]{:S(2)}, u32[]{:S(2)}) %collective-permute-start.21) | collective-permute-done | bytes 524320 | tf_op jit(solution)/shard_map/ppermute | solution.py:30
  234.4 17.8 %mlp.5 = (bf16[1024,448]{1,0:T(8,128)(2,1)}, bf16[1024,448]{1,0:T(8,128)(2,1)}, bf16[1024,448]{1,0:T(8,128)(2,1)}, bf16[1024,2048]{1,0:T(8,128)(2,1)}) custom-call(bf16[1024,2048]{1,0:T(8,128)(2,1)} %constant_dynamic-update-slice_fusion.4.x_ref.refs_5_, bf16[1024,2048]{1,0:T(8,128)(2,1)} %constant_dynamic-update-slice_fusion.9.g_ref.refs_6_, ...), custom_call_target="tpu_custom_call" | custom-call | flops 9395240960 | bytes 25165824 | tf_op jit(solution)/shard_map/mlp/pallas_call | solution.py:540
  252.3 17.8 %mlp.4 = (bf16[1024,448]{1,0:T(8,128)(2,1)}, bf16[1024,448]{1,0:T(8,128)(2,1)}, bf16[1024,448]{1,0:T(8,128)(2,1)}, bf16[1024,2048]{1,0:T(8,128)(2,1)}) custom-call(bf16[1024,2048]{1,0:T(8,128)(2,1)} %collective-permute-done.23.x_ref.refs_0_, bf16[1024,2048]{1,0:T(8,128)(2,1)} %collective-permute-done.26.g_ref.refs_1_, bf16[4,3,112,2048]{3,2,1,0:T(8,128)(2,1)} %bitcast.178), custom_call_target="tpu_custom_call" | custom-call | flops 9395240960 | bytes 25165824 | tf_op jit(solution)/shard_map/mlp/pallas_call | solution.py:540
  270.0 26.7 %mlp_weights.2 = (bf16[4,3,112,2048]{3,2,1,0:T(8,128)(2,1)}, bf16[1024,2048]{1,0:T(8,128)(2,1)}, bf16[1024,2048]{1,0:T(8,128)(2,1)}) custom-call(bf16[1024,2048]{1,0:T(8,128)(2,1)} %collective-permute-done.23.x_ref.refs_0_, bf16[1024,2048]{1,0:T(8,128)(2,1)} %collective-permute-done.26.g_ref.refs_1_, bf16[1024,448]{1,0:T(8,128)(2,1)} %get-tuple-element.148.refs_2_, ...), custom_call_target="tpu_custom_call" | custom-call | flops 15032385536 | bytes 33554432 | tf_op jit(solution)/shard_map/mlp_weights/pallas_call | solution.py:604
  296.8 16.0 %mlp.6 = (bf16[1024,256]{1,0:T(8,128)(2,1)}, bf16[1024,256]{1,0:T(8,128)(2,1)}, bf16[1024,256]{1,0:T(8,128)(2,1)}, bf16[1024,2048]{1,0:T(8,128)(2,1)}) custom-call(bf16[1024,2048]{1,0:T(8,128)(2,1)} %collective-permute-done.23.x_ref.refs_0_, bf16[1024,2048]{1,0:T(8,128)(2,1)} %collective-permute-done.26.g_ref.refs_1_, bf16[4,3,64,2048]{3,2,1,0:T(8,128)(2,1)} %bitcast.180, ...), custom_call_target="tpu_custom_call" | custom-call | flops 5368709120 | bytes 25165824 | tf_op jit(solution)/shard_map/mlp/pallas_call | solution.py:540
  313.4 16.6 %mlp.7 = (bf16[1024,256]{1,0:T(8,128)(2,1)}, bf16[1024,256]{1,0:T(8,128)(2,1)}, bf16[1024,256]{1,0:T(8,128)(2,1)}, bf16[1024,2048]{1,0:T(8,128)(2,1)}) custom-call(bf16[1024,2048]{1,0:T(8,128)(2,1)} %constant_dynamic-update-slice_fusion.4.x_ref.refs_5_, bf16[1024,2048]{1,0:T(8,128)(2,1)} %constant_dynamic-update-slice_fusion.9.g_ref.refs_6_, ...), custom_call_target="tpu_custom_call" | custom-call | flops 5368709120 | bytes 25165824 | tf_op jit(solution)/shard_map/mlp/pallas_call | solution.py:540
  334.9 21.6 %mlp_weights.3 = (bf16[4,3,64,2048]{3,2,1,0:T(8,128)(2,1)}, bf16[1024,2048]{1,0:T(8,128)(2,1)}, bf16[1024,2048]{1,0:T(8,128)(2,1)}) custom-call(bf16[1024,2048]{1,0:T(8,128)(2,1)} %collective-permute-done.23.x_ref.refs_0_, bf16[1024,2048]{1,0:T(8,128)(2,1)} %collective-permute-done.26.g_ref.refs_1_, bf16[1024,256]{1,0:T(8,128)(2,1)} %get-tuple-element.169.refs_2_, ...), custom_call_target="tpu_custom_call" | custom-call | flops 8589934592 | bytes 33554432 | tf_op jit(solution)/shard_map/mlp_weights/pallas_call | solution.py:604
  364.8 11.5 %collective-permute-done.31 = bf16[128,2048]{1,0:T(8,128)(2,1)S(1)} collective-permute-done((bf16[128,2048]{1,0:T(8,128)(2,1)S(1)}, bf16[128,2048]{1,0:T(8,128)(2,1)S(1)}, u32[]{:S(2)}, u32[]{:S(2)}) %collective-permute-start.31) | collective-permute-done | bytes 524320 | tf_op jit(solution)/shard_map/ppermute | solution.py:30
  376.4 3.7 convert_add_fusion.2.grad_ref
  384.2 5.3 norm_two_back.1
  391.8 17.2 %reduce-scatter.5.cloned.1.call-done = bf16[1,3,112,2048]{3,2,1,0:T(8,128)(2,1)} async-done(((bf16[4,3,112,2048]{3,2,1,0:T(8,128)(2,1)}), bf16[1,3,112,2048]{3,2,1,0:T(8,128)(2,1)}) %reduce-scatter.5.cloned.1.call-update) | async-done | bytes 1376272 | tf_op jit(solution)/shard_map/reduce_scatter | solution.py:752
  415.4 6.6 %outer.1 = bf16[4,4,512,256]{3,2,1,0:T(8,128)(2,1)} custom-call(bf16[512,2048]{1,0:T(8,128)(2,1)} %constant_dynamic-update-slice_fusion.14.a_ref.refs_0_, bf16[512,1024]{1,0:T(8,128)(2,1)} %get-tuple-element.136.m_ref.b_ref), custom_call_target="tpu_custom_call" | custom-call | flops 2147483648 | bytes 8388608 | tf_op jit(solution)/shard_map/outer/pallas_call | solution.py:444
  427.8 41.2 %attend_back.1 = (bf16[512,1024]{1,0:T(8,128)(2,1)}, f32[2048,128]{1,0:T(8,128)}, f32[2048,128]{1,0:T(8,128)}) custom-call(bf16[512,2048]{1,0:T(8,128)(2,1)} %constant_dynamic-update-slice_fusion.14.a_ref.refs_0_, bf16[4,512,256]{2,1,0:T(8,128)(2,1)} %bitcast.161, bf16[4,512,256]{2,1,0:T(8,128)(2,1)} %collective-permute-done.11.refs_1_.refs_2_, ...), custom_call_target="tpu_custom_call" | custom-call | flops 12884901888 | bytes 33554432 | tf_op jit(solution)/shard_map/attend_back/pallas_call | solution.py:407
  476.8 13.9 %query_back.1 = (bf16[4,4,512,256]{3,2,1,0:T(8,128)(2,1)}, f32[256,2048]{1,0:T(8,128)}, f32[256,2048]{1,0:T(8,128)}) custom-call(bf16[512,2048]{1,0:T(8,128)(2,1)} %norm_one.1.refs_0_.n_ref, bf16[512,1024]{1,0:T(8,128)(2,1)} %get-tuple-element.204.dq_ref, bf16[4,512,256]{2,1,0:T(8,128)(2,1)} %bitcast.186, ...), custom_call_target="tpu_custom_call" | custom-call | flops 4294967296 | bytes 16777216 | tf_op jit(solution)/shard_map/query_back/pallas_call | solution.py:480
  502.6 11.7 %collective-permute-done.45 = bf16[1024,128]{1,0:T(8,128)(2,1)S(1)} collective-permute-done((bf16[1024,128]{1,0:T(8,128)(2,1)S(1)}, bf16[1024,128]{1,0:T(8,128)(2,1)S(1)}, u32[]{:S(2)}, u32[]{:S(2)}) %collective-permute-start.45) | collective-permute-done | bytes 262176 | tf_op jit(solution)/shard_map/ppermute | solution.py:30
  515.8 3.7 collective-permute-done.46
  528.8 10.3 %collective-permute-done.41 = bf16[2,2,512,256]{3,2,1,0:T(8,128)(2,1)S(1)} collective-permute-done((bf16[2,2,512,256]{3,2,1,0:T(8,128)(2,1)S(1)}, bf16[2,2,512,256]{3,2,1,0:T(8,128)(2,1)S(1)}, u32[]{:S(2)}, u32[]{:S(2)}) %collective-permute-start.41) | collective-permute-done | bytes 1048608 | tf_op jit(solution)/shard_map/ppermute | solution.py:30
  547.4 8.6 %collective-permute-done.55 = bf16[2,512,256]{2,1,0:T(8,128)(2,1)} collective-permute-done((bf16[2,512,256]{2,1,0:T(8,128)(2,1)}, bf16[2,512,256]{2,1,0:T(8,128)(2,1)}, u32[]{:S(2)}, u32[]{:S(2)}) %collective-permute-start.55) | collective-permute-done | bytes 524320 | tf_op jit(solution)/shard_map/ppermute | solution.py:30
  561.3 6.2 norm_one_back.1
  580.6 3.7 collective-permute-done.51
  587.7 4.1 add_convert_fusion
  596.1 6.3 collective-permute-done.58
  605.2 10.9 %collective-permute-done.53 = f32[520,128]{1,0:T(8,128)S(1)} collective-permute-done((f32[520,128]{1,0:T(8,128)S(1)}, f32[520,128]{1,0:T(8,128)S(1)}, u32[]{:S(2)}, u32[]{:S(2)}) %collective-permute-start.53) | collective-permute-done | bytes 266272 | tf_op jit(solution)/shard_map/ppermute | solution.py:30
  (332 shorter events, 200.8 us)
Async XLA Ops:
  7.2 39.7 %all-gather.9.cloned.1.call-start = ((), (), s32[]{:S(2)}) async-start(), calls=%async_computation.8 | async-start | bytes 1310720 | tf_op jit(solution)/shard_map/all_gather | solution.py:646
  16.9 68.7 %all-gather.11.cloned.1.call-start = ((), (), s32[]{:S(2)}) async-start(), calls=%async_computation.9 | async-start | bytes 1310720 | tf_op jit(solution)/shard_map/all_gather | solution.py:683
  46.9 29.4 %collective-permute-start.8 = (bf16[4,512,256]{2,1,0:T(8,128)(2,1)}, bf16[4,512,256]{2,1,0:T(8,128)(2,1)S(1)}, u32[]{:S(2)}, u32[]{:S(2)}) collective-permute-start(bf16[4,512,256]{2,1,0:T(8,128)(2,1)} %bitcast.183), channel_id=1, source_target_pairs={{0,16},{8,24},{16,0},{24,8},{1,17},{9,25},{17,1},{25,9},{2,18},{10... | collective-permute-start | bytes 3145736 | tf_op jit(solution)/shard_map/ppermute | solution.py:30
  48.3 28.0 %collective-permute-start.7 = (bf16[4,512,256]{2,1,0:T(8,128)(2,1)}, bf16[4,512,256]{2,1,0:T(8,128)(2,1)}, u32[]{:S(2)}, u32[]{:S(2)}) collective-permute-start(bf16[4,512,256]{2,1,0:T(8,128)(2,1)} %bitcast.184), channel_id=1, source_target_pairs={{0,8},{8,0},{16,24},{24,16},{1,9},{9,1},{17,25},{25,17},{2,10},{10... | collective-permute-start | bytes 3145736 | tf_op jit(solution)/shard_map/ppermute | solution.py:30
  50.6 183.4 %all-gather.13.cloned.1.call-start = ((), (), s32[]{:S(2)}) async-start(), calls=%async_computation.10 | async-start | bytes 6881280 | tf_op jit(solution)/shard_map/all_gather | solution.py:700
  93.0 38.3 %collective-permute-start.14 = (bf16[256,2048]{1,0:T(8,128)(2,1)}, bf16[256,2048]{1,0:T(8,128)(2,1)}, u32[]{:S(2)}, u32[]{:S(2)}) collective-permute-start(bf16[256,2048]{1,0:T(8,128)(2,1)} %out_grad_ref.1), channel_id=1, source_target_pairs={{0,16},{8,24},{16,0},{24,8},{1,17},{9,25},{17,1},{25,9},{2,18},{10... | collective-permute-start | bytes 3145736 | tf_op jit(solution)/shard_map/ppermute | solution.py:30
  94.2 37.1 %collective-permute-start.13 = (bf16[256,2048]{1,0:T(8,128)(2,1)}, bf16[256,2048]{1,0:T(8,128)(2,1)}, u32[]{:S(2)}, u32[]{:S(2)}) collective-permute-start(bf16[256,2048]{1,0:T(8,128)(2,1)} %out_grad_ref.1), channel_id=1, source_target_pairs={{0,8},{8,0},{16,24},{24,16},{1,9},{9,1},{17,25},{25,17},{2,10},{10... | collective-permute-start | bytes 3145736 | tf_op jit(solution)/shard_map/ppermute | solution.py:30
  95.6 44.6 %collective-permute-start.12 = (bf16[4,512,256]{2,1,0:T(8,128)(2,1)}, bf16[4,512,256]{2,1,0:T(8,128)(2,1)}, u32[]{:S(2)}, u32[]{:S(2)}) collective-permute-start(bf16[4,512,256]{2,1,0:T(8,128)(2,1)} %bitcast.158), channel_id=1, source_target_pairs={{0,16},{8,24},{16,0},{24,8},{1,17},{9,25},{17,1},{25,9},{2,18},{10... | collective-permute-start | bytes 3145736 | tf_op jit(solution)/shard_map/ppermute | solution.py:30
  96.5 45.4 %collective-permute-start.11 = (bf16[4,512,256]{2,1,0:T(8,128)(2,1)}, bf16[4,512,256]{2,1,0:T(8,128)(2,1)}, u32[]{:S(2)}, u32[]{:S(2)}) collective-permute-start(bf16[4,512,256]{2,1,0:T(8,128)(2,1)} %bitcast.159), channel_id=1, source_target_pairs={{0,8},{8,0},{16,24},{24,16},{1,9},{9,1},{17,25},{25,17},{2,10},{10... | collective-permute-start | bytes 3145736 | tf_op jit(solution)/shard_map/ppermute | solution.py:30
  97.1 199.7 %all-gather.15.cloned.1.call-start = ((), (), s32[]{:S(2)}) async-start(), calls=%async_computation.11 | async-start | bytes 3932160 | tf_op jit(solution)/shard_map/all_gather | solution.py:700
  177.8 37.6 %collective-permute-start.19 = (bf16[256,2048]{1,0:T(8,128)(2,1)}, bf16[256,2048]{1,0:T(8,128)(2,1)S(1)}, u32[]{:S(2)}, u32[]{:S(2)}) collective-permute-start(bf16[256,2048]{1,0:T(8,128)(2,1)} %get-tuple-element.142), channel_id=1, source_target_pairs={{0,8},{8,0},{16,24},{24,16},{1,9},{9,1},{17,25},{25,17},{2,10},{10... | collective-permute-start | bytes 3145736 | tf_op jit(solution)/shard_map/ppermute | solution.py:30
  182.9 31.6 %collective-permute-start.25 = (bf16[128,2048]{1,0:T(8,128)(2,1)S(1)}, bf16[128,2048]{1,0:T(8,128)(2,1)S(1)}, u32[]{:S(2)}, u32[]{:S(2)}) collective-permute-start(bf16[128,2048]{1,0:T(8,128)(2,1)S(1)} %slice.385), channel_id=1, source_target_pairs={{0,8},{8,0},{16,24},{24,16},{1,9},{9,1},{17,25},{25,17},{2,10},{10... | collective-permute-start | bytes 1572872 | tf_op jit(solution)/shard_map/ppermute | solution.py:30
  183.3 34.7 %collective-permute-start.20 = (bf16[256,2048]{1,0:T(8,128)(2,1)S(1)}, bf16[256,2048]{1,0:T(8,128)(2,1)S(1)}, u32[]{:S(2)}, u32[]{:S(2)}) collective-permute-start(bf16[256,2048]{1,0:T(8,128)(2,1)S(1)} %copy-done.17), channel_id=1, source_target_pairs={{0,16},{8,24},{16,0},{24,8},{1,17},{9,25},{17,1},{25,9},{2,18},{10... | collective-permute-start | bytes 3145736 | tf_op jit(solution)/shard_map/ppermute | solution.py:30
  215.3 36.9 %collective-permute-start.26 = (bf16[1024,2048]{1,0:T(8,128)(2,1)}, bf16[1024,2048]{1,0:T(8,128)(2,1)}, u32[]{:S(2)}, u32[]{:S(2)}) collective-permute-start(bf16[1024,2048]{1,0:T(8,128)(2,1)} %constant_dynamic-update-slice_fusion.9.g_ref.refs_6_), channel_id=1, source_target_pairs={{0,1},{1,0},{2,3},{3,2},{4,5},{5,4},{6,7},{7,6},{8,9},{9,8},{10,11... | collective-permute-start | bytes 12582920 | tf_op jit(solution)/shard_map/ppermute | solution.py:26
  234.0 175.0 %reduce-scatter.5.cloned.1.call-start = ((), (), s32[]{:S(2)}) async-start(), calls=%async_computation.4 | async-start | bytes 6881280 | tf_op jit(solution)/shard_map/reduce_scatter | solution.py:752
  313.3 229.4 %reduce-scatter.7.cloned.1.call-start = ((), (), s32[]{:S(2)}) async-start(), calls=%async_computation.5 | async-start | bytes 3932160 | tf_op jit(solution)/shard_map/reduce_scatter | solution.py:752
  333.2 25.0 %collective-permute-start.28 = (bf16[2,128,2048]{2,1,0:T(8,128)(2,1)S(1)}, bf16[2,128,2048]{2,1,0:T(8,128)(2,1)}, u32[]{:S(2)}, u32[]{:S(2)}) collective-permute-start(bf16[2,128,2048]{2,1,0:T(8,128)(2,1)S(1)} %pad_maximum_fusion.1), channel_id=1, source_target_pairs={{0,8},{8,0},{16,24},{24,16},{1,9},{9,1},{17,25},{25,17},{2,10},{10... | collective-permute-start | bytes 3145736 | tf_op jit(solution)/shard_map/ppermute | solution.py:30
  334.8 24.8 %collective-permute-start.29 = (bf16[2,128,2048]{2,1,0:T(8,128)(2,1)S(1)}, bf16[2,128,2048]{2,1,0:T(8,128)(2,1)}, u32[]{:S(2)}, u32[]{:S(2)}) collective-permute-start(bf16[2,128,2048]{2,1,0:T(8,128)(2,1)S(1)} %pad_maximum_fusion.2), channel_id=1, source_target_pairs={{0,16},{8,24},{16,0},{24,8},{1,17},{9,25},{17,1},{25,9},{2,18},{10... | collective-permute-start | bytes 3145736 | tf_op jit(solution)/shard_map/ppermute | solution.py:30
  389.5 130.0 %collective-permute-start.47 = (bf16[256,128]{1,0:T(8,128)(2,1)S(1)}, bf16[256,128]{1,0:T(8,128)(2,1)S(1)}, u32[]{:S(2)}, u32[]{:S(2)}) collective-permute-start(bf16[256,128]{1,0:T(8,128)(2,1)S(1)} %get-tuple-element.289), channel_id=1, source_target_pairs={{0,1},{1,0},{2,3},{3,2},{4,5},{5,4},{6,7},{7,6},{8,9},{9,8},{10,11... | collective-permute-start | bytes 196616 | tf_op jit(solution)/shard_map/ppermute | solution.py:26
  409.0 176.9 %reduce-scatter.9.cloned.1.call-start = ((), (), s32[]{:S(2)}) async-start(), calls=%async_computation.6 | async-start | bytes 1310720 | tf_op jit(solution)/shard_map/reduce_scatter | solution.py:784
  409.0 60.0 %collective-permute-start.33 = (bf16[2,128,2048]{2,1,0:T(8,128)(2,1)}, bf16[2,128,2048]{2,1,0:T(8,128)(2,1)}, u32[]{:S(2)}, u32[]{:S(2)}) collective-permute-start(bf16[2,128,2048]{2,1,0:T(8,128)(2,1)} %pad_maximum_fusion.3), channel_id=1, source_target_pairs={{0,8},{8,0},{16,24},{24,16},{1,9},{9,1},{17,25},{25,17},{2,10},{10... | collective-permute-start | bytes 3145736 | tf_op jit(solution)/shard_map/ppermute | solution.py:30
  410.6 58.5 %collective-permute-start.34 = (bf16[2,128,2048]{2,1,0:T(8,128)(2,1)}, bf16[2,128,2048]{2,1,0:T(8,128)(2,1)}, u32[]{:S(2)}, u32[]{:S(2)}) collective-permute-start(bf16[2,128,2048]{2,1,0:T(8,128)(2,1)} %pad_maximum_fusion.4), channel_id=1, source_target_pairs={{0,16},{8,24},{16,0},{24,8},{1,17},{9,25},{17,1},{25,9},{2,18},{10... | collective-permute-start | bytes 3145736 | tf_op jit(solution)/shard_map/ppermute | solution.py:30
  426.7 42.4 %collective-permute-start.36 = (bf16[2,2,512,256]{3,2,1,0:T(8,128)(2,1)}, bf16[2,2,512,256]{3,2,1,0:T(8,128)(2,1)}, u32[]{:S(2)}, u32[]{:S(2)}) collective-permute-start(bf16[2,2,512,256]{3,2,1,0:T(8,128)(2,1)} %pad_maximum_fusion.5), channel_id=1, source_target_pairs={{0,8},{8,0},{16,24},{24,16},{1,9},{9,1},{17,25},{25,17},{2,10},{10... | collective-permute-start | bytes 3145736 | tf_op jit(solution)/shard_map/ppermute | solution.py:30
  427.3 41.8 %collective-permute-start.37 = (bf16[2,2,512,256]{3,2,1,0:T(8,128)(2,1)}, bf16[2,2,512,256]{3,2,1,0:T(8,128)(2,1)}, u32[]{:S(2)}, u32[]{:S(2)}) collective-permute-start(bf16[2,2,512,256]{3,2,1,0:T(8,128)(2,1)} %stack.108), channel_id=1, source_target_pairs={{0,16},{8,24},{16,0},{24,8},{1,17},{9,25},{17,1},{25,9},{2,18},{10... | collective-permute-start | bytes 3145736 | tf_op jit(solution)/shard_map/ppermute | solution.py:30
  473.8 24.2 %collective-permute-start.44 = (bf16[2048,128]{1,0:T(8,128)(2,1)}, bf16[2048,128]{1,0:T(8,128)(2,1)}, u32[]{:S(2)}, u32[]{:S(2)}) collective-permute-start(bf16[2048,128]{1,0:T(8,128)(2,1)} %select_convert_fusion), channel_id=1, source_target_pairs={{0,1},{1,0},{2,3},{3,2},{4,5},{5,4},{6,7},{7,6},{8,9},{9,8},{10,11... | collective-permute-start | bytes 1572872 | tf_op jit(solution)/shard_map/ppermute | solution.py:26
  473.9 28.6 %collective-permute-start.39 = (bf16[2,512,256]{2,1,0:T(8,128)(2,1)}, bf16[2,512,256]{2,1,0:T(8,128)(2,1)}, u32[]{:S(2)}, u32[]{:S(2)}) collective-permute-start(bf16[2,512,256]{2,1,0:T(8,128)(2,1)} %get-tuple-element.251), channel_id=1, source_target_pairs={{0,16},{8,24},{16,0},{24,8},{1,17},{9,25},{17,1},{25,9},{2,18},{10... | collective-permute-start | bytes 1572872 | tf_op jit(solution)/shard_map/ppermute | solution.py:30
  475.4 27.0 %collective-permute-start.38 = (bf16[2,512,256]{2,1,0:T(8,128)(2,1)S(1)}, bf16[2,512,256]{2,1,0:T(8,128)(2,1)}, u32[]{:S(2)}, u32[]{:S(2)}) collective-permute-start(bf16[2,512,256]{2,1,0:T(8,128)(2,1)S(1)} %get-tuple-element.252), channel_id=1, source_target_pairs={{0,8},{8,0},{16,24},{24,16},{1,9},{9,1},{17,25},{25,17},{2,10},{10... | collective-permute-start | bytes 1572872 | tf_op jit(solution)/shard_map/ppermute | solution.py:30
  514.6 24.5 %collective-permute-start.41 = (bf16[2,2,512,256]{3,2,1,0:T(8,128)(2,1)S(1)}, bf16[2,2,512,256]{3,2,1,0:T(8,128)(2,1)S(1)}, u32[]{:S(2)}, u32[]{:S(2)}) collective-permute-start(bf16[2,2,512,256]{3,2,1,0:T(8,128)(2,1)S(1)} %pad_maximum_fusion.6), channel_id=1, source_target_pairs={{0,8},{8,0},{16,24},{24,16},{1,9},{9,1},{17,25},{25,17},{2,10},{10... | collective-permute-start | bytes 3145736 | tf_op jit(solution)/shard_map/ppermute | solution.py:30
  525.8 35.4 %collective-permute-start.48 = (f32[256,2048]{1,0:T(8,128)}, f32[256,2048]{1,0:T(8,128)}, u32[]{:S(2)}, u32[]{:S(2)}) collective-permute-start(f32[256,2048]{1,0:T(8,128)} %get-tuple-element.245), channel_id=1, source_target_pairs={{0,1},{1,0},{2,3},{3,2},{4,5},{5,4},{6,7},{7,6},{8,9},{9,8},{10,11... | collective-permute-start | bytes 6291464 | tf_op jit(solution)/shard_map/ppermute | solution.py:26
  544.2 76.4 %reduce-scatter.11.cloned.1.call-start = ((), (), s32[]{:S(2)}) async-start(), calls=%async_computation.7 | async-start | bytes 1310720 | tf_op jit(solution)/shard_map/reduce_scatter | solution.py:784
  545.1 40.9 %collective-permute-start.42 = (bf16[128,2048]{1,0:T(8,128)(2,1)}, bf16[128,2048]{1,0:T(8,128)(2,1)}, u32[]{:S(2)}, u32[]{:S(2)}) collective-permute-start(bf16[128,2048]{1,0:T(8,128)(2,1)} %get-tuple-element.207), channel_id=1, source_target_pairs={{0,16},{8,24},{16,0},{24,8},{1,17},{9,25},{17,1},{25,9},{2,18},{10... | collective-permute-start | bytes 1572872 | tf_op jit(solution)/shard_map/ppermute | solution.py:30
  546.7 41.0 %collective-permute-start.43 = (bf16[128,2048]{1,0:T(8,128)(2,1)}, bf16[128,2048]{1,0:T(8,128)(2,1)}, u32[]{:S(2)}, u32[]{:S(2)}) collective-permute-start(bf16[128,2048]{1,0:T(8,128)(2,1)} %get-tuple-element.208), channel_id=1, source_target_pairs={{0,8},{8,0},{16,24},{24,16},{1,9},{9,1},{17,25},{25,17},{2,10},{10... | collective-permute-start | bytes 1572872 | tf_op jit(solution)/shard_map/ppermute | solution.py:30
  (70 other events, 1012.4 us)
Sparse Core Ops, SparseCore 0:
  17.0 29.6 all-gather.8
  50.7 32.5 all-gather.10
  97.2 103.1 all-gather.12
  234.1 61.0 all-gather.14
  313.5 95.4 reduce-scatter.4
  411.1 60.9 reduce-scatter.6
  544.3 26.4 reduce-scatter.8
  586.1 29.8 reduce-scatter.10
